TPU v7x, 256 devices: a whole 4x4x8 slice. The times are simulated.
256 devices in a mesh: seq: 64 (over x, z, core), head: 4 (over y).
Axes of the slice: x: 4, y: 4, z: 8, core: 2. Of those that a mesh axis runs over, the one named last changes fastest.
Arguments:
- queries: bfloat16 [8192, 128], P('seq'), may hold values from -6 to 6
- key_rows: bfloat16 [8192, 128], P('seq'), may hold values from -0.0078125 to 0.0078125
- values: bfloat16 [8192, 5120], P('seq', 'head'), may hold values from -6 to 6
- gate_rows: bfloat16 [8192, 5120], P('seq', 'head'), may hold values from -6 to 6
- log_decay: float32 [8192, 80], P('seq', 'head'), may hold values from -0.69 to 0
- skip_gain: float32 [80], P('head'), may hold values from 0.3 to 4.2
- lam_index: int32 [8192], P('seq'), may hold values from 0 to 63
- segments: int32 [8192], P('seq'), may hold values from 0 to 255, never falling along the last dimension, each value on 1 to 64 neighbouring positions
- lam_table: float32 [64, 8, 80], P(None, None, 'head'), may hold values from 0.2 to 2
- norm_gain: float32 [5120], P('head'), may hold values from 0.25 to 1.75
- out_proj: bfloat16 [5120, 2560], P('head', 'seq'), may hold values from -0.078125 to 0.078125
Outputs:
- mixer_out: bfloat16 [8192, 2560], P(('seq', 'head'))
Inputs may be any that keep to these rules, and one draw needn't show every extreme that they name: `segments`: stretch numbers never fall along the sequence; each stretch has 1 to 64 tokens.
All inputs are finite; a program needn't handle non-finite values.
Results may differ from a plain program's by a relative error of at most 0.012.
Values may be sent and summed in bfloat16 or wider, within the bound.
No kernel may reach another device: no remote copies, remote signals or barrier semaphores. Data moves between devices by JAX's collectives and lax.ppermute only.
A program may use at most 128 MiB of HBM per device.

v0:
```python
import jax
import jax.numpy as jnp
from jax import lax
from jax.sharding import PartitionSpec as P

DI = 5120


epsilon = 1e-05
highest = lax.Precision.HIGHEST


def from_everyone(array, axis):
    copies = jnp.broadcast_to(array, (lax.axis_size(axis), *array.shape))
    return lax.all_to_all(copies, axis, split_axis=0, concat_axis=0, tiled=True)


def laid_out(parts, dim):
    parts = jnp.moveaxis(parts, 0, dim)
    shape = parts.shape
    return parts.reshape(*shape[:dim], shape[dim] * shape[dim + 1], *shape[dim + 2 :])


def gather_directly(array, axis, dim):
    parts = from_everyone(array, axis)
    return laid_out(parts, dim)


def swapped(value, axis, distance):
    mask = 2**distance
    pairs = [(source, source ^ mask) for source in range(lax.axis_size(axis))]
    return lax.ppermute(value, axis, pairs)


def of_everyone(array, axis):
    everything = from_everyone(array, axis)
    return jnp.sum(everything, axis=0)


def split_up(array, dim, peers):
    shape = array.shape
    parts = array.reshape(*shape[:dim], peers, shape[dim] // peers, *shape[dim + 1 :])
    return jnp.moveaxis(parts, dim, 0)


def summed_on_arrival(array, axis, dim):
    peers = lax.axis_size(axis)
    parts = lax.all_to_all(split_up(array, dim, peers), axis, 0, 0, tiled=True)
    return jnp.sum(parts.astype(jnp.float32), axis=0)


def widen(matrix, head_dim):
    return jnp.repeat(matrix, head_dim, axis=-1)


def per_device(
    queries,
    key_rows,
    values,
    gate_rows,
    log_decay,
    skip_gain,
    lam_index,
    segments,
    lam_table,
    norm_gain,
    out_proj,
):
    tok_rows, state_dim = queries.shape
    head_count = log_decay.shape[1]
    col_count = values.shape[1]
    head_dim = col_count // head_count
    class_count = lam_table.shape[0]
    level_count = lam_table.shape[1]
    cross_levels = level_count - 2
    shard_pos = lax.axis_index("seq")
    cum_decay = jnp.cumsum(log_decay, axis=0)
    onehot = (lam_index[:, None] == jnp.arange(class_count, dtype=jnp.int32)[None, :]).astype(
        jnp.float32
    )
    level_wts = jnp.dot(
        onehot, lam_table.reshape(class_count, level_count * head_count), precision=highest
    )
    level_wts = level_wts.reshape(tok_rows, level_count, head_count)
    decay_end = widen(jnp.exp(cum_decay[-1][None, :] - cum_decay), head_dim)
    decayed = (values.astype(jnp.float32) * decay_end).astype(jnp.bfloat16)
    end_state = jnp.dot(key_rows.T, decayed, preferred_element_type=jnp.float32).astype(
        jnp.bfloat16
    )
    shard_span = cum_decay[-1]
    totals = gather_directly(shard_span[None, :], "seq", 0)
    bounds = jnp.concatenate(
        [jnp.zeros((1, head_count), jnp.float32), jnp.cumsum(totals, axis=0)], axis=0
    )
    here_bound = lax.dynamic_index_in_dim(bounds, shard_pos, 0, keepdims=False)
    bucket_list = []
    group_state = end_state
    for level_pos in range(cross_levels):
        partner_state = swapped(group_state, "seq", level_pos)
        is_upper = jnp.bitwise_and(jnp.right_shift(shard_pos, level_pos), 1) == 1
        group_idx = jnp.right_shift(shard_pos, level_pos)
        start_row = jnp.left_shift(group_idx, level_pos)
        start_bound = lax.dynamic_index_in_dim(bounds, start_row, 0, keepdims=False)
        factor = widen(jnp.exp(here_bound - start_bound), head_dim)[None, :]
        bucket_list.append(jnp.where(is_upper, factor * partner_state.astype(jnp.float32), 0.0))
        if level_pos + 1 < cross_levels:
            upper_start = jnp.bitwise_or(start_row, 2**level_pos)
            upper_begin = lax.dynamic_index_in_dim(bounds, upper_start, 0, keepdims=False)
            upper_end = lax.dynamic_index_in_dim(
                bounds, upper_start + 2**level_pos, 0, keepdims=False
            )
            span_factor = widen(jnp.exp(upper_end - upper_begin), head_dim)[None, :]
            upper_state = jnp.where(is_upper, group_state, partner_state).astype(jnp.float32)
            lower_state = jnp.where(is_upper, partner_state, group_state).astype(jnp.float32)
            group_state = (upper_state + span_factor * lower_state).astype(jnp.bfloat16)
    buckets = jnp.stack(bucket_list)
    block_rows = min(tok_rows, 512)
    block_count = tok_rows // block_rows
    value_heads = values.reshape(tok_rows, head_count, head_dim)
    key_cols = cum_decay.T
    key_pos = jnp.arange(tok_rows, dtype=jnp.int32)

    def local_block(block_pos):
        first_row = block_pos * block_rows
        scores = jnp.dot(queries, key_rows.T, preferred_element_type=jnp.float32)
        query_pos = first_row + jnp.arange(block_rows, dtype=jnp.int32)
        causal = query_pos[:, None] >= key_pos[None, :]
        log_gaps = jnp.where(causal[None], cum_decay.T[:, :, None] - key_cols[:, None, :], -jnp.inf)
        same_seg = segments[:, None] == segments[None, :]
        level_w = jnp.where(
            same_seg[None], level_wts[:, 0, :].T[:, :, None], level_wts[:, 1, :].T[:, :, None]
        )
        weights_bf = (scores[None] * jnp.exp(log_gaps) * level_w).astype(jnp.bfloat16)
        block_out = jnp.einsum(
            "htj,jhp->thp", weights_bf, value_heads, preferred_element_type=jnp.float32
        )
        return block_out.reshape(block_rows, col_count)

    local_out = lax.map(local_block, jnp.arange(block_count, dtype=jnp.int32)).reshape(
        tok_rows, col_count
    )
    query_f32 = queries.astype(jnp.float32)
    cross_out = jnp.zeros((tok_rows, col_count), jnp.float32)
    for level_pos in range(cross_levels):
        level_read = jnp.dot(query_f32, buckets[level_pos], precision=highest)
        cross_out = cross_out + level_read * widen(level_wts[:, 2 + level_pos, :], head_dim)
    cross_out = cross_out * widen(jnp.exp(cum_decay), head_dim)
    mixer_sum = (
        local_out + cross_out + widen(skip_gain, head_dim)[None, :] * values.astype(jnp.float32)
    )
    gated = mixer_sum * jax.nn.silu(gate_rows.astype(jnp.float32))
    square_sum = of_everyone(jnp.sum(gated * gated, axis=1), "head")
    inv_rms = lax.rsqrt(square_sum / DI + epsilon)
    normed = (gated * inv_rms[:, None] * norm_gain[None, :]).astype(jnp.bfloat16)
    partial_terms = jnp.dot(
        normed,
        lax.all_gather(out_proj, "seq", axis=1, tiled=True),
        preferred_element_type=jnp.float32,
    )
    return summed_on_arrival(partial_terms.astype(jnp.bfloat16), "head", 0).astype(jnp.bfloat16)


def solution(mesh):
    return jax.shard_map(
        per_device,
        mesh=mesh,
        in_specs=(
            P("seq", None),
            P("seq", None),
            P("seq", "head"),
            P("seq", "head"),
            P("seq", "head"),
            P("head"),
            P("seq"),
            P("seq"),
            P(None, None, "head"),
            P("head"),
            P("head", "seq"),
        ),
        out_specs=P(("seq", "head"), None),
        check_vma=False,
    )
```

profile of v0, /device:TPU:6, one launch (start us, length us, event | category | flops | bytes accessed | tf_op | source)
XLA Modules:
  0.0 143.5 jit_solution(3442905027183908740)
XLA Ops:
  6.5 0.7 all-gather.2.cloned.1.call-update
  7.3 0.8 copy.47
  8.3 0.6 broadcast_in_dim.159
  8.9 12.2 %all-to-all-start = ((f32[64,1,20]{2,1,0:T(1,128)}), f32[64,1,20]{2,1,0:T(1,128)S(1)}, u32[]{:S(2)}, u32[]{:S(2)}) async-start(f32[64,1,20]{2,1,0:T(1,128)} %broadcast_in_dim.159), calls=%async_computation | async-start | bytes 65536 | tf_op jit(solution)/shard_map/all_to_all | solution.py:15
  21.2 1.2 copy.51
  23.3 5.3 %all-to-all-done = f32[64,1,20]{2,1,0:T(1,128)S(1)} async-done(((f32[64,1,20]{2,1,0:T(1,128)}), f32[64,1,20]{2,1,0:T(1,128)S(1)}, u32[]{:S(2)}, u32[]{:S(2)}) %all-to-all-start) | async-done | bytes 5152 | tf_op jit(solution)/shard_map/all_to_all | solution.py:15
  29.0 0.3 add_convert_fusion.4
  29.3 0.7 collective-permute-start.1
  30.3 9.7 %collective-permute-done.1 = bf16[128,1280]{0,1:T(8,128)(2,1)S(1)} collective-permute-done((bf16[128,1280]{0,1:T(8,128)(2,1)S(1)}, bf16[128,1280]{0,1:T(8,128)(2,1)S(1)}, u32[]{:S(2)}, u32[]{:S(2)}) %collective-permute-start.1) | collective-permute-done | bytes 327712 | tf_op jit(solution)/shard_map/ppermute | solution.py:32
  40.0 0.3 add_convert_fusion.3
  40.3 1.0 collective-permute-start.2
  41.9 1.2 fusion.16
  43.2 15.2 %collective-permute-done.2 = bf16[128,1280]{0,1:T(8,128)(2,1)S(1)} collective-permute-done((bf16[128,1280]{0,1:T(8,128)(2,1)S(1)}, bf16[128,1280]{0,1:T(8,128)(2,1)S(1)}, u32[]{:S(2)}, u32[]{:S(2)}) %collective-permute-start.2) | collective-permute-done | bytes 327712 | tf_op jit(solution)/shard_map/ppermute | solution.py:32
  58.4 0.3 add_convert_fusion.2
  58.7 2.2 %collective-permute-start.3 = (bf16[128,1280]{0,1:T(8,128)(2,1)S(1)}, bf16[128,1280]{0,1:T(8,128)(2,1)S(1)}, u32[]{:S(2)}, u32[]{:S(2)}) collective-permute-start(bf16[128,1280]{0,1:T(8,128)(2,1)S(1)} %add_convert_fusion.2), channel_id=1, source_target_pairs={{0,32},{4,36},{8,40},{12,44},{16,48},{20,52},{24,56},{28,60},{32,0... | collective-permute-start | bytes 983048 | tf_op jit(solution)/shard_map/ppermute | solution.py:32
  62.2 0.6 fusion.14
  62.7 19.2 %collective-permute-done.3 = bf16[128,1280]{0,1:T(8,128)(2,1)S(1)} collective-permute-done((bf16[128,1280]{0,1:T(8,128)(2,1)S(1)}, bf16[128,1280]{0,1:T(8,128)(2,1)S(1)}, u32[]{:S(2)}, u32[]{:S(2)}) %collective-permute-start.3) | collective-permute-done | bytes 327712 | tf_op jit(solution)/shard_map/ppermute | solution.py:32
  81.9 0.3 add_convert_fusion.1
  82.2 1.2 collective-permute-start.4
  83.4 0.5 fusion.13
  84.0 0.5 fusion.11
  84.5 11.5 %collective-permute-done.4 = bf16[128,1280]{0,1:T(8,128)(2,1)S(1)} collective-permute-done((bf16[128,1280]{0,1:T(8,128)(2,1)S(1)}, bf16[128,1280]{0,1:T(8,128)(2,1)S(1)}, u32[]{:S(2)}, u32[]{:S(2)}) %collective-permute-start.4) | collective-permute-done | bytes 327712 | tf_op jit(solution)/shard_map/ppermute | solution.py:32
  96.1 0.3 add_convert_fusion
  96.3 0.3 collective-permute-start.5
  96.7 0.5 fusion.9
  97.3 0.5 fusion.7
  97.8 9.3 %collective-permute-done.5 = bf16[128,1280]{0,1:T(8,128)(2,1)S(1)} collective-permute-done((bf16[128,1280]{0,1:T(8,128)(2,1)S(1)}, bf16[128,1280]{0,1:T(8,128)(2,1)S(1)}, u32[]{:S(2)}, u32[]{:S(2)}) %collective-permute-start.5) | collective-permute-done | bytes 327712 | tf_op jit(solution)/shard_map/ppermute | solution.py:32
  107.2 1.6 %multiply_reduce_fusion = (f32[128]{0:T(128)S(1)}, f32[128,1280]{0,1:T(8,128)S(1)}) fusion(bf16[128,1280]{0,1:T(8,128)(2,1)S(1)} %copy.55, bf16[128,1280]{0,1:T(8,128)(2,1)S(1)} %copy.51, f32[1280]{0:T(1024)S(1)} %mul.232, f32[128,1280]{0,1:T(8,128)S(1)} %bitcast.137, f32[128,1280]{0,1:T(8,128)S(1)} %bitcast.132, f32[128,1280]{0,1:T(8,128)S(1)} %fusion.7, ...), kind=kOutput, calls=%fused_computation.35 | convolution fusion | flops 254607232 | bytes 4303361 | tf_op jit(solution)/shard_map/dot_general | solution.py:145
  108.8 10.3 %all_to_all.16 = f32[4,1,128]{2,1,0:T(1,128)S(1)} all-to-all(f32[4,1,128]{2,1,0:T(1,128)S(1)} %broadcast_in_dim.181), channel_id=1, replica_groups=mesh['seq'=64,'head'=4] {'head'}, dimensions={0} | all-to-all | bytes 4096 | tf_op jit(solution)/shard_map/all_to_all | solution.py:15
  119.2 5.4 %convolution_convert_fusion = bf16[128,2560]{1,0:T(8,128)(2,1)S(1)} fusion(bf16[1280,2560]{0,1:T(8,128)(2,1)} %all-gather.2.cloned.1.call-done, f32[128,1280]{0,1:T(8,128)S(1)} %get-tuple-element.60, f32[1280]{0:T(1024)S(1)} %copy-done.4, f32[128]{0:T(128)S(1)} %add_rsqrt_fusion), kind=kOutput, calls=%fused_computation | convolution fusion | flops 839680000 | bytes 7869952 | tf_op jit(solution)/shard_map/dot_general | solution.py:155
  124.6 11.2 %all_to_all.17 = bf16[4,32,2560]{2,1,0:T(8,128)(2,1)S(1)} all-to-all(bf16[4,32,2560]{2,1,0:T(8,128)(2,1)S(1)} %bitcast.124), channel_id=1, replica_groups=mesh['seq'=64,'head'=4] {'head'}, dimensions={0} | all-to-all | bytes 1310720 | tf_op jit(solution)/shard_map/all_to_all | solution.py:48
  135.8 0.8 reduce_sum.32
  (73 shorter events, 4.0 us)
Async XLA Ops:
  6.5 23.5 %copy-start = (bf16[128,128]{1,0:T(8,128)(2,1)S(1)}, bf16[128,128]{1,0:T(8,128)(2,1)}, u32[]{:S(2)}) copy-start(bf16[128,128]{1,0:T(8,128)(2,1)} %param.11) | copy-start | bytes 98308
  6.5 16.0 %copy-start.2 = (bf16[128,128]{1,0:T(8,128)(2,1)S(1)}, bf16[128,128]{1,0:T(8,128)(2,1)}, u32[]{:S(2)}) copy-start(bf16[128,128]{1,0:T(8,128)(2,1)} %param.12) | copy-start | bytes 98308
  6.5 112.6 %all-gather.2.cloned.1.call-start = ((), (), s32[]{:S(2)}) async-start(), calls=%async_computation.3 | async-start | bytes 6656000 | tf_op jit(solution)/shard_map/all_gather | solution.py:157
  7.3 15.7 %copy-start.3 = (f32[64,8,20]{0,1,2:T(8,128)S(1)}, f32[64,8,20]{0,1,2:T(8,128)}, u32[]{:S(2)}) copy-start(f32[64,8,20]{0,1,2:T(8,128)} %param.19) | copy-start | bytes 122884
  8.9 19.7 %all-to-all-start = ((f32[64,1,20]{2,1,0:T(1,128)}), f32[64,1,20]{2,1,0:T(1,128)S(1)}, u32[]{:S(2)}, u32[]{:S(2)}) async-start(f32[64,1,20]{2,1,0:T(1,128)} %broadcast_in_dim.159), calls=%async_computation | async-start | bytes 65536 | tf_op jit(solution)/shard_map/all_to_all | solution.py:15
  21.1 1.9 %copy-start.6 = (s32[128]{0:T(128)S(1)}, s32[128]{0:T(128)}, u32[]{:S(2)}) copy-start(s32[128]{0:T(128)} %param.17) | copy-start | bytes 1540
  22.7 6.3 %collective-permute-start = (bf16[128,1280]{0,1:T(8,128)(2,1)S(1)}, bf16[128,1280]{0,1:T(8,128)(2,1)S(1)}, u32[]{:S(2)}, u32[]{:S(2)}) collective-permute-start(bf16[128,1280]{0,1:T(8,128)(2,1)S(1)} %fusion.15), channel_id=1, source_target_pairs={{0,4},{4,0},{8,12},{12,8},{16,20},{20,16},{24,28},{28,24},{32,36},... | collective-permute-start | bytes 983048 | tf_op jit(solution)/shard_map/ppermute | solution.py:32
  23.2 18.0 %copy-start.5 = (s32[128]{0:T(128)S(1)}, s32[128]{0:T(128)}, u32[]{:S(2)}) copy-start(s32[128]{0:T(128)} %param.18) | copy-start | bytes 1540
  28.8 12.6 %copy-start.1 = (bf16[128,1280]{1,0:T(8,128)(2,1)S(1)}, bf16[128,1280]{1,0:T(8,128)(2,1)}, u32[]{:S(2)}) copy-start(bf16[128,1280]{1,0:T(8,128)(2,1)} %param.14) | copy-start | bytes 983044
  29.3 12.4 %copy-start.7 = (f32[20]{0:T(128)S(1)}, f32[20]{0:T(128)}, u32[]{:S(2)}) copy-start(f32[20]{0:T(128)} %param.16) | copy-start | bytes 244
  29.3 10.7 %collective-permute-start.1 = (bf16[128,1280]{0,1:T(8,128)(2,1)S(1)}, bf16[128,1280]{0,1:T(8,128)(2,1)S(1)}, u32[]{:S(2)}, u32[]{:S(2)}) collective-permute-start(bf16[128,1280]{0,1:T(8,128)(2,1)S(1)} %add_convert_fusion.4), channel_id=1, source_target_pairs={{0,8},{4,12},{8,0},{12,4},{16,24},{20,28},{24,16},{28,20},{32,40},... | collective-permute-start | bytes 983048 | tf_op jit(solution)/shard_map/ppermute | solution.py:32
  40.3 18.1 %collective-permute-start.2 = (bf16[128,1280]{0,1:T(8,128)(2,1)S(1)}, bf16[128,1280]{0,1:T(8,128)(2,1)S(1)}, u32[]{:S(2)}, u32[]{:S(2)}) collective-permute-start(bf16[128,1280]{0,1:T(8,128)(2,1)S(1)} %add_convert_fusion.3), channel_id=1, source_target_pairs={{0,16},{4,20},{8,24},{12,28},{16,0},{20,4},{24,8},{28,12},{32,48},... | collective-permute-start | bytes 983048 | tf_op jit(solution)/shard_map/ppermute | solution.py:32
  58.7 23.2 %collective-permute-start.3 = (bf16[128,1280]{0,1:T(8,128)(2,1)S(1)}, bf16[128,1280]{0,1:T(8,128)(2,1)S(1)}, u32[]{:S(2)}, u32[]{:S(2)}) collective-permute-start(bf16[128,1280]{0,1:T(8,128)(2,1)S(1)} %add_convert_fusion.2), channel_id=1, source_target_pairs={{0,32},{4,36},{8,40},{12,44},{16,48},{20,52},{24,56},{28,60},{32,0... | collective-permute-start | bytes 983048 | tf_op jit(solution)/shard_map/ppermute | solution.py:32
  82.2 13.9 %collective-permute-start.4 = (bf16[128,1280]{0,1:T(8,128)(2,1)S(1)}, bf16[128,1280]{0,1:T(8,128)(2,1)S(1)}, u32[]{:S(2)}, u32[]{:S(2)}) collective-permute-start(bf16[128,1280]{0,1:T(8,128)(2,1)S(1)} %add_convert_fusion.1), channel_id=1, source_target_pairs={{0,64},{4,68},{8,72},{12,76},{16,80},{20,84},{24,88},{28,92},{32,9... | collective-permute-start | bytes 983048 | tf_op jit(solution)/shard_map/ppermute | solution.py:32
  96.3 10.8 %collective-permute-start.5 = (bf16[128,1280]{0,1:T(8,128)(2,1)S(1)}, bf16[128,1280]{0,1:T(8,128)(2,1)S(1)}, u32[]{:S(2)}, u32[]{:S(2)}) collective-permute-start(bf16[128,1280]{0,1:T(8,128)(2,1)S(1)} %add_convert_fusion), channel_id=1, source_target_pairs={{0,128},{4,132},{8,136},{12,140},{16,144},{20,148},{24,152},{28,15... | collective-permute-start | bytes 983048 | tf_op jit(solution)/shard_map/ppermute | solution.py:32
  107.2 12.0 %copy-start.4 = (f32[1280]{0:T(1024)S(1)}, f32[1280]{0:T(1024)}, u32[]{:S(2)}) copy-start(f32[1280]{0:T(1024)} %param.20) | copy-start | bytes 15364
Sparse Core Ops, SparseCore 0:
  10.0 92.0 all-gather.1
where the time goes:
time: 144 us; the launch traced here: 143 us
  waiting for transfers between devices  71 us (49%)
  blocking collectives  21.5 us (15%)
  starting transfers between devices  17.8 us (12%)
  between operations  13.8 us (10%)
  matrix products  11.5 us (8%)
  local copies, waits for them, and re-layouts  5.27 us (4%)
  other arithmetic  2.67 us (2%)
    ppermute x6, waiting for transfers between devices, swapped(): return lax.ppermute(value, axis, pairs)  64.9 us
    all_to_all x1, starting transfers between devices, from_everyone(): return lax.all_to_all(copies, axis, split_axis=0, concat_axis=0, tiled=True)  12.2 us
    all_to_all x1, blocking collectives, summed_on_arrival(): parts = lax.all_to_all(split_up(array, dim, peers), axis, 0, 0, tiled=True)  11.2 us
    all_to_all x1, blocking collectives, from_everyone(): return lax.all_to_all(copies, axis, split_axis=0, concat_axis=0, tiled=True)  10.3 us
    ppermute x6, starting transfers between devices, swapped(): return lax.ppermute(value, axis, pairs)  5.58 us
    dot_general x1, matrix products, per_device(): jnp.dot(normed, lax.all_gather(out_proj, 'seq', axis=1, tiled=True), pref...  5.43 us
    all_to_all x1, waiting for transfers between devices, from_everyone(): return lax.all_to_all(copies, axis, split_axis=0, concat_axis=0, tiled=True)  5.35 us
    dot_general x6, matrix products, per_device(): level_read = jnp.dot(query_f32, buckets[level_pos], precision=highest)  4.3 us
  transfers between devices with their start and end apart: 8, of which 6 were waited for; matrix products, arithmetic and copies ran while one was open for 9% of the time, Pallas kernels for 0%

commit v1 on v0

v1 whole, which is shorter than its diff:
```python
import jax
import jax.numpy as jnp
from jax import lax
from jax.experimental import pallas as pl
from jax.experimental.pallas import tpu as pltpu
from jax.sharding import Mesh
from jax.sharding import PartitionSpec as P

DI = 5120
EPS = 1e-05
NX, NZ, NY = 4, 8, 4
TOK, COLS, HEADS, NST = 128, 1280, 20, 128
HALF, QUART = 640, 320
LANE = 128
BF = jnp.bfloat16
F32 = jnp.float32
I32 = jnp.int32
NT = (((1,), (1,)), ((), ()))
TN = (((0,), (0,)), ((), ()))


def flip(value, axis, mask, size):
    return lax.ppermute(value, axis, [(i, i ^ mask) for i in range(size)])


def shift(value, axis, step, size):
    return lax.ppermute(value, axis, [(i, (i + step) % size) for i in range(size)])


def call(body, place, args, outs, scratch=(), flops=10**8, vmem=4):
    return pl.pallas_call(
        body,
        out_shape=outs,
        in_specs=[pl.BlockSpec(memory_space=pltpu.SMEM)]
        + [pl.BlockSpec(memory_space=pltpu.VMEM)] * len(args),
        out_specs=[pl.BlockSpec(memory_space=pltpu.VMEM)] * len(outs),
        scratch_shapes=list(scratch),
        compiler_params=pltpu.CompilerParams(vmem_limit_bytes=vmem << 20),
        cost_estimate=pl.CostEstimate(flops=flops, bytes_accessed=1 << 20, transcendentals=0),
    )(place, *args)


def shaped(*shape, dtype=BF):
    return jax.ShapeDtypeStruct(shape, dtype)


def lanes():
    return lax.broadcasted_iota(I32, (TOK, LANE), 1)


def rows():
    return lax.broadcasted_iota(I32, (TOK, LANE), 0)


def two_heads(first, second, lane):
    return jnp.where(lane < 64, first, second)


def padded(value, width=LANE):
    zeros = jnp.zeros((value.shape[0], width - value.shape[1]), value.dtype)
    return jnp.concatenate([value, zeros], axis=1)


def put_totals(ref, at, size, totals):
    hi = totals.astype(BF)
    rest = totals - hi.astype(F32)
    mid = rest.astype(BF)
    low = (rest - mid.astype(F32)).astype(BF)
    ref[at : at + size, :] = hi
    ref[at + size : at + 2 * size, :] = mid
    ref[at + 2 * size : at + 3 * size, :] = low


def get_totals(ref, at, size):
    parts = ref[at : at + 3 * size, :].astype(F32)
    return parts[:size] + parts[size : 2 * size] + parts[2 * size :]


def state_kernel(place, values, keys, log_decay, msg, cum_ref):
    cum = padded(log_decay[...])
    row, lane = rows(), lanes()
    step = 1
    while step < TOK:
        cum = cum + jnp.where(row >= step, pltpu.roll(cum, step, 0), 0.0)
        step *= 2
    cum_ref[...] = cum
    total = cum[TOK - 1 : TOK, :]
    factor = jnp.exp(total - cum)
    spread = jnp.broadcast_to(total, (TOK, LANE))
    spread = jnp.where(lane < 10, spread, pltpu.roll(spread, 6, 1))
    spread = jnp.where((lane < 10) | ((lane >= 16) & (lane < 26)), spread, 0.0)
    put_totals(msg, COLS, 32, spread.T[:32])
    key = keys[...]
    for p in range(10):
        cols = slice(p * LANE, (p + 1) * LANE)
        wide = two_heads(factor[:, 2 * p : 2 * p + 1], factor[:, 2 * p + 1 : 2 * p + 2], lane)
        decayed = (values[:, cols].astype(F32) * wide).astype(BF)
        msg[cols, :] = lax.dot_general(decayed, key, TN, preferred_element_type=F32).astype(BF)


def pair_kernel(place, own, got, msg, prefix):
    core = place[0]
    own_total = get_totals(own, COLS, 32)
    got_total = get_totals(got, COLS, 32)
    own_total = jnp.where(core == 0, own_total[:16], own_total[16:])
    got_total = jnp.where(core == 0, got_total[:16], got_total[16:])
    upper = core == 1
    own_factor = jnp.where(upper, 1.0, jnp.exp(got_total))
    got_factor = jnp.where(upper, jnp.exp(own_total), 1.0)
    put_totals(msg, HALF, 16, own_total + got_total)
    prefix[...] = jnp.where(upper, got_total, own_total)
    for h in range(10):
        at = pl.ds(pl.multiple_of(core * HALF + h * 64, 64), 64)
        merged = own_factor[h : h + 1] * own[at, :].astype(F32) + got_factor[h : h + 1] * got[at, :].astype(F32)
        msg[h * 64 : h * 64 + 64, :] = merged.astype(BF)


def chip_kernel(place, own, got, msg, prefix):
    zq = lax.rem(place[3], 2)
    upper = zq == 1
    own_total = get_totals(own, HALF, 16)
    got_total = get_totals(got, HALF, 16)
    own_factor = jnp.where(upper, 1.0, jnp.exp(got_total))
    got_factor = jnp.where(upper, jnp.exp(own_total), 1.0)
    put_totals(msg, QUART, 16, own_total + got_total)
    prefix[...] = jnp.where(upper, got_total, 0.0)
    for k in range(5):
        at = pl.ds(pl.multiple_of(zq * QUART + k * 64, 64), 64)
        own_f = jnp.where(zq == 0, own_factor[k : k + 1], own_factor[k + 5 : k + 6])
        got_f = jnp.where(zq == 0, got_factor[k : k + 1], got_factor[k + 5 : k + 6])
        merged = own_f * own[at, :].astype(F32) + got_f * got[at, :].astype(F32)
        msg[k * 64 : k * 64 + 64, :] = merged.astype(BF)


def merge_kernel(bit, place, own, got, old, msg, prefix):
    zq = lax.rem(place[3], 2)
    upper = lax.rem(place[3] // bit, 2) == 1
    own_total = get_totals(own, QUART, 16)
    got_total = get_totals(got, QUART, 16)
    own_factor = jnp.where(upper, 1.0, jnp.exp(got_total))
    got_factor = jnp.where(upper, jnp.exp(own_total), 1.0)
    put_totals(msg, QUART, 16, own_total + got_total)
    prefix[...] = old[...] + jnp.where(upper, got_total, 0.0)
    for k in range(5):
        at = slice(k * 64, k * 64 + 64)
        own_f = jnp.where(zq == 0, own_factor[k : k + 1], own_factor[k + 5 : k + 6])
        got_f = jnp.where(zq == 0, got_factor[k : k + 1], got_factor[k + 5 : k + 6])
        msg[at, :] = (own_f * own[at, :].astype(F32) + got_f * got[at, :].astype(F32)).astype(BF)


def merge_side_kernel(bit, place, own, got, old, before, msg, prefix, side):
    merge_kernel(bit, place, own, got, old, msg, prefix)
    side[:QUART, :] = before[:QUART, :]
    side[QUART:, :] = got[:QUART, :]


def lines_kernel(place, r1, r2, r3, old, late, prefix):
    zq = lax.rem(place[3], 2)
    odd = lax.rem(place[2], 2) == 1
    t1 = get_totals(r1, QUART, 16)
    t2 = get_totals(r2, QUART, 16)
    t3 = get_totals(r3, QUART, 16)
    prefix[...] = old[...] + jnp.where(odd, t1, 0.0)
    late[:QUART, :] = r1[:QUART, :]
    f2 = jnp.where(odd, 1.0, jnp.exp(t3))
    f3 = jnp.where(odd, jnp.exp(t2), 1.0)
    for k in range(5):
        at = slice(k * 64, k * 64 + 64)
        a = jnp.where(zq == 0, f2[k : k + 1], f2[k + 5 : k + 6])
        b = jnp.where(zq == 0, f3[k : k + 1], f3[k + 5 : k + 6])
        late[QUART + k * 64 : QUART + k * 64 + 64, :] = (
            a * r2[at, :].astype(F32) + b * r3[at, :].astype(F32)
        ).astype(BF)


def local_kernel(
    place, queries, keys, values, cum_ref, lam_index, segments, lam_table, skip, got, base, factors, mail
):
    core = place[0]
    row, lane = rows(), lanes()
    cum = cum_ref[...]
    cum_t = cum.T
    grow = jnp.exp(cum)
    picks = lax.broadcasted_iota(I32, (64, TOK), 0)
    onehot = (picks == lam_index[...]).astype(F32).astype(BF)

    def level(number):
        table = padded(lam_table[:, number, :])
        hi = table.astype(BF)
        rest = table - hi.astype(F32)
        mid = rest.astype(BF)
        low = (rest - mid.astype(F32)).astype(BF)
        out = lax.dot_general(onehot, hi, TN, preferred_element_type=F32)
        out = out + lax.dot_general(onehot, mid, TN, preferred_element_type=F32)
        return out + lax.dot_general(onehot, low, TN, preferred_element_type=F32)

    mine = jnp.zeros((TOK, LANE), F32)
    theirs = jnp.zeros((TOK, LANE), F32)
    for number in range(5):
        value = level(3 + number) * grow
        there = (lane >= number * 16) & (lane < number * 16 + 10)
        to_first = pltpu.roll(value, number * 16, 1)
        to_second = pltpu.roll(value, (number * 16 + LANE - 10) % LANE, 1)
        mine = jnp.where(there, jnp.where(core == 0, to_first, to_second), mine)
        theirs = jnp.where(there, jnp.where(core == 0, to_second, to_first), theirs)
    factors[...] = mine
    mail[:TOK, :] = queries[...]
    hi = theirs.astype(BF)
    mail[TOK : 2 * TOK, :] = hi
    mail[2 * TOK :, :] = (theirs - hi.astype(F32)).astype(BF)

    zero_level = jnp.where(core == 1, level(2) * grow, 0.0)
    near, far = level(0), level(1)
    q = queries[...]
    scores = lax.dot_general(q, keys[...], NT, preferred_element_type=F32)
    seg_row = jnp.broadcast_to(segments[...].astype(F32), (TOK, LANE))
    same = seg_row == seg_row.T
    causal = row >= lane
    for p in range(10):
        cols = slice(p * LANE, (p + 1) * LANE)
        pieces = []
        for h in (2 * p, 2 * p + 1):
            gap = jnp.where(causal, cum[:, h : h + 1] - cum_t[h : h + 1, :], -1e30)
            weight = jnp.where(same, near[:, h : h + 1], far[:, h : h + 1])
            weight = (scores * jnp.exp(gap) * weight).astype(BF)
            pieces.append(
                jnp.dot(weight, values[:, h * 64 : h * 64 + 64], preferred_element_type=F32)
            )
        read = lax.dot_general(q, got[cols, :], NT, preferred_element_type=F32)
        read = read * two_heads(zero_level[:, 2 * p : 2 * p + 1], zero_level[:, 2 * p + 1 : 2 * p + 2], lane)
        gain = two_heads(skip[:, 2 * p : 2 * p + 1], skip[:, 2 * p + 1 : 2 * p + 2], lane)
        base[:, cols] = jnp.concatenate(pieces, axis=1) + read + gain * values[:, cols].astype(F32)


def level_weights(place, factors, mail, first_total, prefixes):
    core, x, z = place[0], place[2], place[3]
    lane = lanes()
    blocks = [jnp.zeros((16, LANE), F32)] + [p[...] for p in prefixes]
    blocks = blocks + [jnp.zeros((16, LANE), F32)] * (8 - len(blocks))
    chip = jnp.concatenate(blocks, axis=0).T
    first = jnp.concatenate([first_total[...]] * 8, axis=0).T
    uppers = [lax.rem(z, 2), lax.rem(z // 2, 2), lax.rem(z // 4, 2), lax.rem(x, 2), lax.rem(x // 2, 2)]
    on = jnp.zeros((TOK, LANE), F32)
    for number in range(5):
        there = (lane >= number * 16) & (lane < number * 16 + 10)
        on = jnp.where(there, uppers[number].astype(F32), on)
    own_chip = jnp.exp(chip + jnp.where(core == 1, first, 0.0)) * on
    other_chip = jnp.exp(chip + jnp.where(core == 1, 0.0, first)) * on
    other = mail[TOK : 2 * TOK, :].astype(F32) + mail[2 * TOK :, :].astype(F32)
    return factors[...] * own_chip, other * other_chip


def add_levels(numbers, place, tables, pairs, q_own, q_other, own_w, other_w, start, finish_own, finish_other):
    zq = lax.rem(place[3], 2)
    lane = lanes()
    tables = list(tables)
    for own_ref, other_ref in pairs:
        own_v, other_v = own_ref(), other_ref()
        tables.append(
            jnp.concatenate(
                [jnp.where(zq == 0, own_v, other_v), jnp.where(zq == 0, other_v, own_v)], axis=0
            )
        )
    for p in range(5):
        cols = slice(p * LANE, (p + 1) * LANE)
        acc_own, acc_other = start(cols)
        for number, table in zip(numbers, tables):
            a, b = number * 16 + 2 * p, number * 16 + 2 * p + 1
            piece = table[p * LANE : (p + 1) * LANE]
            read = lax.dot_general(q_own, piece, NT, preferred_element_type=F32)
            acc_own = acc_own + read * two_heads(own_w[:, a : a + 1], own_w[:, b : b + 1], lane)
            read = lax.dot_general(q_other, piece, NT, preferred_element_type=F32)
            acc_other = acc_other + read * two_heads(other_w[:, a : a + 1], other_w[:, b : b + 1], lane)
        finish_own(cols, acc_own)
        finish_other(cols, acc_other)


def rows_of(ref, start=0):
    return lambda: ref[start : start + QUART, :]


def cross_kernel(
    place, queries, factors, mail, first_total, p2, p3, p4, p5, got1, got2, got3, side, own, other, own_w, other_w
):
    mine, theirs = level_weights(place, factors, mail, first_total, [p2, p3, p4, p5])
    own_w[...] = mine
    other_w[...] = theirs
    zero = jnp.zeros((TOK, LANE), F32)

    def keep_own(cols, value):
        own[:, cols] = value

    def keep_other(cols, value):
        other[:, cols] = value

    pairs = [(rows_of(got2), rows_of(side)), (rows_of(got3), rows_of(side, QUART))]
    add_levels(
        (0, 1, 2), place, [got1[:HALF, :]], pairs, queries[...], mail[:TOK, :], mine, theirs,
        lambda cols: (zero, zero), keep_own, keep_other,
    )


def late_kernel(place, queries, mail, own_w, other_w, late, late_side, own_in, other_in, own, back):
    def keep_own(cols, value):
        own[:, cols] = value

    def keep_back(cols, value):
        back[:, cols] = value.astype(BF)

    pairs = [
        (rows_of(late), rows_of(late_side)),
        (rows_of(late, QUART), rows_of(late_side, QUART)),
    ]
    add_levels(
        (3, 4), place, [], pairs, queries[...], mail[:TOK, :], own_w[...], other_w[...],
        lambda cols: (own_in[:, cols], other_in[:, cols]), keep_own, keep_back,
    )


def project_kernel(place, base, own, back, gate, gain, *refs):
    core, y = place[0], place[1]
    w_refs, out_refs, y_ref = refs[:16], refs[16:20], refs[20]
    part = TOK // NY
    lane = lanes()
    squares = jnp.zeros((TOK, LANE), F32)
    for p in range(10):
        cols = slice(p * LANE, (p + 1) * LANE)
        inner = slice((p % 5) * LANE, (p % 5) * LANE + LANE)
        cross = jnp.where(core == p // 5, own[:, inner], back[:, inner].astype(F32))
        gated = base[:, cols] + cross
        v = gate[:, cols].astype(F32)
        gated = gated * (v / (1.0 + jnp.exp(-v)))
        squares = squares + gated * gated
        y_ref[:, cols] = (gated * gain[:, cols]).astype(BF)
    squares = jnp.sum(squares, axis=1, keepdims=True)
    hi = squares.astype(BF).astype(F32)
    mid = (squares - hi).astype(BF).astype(F32)
    low = squares - hi - mid
    squares = jnp.where(lane == 0, hi, jnp.where(lane == 1, mid, jnp.where(lane == 2, low, 0.0)))
    squares = squares.astype(BF)
    mine = pl.ds(pl.multiple_of(core * HALF, HALF), HALF)
    rest = pl.ds(pl.multiple_of((1 - core) * HALF, HALF), HALF)
    y_mine, y_rest = y_ref[:, mine], y_ref[:, rest]

    def store(d, cols, value):
        for owner in range(NY):

            @pl.when(lax.rem(y + d, NY) == owner)
            def _():
                out_refs[d][:, cols] = value[owner * part : (owner + 1) * part]

    for d in range(NY):
        store(d, slice(2560, 2688), squares)
    for block in range(4):
        mine_w = jnp.concatenate([w_refs[2 * block][...], w_refs[2 * block + 1][...]], axis=0)
        rest_w = jnp.concatenate([w_refs[8 + 2 * block][...], w_refs[9 + 2 * block][...]], axis=0)
        total = lax.dot_general(y_mine, mine_w, NT, preferred_element_type=F32)
        total = total + lax.dot_general(y_rest, rest_w, NT, preferred_element_type=F32)
        total = total.astype(BF)
        for d in range(NY):
            store(d, slice(block * HALF, (block + 1) * HALF), total)


def finish_kernel(place, a_ref, b_ref, c_ref, d_ref, out_ref):
    x, z = place[2], place[3]

    def total(cols):
        left = a_ref[:, cols].astype(F32) + b_ref[:, cols].astype(F32)
        return left + (c_ref[:, cols].astype(F32) + d_ref[:, cols].astype(F32))

    squares = total(slice(2560, 2688))
    squares = squares[:, 0:1] + squares[:, 1:2] + squares[:, 2:3]
    inv = lax.rsqrt(squares / DI + EPS)
    amount = lax.rem(z + (NZ - 2), NZ) * 80
    for block in range(4):
        part = total(slice(block * HALF, (block + 1) * HALF)) * inv
        part = pltpu.roll(part, amount, 1)
        at = pl.multiple_of(lax.rem(x + (NX - 1 + block), NX) * HALF, HALF)
        out_ref[:, pl.ds(at, HALF)] = part.astype(BF)


def gather_weights(out_proj):
    core = lax.axis_index("core")
    own_rows = out_proj.T
    other_rows = flip(own_rows, "core", 1, 2)
    first = core == 0
    pair = jnp.concatenate(
        [jnp.where(first, own_rows, other_rows), jnp.where(first, other_rows, own_rows)], axis=0
    )
    mine = lax.dynamic_slice_in_dim(pair, core * HALF, HALF, 1)
    below1 = shift(mine, "z", 1, NZ)
    above1 = shift(mine, "z", -1, NZ)
    below2 = shift(below1, "z", 1, NZ)
    above2 = shift(above1, "z", -1, NZ)
    below3 = shift(below2, "z", 1, NZ)
    above3 = shift(above2, "z", -1, NZ)
    above4 = shift(above3, "z", -1, NZ)
    near = joined(below2, below1, mine, above1)
    far = joined(above2, above3, above4, below3)
    near_left = shift(near, "x", 1, NX)
    near_right = shift(near, "x", -1, NX)
    far_left = shift(far, "x", 1, NX)
    far_right = shift(far, "x", -1, NX)
    near_across = shift(near_left, "x", 1, NX)
    far_across = shift(far_right, "x", -1, NX)
    own = [near_left, far_left, near, far, near_right, far_right, near_across, far_across]
    order = (2, 3, 0, 4, 6, 1, 5, 7)
    others = [None] * 8
    for at in order:
        others[at] = flip(own[at], "core", 1, 2)
    return own, others


def join_kernel(place, a, b, c, d, out):
    for number, ref in enumerate((a, b, c, d)):
        out[number * 80 : (number + 1) * 80, :] = ref[...]


def joined(*pieces):
    return call(join_kernel, jnp.zeros((1,), I32), pieces, [shaped(QUART, HALF)], flops=10**6)[0]


def mixer(
    queries, key_rows, values, gate_rows, log_decay, skip_gain, lam_index, segments, lam_table, norm_gain, out_proj
):
    places = [lax.axis_index(name) for name in ("core", "y", "x", "z")]
    place = jnp.stack(places).astype(I32)
    own_w, other_w = gather_weights(out_proj)
    state, cum = call(
        state_kernel, place, (values, key_rows, log_decay),
        [shaped(COLS + 96, NST), shaped(TOK, LANE, dtype=F32)],
        vmem=6,
    )
    got0 = flip(state, "core", 1, 2)
    quart = shaped(QUART + 48, NST)
    line = shaped(16, LANE, dtype=F32)
    msg1, first_total = call(pair_kernel, place, (state, got0), [shaped(HALF + 48, NST), line])
    got1 = flip(msg1, "z", 1, NZ)
    msg2, p2 = call(chip_kernel, place, (msg1, got1), [quart, line])
    got2 = flip(msg2, "z", 2, NZ)
    msg3, p3 = call(lambda *r: merge_kernel(2, *r), place, (msg2, got2, p2), [quart, line])
    got3 = flip(msg3, "z", 4, NZ)
    msg4, p4, side = call(
        lambda *r: merge_side_kernel(4, *r), place, (msg3, got3, p3, got2), [quart, line, shaped(HALF, NST)]
    )
    r1 = flip(msg4, "x", 1, NX)
    r3 = flip(msg4, "x", 3, NX)
    r2 = flip(msg4, "x", 2, NX)
    side = flip(side, "z", 1, NZ)

    base, factors, mail = call(
        local_kernel, place,
        (
            queries, key_rows, values, cum, lam_index.reshape(1, TOK), segments.reshape(1, TOK),
            lam_table, skip_gain.reshape(1, HEADS), got0,
        ),
        [shaped(TOK, COLS, dtype=F32), shaped(TOK, LANE, dtype=F32), shaped(3 * TOK, LANE)],
        flops=3 * 10**8,
        vmem=12,
    )
    mail = flip(mail, "core", 1, 2)
    half = shaped(TOK, HALF, dtype=F32)
    late, p5 = call(lines_kernel, place, (r1, r2, r3, p4), [shaped(HALF, NST), line])
    late_side = flip(late, "z", 1, NZ)
    square = shaped(TOK, LANE, dtype=F32)
    own_acc, other_acc, own_lw, other_lw = call(
        cross_kernel, place,
        (queries, factors, mail, first_total, p2, p3, p4, p5, got1, got2, got3, side),
        [half, half, square, square],
        vmem=8,
    )
    own_cross, back = call(
        late_kernel, place,
        (queries, mail, own_lw, other_lw, late, late_side, own_acc, other_acc),
        [half, shaped(TOK, HALF)],
        vmem=8,
    )
    back = flip(back, "core", 1, 2)
    parts = call(
        project_kernel, place,
        (base, own_cross, back, gate_rows, norm_gain.reshape(1, COLS), *own_w, *other_w),
        [shaped(TOK // NY, 2688)] * NY,
        scratch=[pltpu.VMEM((TOK, COLS), BF)],
        flops=10**9,
        vmem=24,
    )
    arrived = [parts[0]]
    for d in range(1, NY):
        arrived.append(shift(parts[d], "y", d, NY))
    return call(finish_kernel, place, arrived, [shaped(TOK // NY, 2560)])[0]


def solution(mesh):
    inner = Mesh(mesh.devices.reshape(NX, NZ, 2, NY), ("x", "z", "core", "y"))
    seq = ("x", "z", "core")
    return jax.shard_map(
        mixer,
        mesh=inner,
        in_specs=(
            P(seq, None),
            P(seq, None),
            P(seq, "y"),
            P(seq, "y"),
            P(seq, "y"),
            P("y"),
            P(seq),
            P(seq),
            P(None, None, "y"),
            P("y"),
            P("y", seq),
        ),
        out_specs=P((*seq, "y"), None),
        check_vma=False,
    )
```

time: 144 us -> 101 us (0.70)
  waiting for transfers between devices: 71 us -> 38.6 us
  blocking collectives: 21.5 us -> 0 us
  Pallas kernels: 0 us -> 18.8 us
  starting transfers between devices: 17.8 us -> 35 us
  between operations: 13.8 us -> 0.31 us
  matrix products: 11.5 us -> 0 us
  other arithmetic: 2.67 us -> 0.11 us
    ppermute x6 -> x36, starting transfers between devices: 5.58 us -> 35 us  [the longest x16 26.3 us: shift(): lax.ppermute(value, axis, [(i, (i + step) % size) for i in range(size)])]
    ppermute x6 -> x36, waiting for transfers between devices: 64.9 us -> 38.6 us  [the longest x20 21.3 us: flip(): return lax.ppermute(value, axis, [(i, i ^ mask) for i in range(size)])]
    all_to_all x2 -> x0, blocking collectives: 21.5 us -> none  [the longest x1 11.2 us: summed_on_arrival(): parts = lax.all_to_all(split_up(array, dim, peers), axis, 0, 0, tiled=True)]
    pallas_call x0 -> x13, Pallas kernels: none -> 18.8 us  [call(): pl.pallas_call(body, out_shape=outs, in_specs=[pl.BlockSpec(memory_space=...]
    all_to_all x1 -> x0, starting transfers between devices: 12.2 us -> none  [from_everyone(): return lax.all_to_all(copies, axis, split_axis=0, concat_axis=0, tiled=True)]
    dot_general x11 -> x0, matrix products: 11.5 us -> none  [the longest x1 5.43 us: per_device(): jnp.dot(normed, lax.all_gather(out_proj, 'seq', axis=1, tiled=True), pref...]
    all_to_all x1 -> x0, waiting for transfers between devices: 5.35 us -> none  [from_everyone(): return lax.all_to_all(copies, axis, split_axis=0, concat_axis=0, tiled=True)]
    unnamed x20 -> x34, local copies, waits for them, and re-layouts: 2.34 us -> 6.21 us
  transfers between devices with their start and end apart: 8 -> 36, of which waited for: 6 -> 15; matrix products, arithmetic and copies ran while one was open for 9% -> 1% of each run, Pallas kernels for 0% -> 14%
where the time goes in v1:
time: 101 us; the launch traced here: 99 us
  waiting for transfers between devices  38.6 us (38%)
  starting transfers between devices  35 us (35%)
  Pallas kernels  18.8 us (19%)
  local copies, waits for them, and re-layouts  6.22 us (6%)
    ppermute x16, starting transfers between devices, shift(): lax.ppermute(value, axis, [(i, (i + step) % size) for i in range(size)])  26.3 us
    ppermute x20, waiting for transfers between devices, flip(): return lax.ppermute(value, axis, [(i, i ^ mask) for i in range(size)])  21.3 us
    pallas_call x13, Pallas kernels, call(): pl.pallas_call(body, out_shape=outs, in_specs=[pl.BlockSpec(memory_space=...  18.8 us
    ppermute x16, waiting for transfers between devices, shift(): lax.ppermute(value, axis, [(i, (i + step) % size) for i in range(size)])  17.3 us
    ppermute x20, starting transfers between devices, flip(): return lax.ppermute(value, axis, [(i, i ^ mask) for i in range(size)])  8.66 us
    unnamed x34, local copies, waits for them, and re-layouts  6.21 us
  transfers between devices with their start and end apart: 36, of which 15 were waited for; matrix products, arithmetic and copies ran while one was open for 1% of the time, Pallas kernels for 14%

profile of v1, /device:TPU:6, one launch (start us, length us, event | category | flops | bytes accessed | tf_op | source)
XLA Modules:
  0.0 99.0 jit_solution(16726397233661684365)
XLA Ops:
  2.4 1.6 %shard_map.109 = (bf16[1376,128]{1,0:T(8,128)(2,1)S(1)}, f32[128,128]{1,0:T(8,128)S(1)}) custom-call(s32[4]{0:T(128)S(1)} %pad_add_fusion.place.r_0_, bf16[128,1280]{1,0:T(8,128)(2,1)S(1)} %copy-done.1, bf16[128,128]{1,0:T(8,128)(2,1)S(1)} %copy-done.6, f32[128,20]{1,0:T(8,128)S(1)} %copy.12.log_decay), custom_call_target="tpu_custom_call" | custom-call | flops 100000000 | bytes 1048576 | tf_op jit(solution)/shard_map/pallas_call | solution.py:31
  4.6 5.9 %collective-permute-start.14 = (bf16[80,640]{1,0:T(8,128)(2,1)S(1)}, bf16[80,640]{1,0:T(8,128)(2,1)S(1)}, u32[]{:S(2)}, u32[]{:S(2)}) collective-permute-start(bf16[80,640]{1,0:T(8,128)(2,1)S(1)} %fusion.c), channel_id=1, source_target_pairs={{0,56},{8,0},{16,8},{24,16},{32,24},{40,32},{48,40},{56,48},{1,57}... | collective-permute-start | bytes 307208 | tf_op jit(solution)/shard_map/ppermute | solution.py:27
  11.3 1.6 %collective-permute-done.14.d = bf16[80,640]{1,0:T(8,128)(2,1)S(1)} collective-permute-done((bf16[80,640]{1,0:T(8,128)(2,1)S(1)}, bf16[80,640]{1,0:T(8,128)(2,1)S(1)}, u32[]{:S(2)}, u32[]{:S(2)}) %collective-permute-start.14) | collective-permute-done | bytes 102432 | tf_op jit(solution)/shard_map/ppermute | solution.py:27
  12.9 3.7 %collective-permute-start.16 = (bf16[80,640]{1,0:T(8,128)(2,1)S(1)}, bf16[80,640]{1,0:T(8,128)(2,1)S(1)}, u32[]{:S(2)}, u32[]{:S(2)}) collective-permute-start(bf16[80,640]{1,0:T(8,128)(2,1)S(1)} %collective-permute-done.14.d), channel_id=1, source_target_pairs={{0,56},{8,0},{16,8},{24,16},{32,24},{40,32},{48,40},{56,48},{1,57}... | collective-permute-start | bytes 307208 | tf_op jit(solution)/shard_map/ppermute | solution.py:27
  16.6 3.0 %collective-permute-done.16.a = bf16[80,640]{1,0:T(8,128)(2,1)S(1)} collective-permute-done((bf16[80,640]{1,0:T(8,128)(2,1)S(1)}, bf16[80,640]{1,0:T(8,128)(2,1)S(1)}, u32[]{:S(2)}, u32[]{:S(2)}) %collective-permute-start.16) | collective-permute-done | bytes 102432 | tf_op jit(solution)/shard_map/ppermute | solution.py:27
  19.6 2.9 %collective-permute-start.17 = (bf16[80,640]{1,0:T(8,128)(2,1)S(1)}, bf16[80,640]{1,0:T(8,128)(2,1)S(1)}, u32[]{:S(2)}, u32[]{:S(2)}) collective-permute-start(bf16[80,640]{1,0:T(8,128)(2,1)S(1)} %collective-permute-done.16.a), channel_id=1, source_target_pairs={{0,56},{8,0},{16,8},{24,16},{32,24},{40,32},{48,40},{56,48},{1,57}... | collective-permute-start | bytes 307208 | tf_op jit(solution)/shard_map/ppermute | solution.py:27
  24.2 2.4 %collective-permute-start.15 = (bf16[320,640]{1,0:T(8,128)(2,1)S(1)}, bf16[320,640]{1,0:T(8,128)(2,1)S(1)}, u32[]{:S(2)}, u32[]{:S(2)}) collective-permute-start(bf16[320,640]{1,0:T(8,128)(2,1)S(1)} %shard_map.118.refs_2_), channel_id=1, source_target_pairs={{0,64},{64,128},{128,192},{192,0},{1,65},{65,129},{129,193},{193,1... | collective-permute-start | bytes 1228808 | tf_op jit(solution)/shard_map/ppermute | solution.py:27
  26.7 2.0 %collective-permute-done.3.r_2_.r_4_.got2 = bf16[368,128]{1,0:T(8,128)(2,1)S(1)} collective-permute-done((bf16[368,128]{1,0:T(8,128)(2,1)S(1)}, bf16[368,128]{1,0:T(8,128)(2,1)S(1)}, u32[]{:S(2)}, u32[]{:S(2)}) %collective-permute-start.3) | collective-permute-done | bytes 94240 | tf_op jit(solution)/shard_map/ppermute | solution.py:23
  28.6 1.3 %collective-permute-start.18 = (bf16[80,640]{1,0:T(8,128)(2,1)S(1)}, bf16[80,640]{1,0:T(8,128)(2,1)S(1)}, u32[]{:S(2)}, u32[]{:S(2)}) collective-permute-start(bf16[80,640]{1,0:T(8,128)(2,1)S(1)} %collective-permute-done.17.b), channel_id=1, source_target_pairs={{0,56},{8,0},{16,8},{24,16},{32,24},{40,32},{48,40},{56,48},{1,57}... | collective-permute-start | bytes 307208 | tf_op jit(solution)/shard_map/ppermute | solution.py:27
  29.9 1.2 %shard_map.113 = (bf16[368,128]{1,0:T(8,128)(2,1)}, f32[16,128]{1,0:T(8,128)S(1)}) custom-call(s32[4]{0:T(128)S(1)} %pad_add_fusion.place.r_0_, bf16[368,128]{1,0:T(8,128)(2,1)S(1)} %get-tuple-element.39.r_1_, bf16[368,128]{1,0:T(8,128)(2,1)S(1)} %collective-permute-done.3.r_2_.r_4_.got2, f32[16,128]{1,0:T(8,128)S(1)} %get-tuple-element.38.r_3_.p2), custom_call_target="tpu_custom_call" | custom-call | flops 100000000 | bytes 1048576 | tf_op jit(solution)/shard_map/pallas_call | solution.py:31
  31.1 1.4 %collective-permute-done.19.d = bf16[80,640]{1,0:T(8,128)(2,1)S(1)} collective-permute-done((bf16[80,640]{1,0:T(8,128)(2,1)S(1)}, bf16[80,640]{1,0:T(8,128)(2,1)S(1)}, u32[]{:S(2)}, u32[]{:S(2)}) %collective-permute-start.19) | collective-permute-done | bytes 102432 | tf_op jit(solution)/shard_map/ppermute | solution.py:27
  32.5 2.1 %collective-permute-start.4 = (bf16[368,128]{1,0:T(8,128)(2,1)}, bf16[368,128]{1,0:T(8,128)(2,1)}, u32[]{:S(2)}, u32[]{:S(2)}) collective-permute-start(bf16[368,128]{1,0:T(8,128)(2,1)} %get-tuple-element.41.r_1_), channel_id=1, source_target_pairs={{0,32},{8,40},{16,48},{24,56},{32,0},{40,8},{48,16},{56,24},{1,33}... | collective-permute-start | bytes 282632 | tf_op jit(solution)/shard_map/ppermute | solution.py:23
  35.0 1.0 %copy.13.lam_table = f32[64,8,20]{2,1,0:T(8,128)S(1)} copy(f32[64,8,20]{0,1,2:T(8,128)} %param.19) | data formatting | bytes 81920 | tf_op args[8]
  38.4 4.0 %shard_map.110 = (f32[128,1280]{1,0:T(8,128)S(1)}, f32[128,128]{1,0:T(8,128)S(1)}, bf16[384,128]{1,0:T(8,128)(2,1)S(1)}) custom-call(s32[4]{0:T(128)S(1)} %pad_add_fusion.place.r_0_, bf16[128,128]{1,0:T(8,128)(2,1)S(1)} %copy-done.5, bf16[128,128]{1,0:T(8,128)(2,1)S(1)} %copy-done.7, bf16[128,1280]{1,0:T(8,128)(2,1)S(1)} %copy-done.2, ...), custom_call_target="tpu_custom_call" | custom-call | flops 300000000 | bytes 1048576 | tf_op jit(solution)/shard_map/pallas_call | solution.py:31
  43.8 3.2 %collective-permute-start.7 = (bf16[368,128]{1,0:T(8,128)(2,1)S(1)}, bf16[368,128]{1,0:T(8,128)(2,1)S(1)}, u32[]{:S(2)}, u32[]{:S(2)}) collective-permute-start(bf16[368,128]{1,0:T(8,128)(2,1)S(1)} %get-tuple-element.43), channel_id=1, source_target_pairs={{0,192},{64,128},{128,64},{192,0},{1,193},{65,129},{129,65},{193,1... | collective-permute-start | bytes 282632 | tf_op jit(solution)/shard_map/ppermute | solution.py:23
  47.1 1.1 %collective-permute-start.20 = (bf16[320,640]{1,0:T(8,128)(2,1)S(1)}, bf16[320,640]{1,0:T(8,128)(2,1)S(1)}, u32[]{:S(2)}, u32[]{:S(2)}) collective-permute-start(bf16[320,640]{1,0:T(8,128)(2,1)S(1)} %shard_map.119.refs_3_), channel_id=1, source_target_pairs={{0,64},{64,128},{128,192},{192,0},{1,65},{65,129},{129,193},{193,1... | collective-permute-start | bytes 1228808 | tf_op jit(solution)/shard_map/ppermute | solution.py:27
  48.2 3.7 %collective-permute-done.7.r3 = bf16[368,128]{1,0:T(8,128)(2,1)S(1)} collective-permute-done((bf16[368,128]{1,0:T(8,128)(2,1)S(1)}, bf16[368,128]{1,0:T(8,128)(2,1)S(1)}, u32[]{:S(2)}, u32[]{:S(2)}) %collective-permute-start.7) | collective-permute-done | bytes 94240 | tf_op jit(solution)/shard_map/ppermute | solution.py:23
  53.1 8.6 %collective-permute-done.5.r1 = bf16[368,128]{1,0:T(8,128)(2,1)S(1)} collective-permute-done((bf16[368,128]{1,0:T(8,128)(2,1)S(1)}, bf16[368,128]{1,0:T(8,128)(2,1)S(1)}, u32[]{:S(2)}, u32[]{:S(2)}) %collective-permute-start.5) | collective-permute-done | bytes 94240 | tf_op jit(solution)/shard_map/ppermute | solution.py:23
  62.5 1.2 %collective-permute-start.24 = (bf16[320,640]{1,0:T(8,128)(2,1)S(1)}, bf16[320,640]{1,0:T(8,128)(2,1)S(1)}, u32[]{:S(2)}, u32[]{:S(2)}) collective-permute-start(bf16[320,640]{1,0:T(8,128)(2,1)S(1)} %collective-permute-done.22.refs_5_), channel_id=1, source_target_pairs={{0,192},{64,0},{128,64},{192,128},{1,193},{65,1},{129,65},{193,129... | collective-permute-start | bytes 1228808 | tf_op jit(solution)/shard_map/ppermute | solution.py:27
  65.2 5.2 %collective-permute-done.9.late_side = bf16[640,128]{1,0:T(8,128)(2,1)S(1)} collective-permute-done((bf16[640,128]{1,0:T(8,128)(2,1)S(1)}, bf16[640,128]{1,0:T(8,128)(2,1)S(1)}, u32[]{:S(2)}, u32[]{:S(2)}) %collective-permute-start.9) | collective-permute-done | bytes 163872 | tf_op jit(solution)/shard_map/ppermute | solution.py:23
  71.0 2.6 %collective-permute-done.23.refs_6_ = bf16[320,640]{1,0:T(8,128)(2,1)S(1)} collective-permute-done((bf16[320,640]{1,0:T(8,128)(2,1)S(1)}, bf16[320,640]{1,0:T(8,128)(2,1)S(1)}, u32[]{:S(2)}, u32[]{:S(2)}) %collective-permute-start.23) | collective-permute-done | bytes 409632 | tf_op jit(solution)/shard_map/ppermute | solution.py:27
  73.6 1.7 %collective-permute-done.24.refs_7_ = bf16[320,640]{1,0:T(8,128)(2,1)S(1)} collective-permute-done((bf16[320,640]{1,0:T(8,128)(2,1)S(1)}, bf16[320,640]{1,0:T(8,128)(2,1)S(1)}, u32[]{:S(2)}, u32[]{:S(2)}) %collective-permute-start.24) | collective-permute-done | bytes 409632 | tf_op jit(solution)/shard_map/ppermute | solution.py:27
  75.3 2.4 %shard_map.116 = (f32[128,640]{1,0:T(8,128)S(1)}, f32[128,640]{1,0:T(8,128)S(1)}, f32[128,128]{1,0:T(8,128)S(1)}, f32[128,128]{1,0:T(8,128)S(1)}) custom-call(s32[4]{0:T(128)S(1)} %pad_add_fusion.place.r_0_, bf16[128,128]{1,0:T(8,128)(2,1)S(1)} %copy-done.5, f32[128,128]{1,0:T(8,128)S(1)} %get-tuple-element.35.factors, ...), custom_call_target="tpu_custom_call" | custom-call | flops 100000000 | bytes 1048576 | tf_op jit(solution)/shard_map/pallas_call | solution.py:31
  77.7 1.5 %shard_map.117 = (f32[128,640]{1,0:T(8,128)S(1)}, bf16[128,640]{1,0:T(8,128)(2,1)S(1)}) custom-call(s32[4]{0:T(128)S(1)} %pad_add_fusion.place.r_0_, bf16[128,128]{1,0:T(8,128)(2,1)S(1)} %copy-done.5, bf16[384,128]{1,0:T(8,128)(2,1)S(1)} %collective-permute-done.1.mail, f32[128,128]{1,0:T(8,128)S(1)} %get-tuple-element.46.own_w, ...), custom_call_target="tpu_custom_call" | custom-call | flops 100000000 | bytes 1048576 | tf_op jit(solution)/shard_map/pallas_call | solution.py:31
  79.9 1.0 %collective-permute-done.10.back = bf16[128,640]{1,0:T(8,128)(2,1)S(1)} collective-permute-done((bf16[128,640]{1,0:T(8,128)(2,1)S(1)}, bf16[128,640]{1,0:T(8,128)(2,1)S(1)}, u32[]{:S(2)}, u32[]{:S(2)}) %collective-permute-start.10) | collective-permute-done | bytes 163872 | tf_op jit(solution)/shard_map/ppermute | solution.py:23
  80.9 3.7 %shard_map.120 = (bf16[32,2688]{1,0:T(8,128)(2,1)S(1)}, bf16[32,2688]{1,0:T(8,128)(2,1)S(1)}, bf16[32,2688]{1,0:T(8,128)(2,1)S(1)}, bf16[32,2688]{1,0:T(8,128)(2,1)S(1)}) custom-call(s32[4]{0:T(128)S(1)} %pad_add_fusion.place.r_0_, f32[128,1280]{1,0:T(8,128)S(1)} %get-tuple-element.33.base, f32[128,640]{1,0:T(8,128)S(1)} %get-tuple-element.51.own, ...), custom_call_target="tpu_custom_call" | custom-call | flops 1000000000 | bytes 1048576 | tf_op jit(solution)/shard_map/pallas_call | solution.py:31
  84.6 1.7 %collective-permute-start.33 = (bf16[32,2688]{1,0:T(8,128)(2,1)S(1)}, bf16[32,2688]{1,0:T(8,128)(2,1)S(1)}, u32[]{:S(2)}, u32[]{:S(2)}) collective-permute-start(bf16[32,2688]{1,0:T(8,128)(2,1)S(1)} %get-tuple-element.54), channel_id=1, source_target_pairs={{0,1},{1,2},{2,3},{3,0},{4,5},{5,6},{6,7},{7,4},{8,9},{9,10},{10,1... | collective-permute-start | bytes 516104 | tf_op jit(solution)/shard_map/ppermute | solution.py:27
  86.3 2.9 %collective-permute-start.34 = (bf16[32,2688]{1,0:T(8,128)(2,1)S(1)}, bf16[32,2688]{1,0:T(8,128)(2,1)S(1)}, u32[]{:S(2)}, u32[]{:S(2)}) collective-permute-start(bf16[32,2688]{1,0:T(8,128)(2,1)S(1)} %get-tuple-element.55), channel_id=1, source_target_pairs={{0,2},{1,3},{2,0},{3,1},{4,6},{5,7},{6,4},{7,5},{8,10},{9,11},{10,... | collective-permute-start | bytes 516104 | tf_op jit(solution)/shard_map/ppermute | solution.py:27
  89.2 1.3 %collective-permute-start.35 = (bf16[32,2688]{1,0:T(8,128)(2,1)S(1)}, bf16[32,2688]{1,0:T(8,128)(2,1)S(1)}, u32[]{:S(2)}, u32[]{:S(2)}) collective-permute-start(bf16[32,2688]{1,0:T(8,128)(2,1)S(1)} %get-tuple-element.56), channel_id=1, source_target_pairs={{0,3},{1,0},{2,1},{3,2},{4,7},{5,4},{6,5},{7,6},{8,11},{9,8},{10,9... | collective-permute-start | bytes 516104 | tf_op jit(solution)/shard_map/ppermute | solution.py:27
  90.5 2.1 %collective-permute-done.33.b_ref = bf16[32,2688]{1,0:T(8,128)(2,1)S(1)} collective-permute-done((bf16[32,2688]{1,0:T(8,128)(2,1)S(1)}, bf16[32,2688]{1,0:T(8,128)(2,1)S(1)}, u32[]{:S(2)}, u32[]{:S(2)}) %collective-permute-start.33) | collective-permute-done | bytes 172064 | tf_op jit(solution)/shard_map/ppermute | solution.py:27
  92.6 4.9 %collective-permute-done.34.c_ref = bf16[32,2688]{1,0:T(8,128)(2,1)S(1)} collective-permute-done((bf16[32,2688]{1,0:T(8,128)(2,1)S(1)}, bf16[32,2688]{1,0:T(8,128)(2,1)S(1)}, u32[]{:S(2)}, u32[]{:S(2)}) %collective-permute-start.34) | collective-permute-done | bytes 172064 | tf_op jit(solution)/shard_map/ppermute | solution.py:27
  97.5 1.5 %shard_map.121 = bf16[32,2560]{1,0:T(8,128)(2,1)} custom-call(s32[4]{0:T(128)S(1)} %pad_add_fusion.place.r_0_, bf16[32,2688]{1,0:T(8,128)(2,1)S(1)} %get-tuple-element.53.a_ref, bf16[32,2688]{1,0:T(8,128)(2,1)S(1)} %collective-permute-done.33.b_ref, bf16[32,2688]{1,0:T(8,128)(2,1)S(1)} %collective-permute-done.34.c_ref, ...), custom_call_target="tpu_custom_call" | custom-call | flops 100000000 | bytes 1048576 | tf_op jit(solution)/shard_map/pallas_call | solution.py:31
  (91 shorter events, 14.2 us)
Async XLA Ops:
  4.0 6.6 %collective-permute-start = (bf16[1376,128]{1,0:T(8,128)(2,1)S(1)}, bf16[1376,128]{1,0:T(8,128)(2,1)S(1)}, u32[]{:S(2)}, u32[]{:S(2)}) collective-permute-start(bf16[1376,128]{1,0:T(8,128)(2,1)S(1)} %get-tuple-element.32.own), channel_id=1, source_target_pairs={{0,4},{4,0},{1,5},{5,1},{2,6},{6,2},{3,7},{7,3},{8,12},{12,8},{9,1... | collective-permute-start | bytes 1056776 | tf_op jit(solution)/shard_map/ppermute | solution.py:23
  4.6 8.3 %collective-permute-start.14 = (bf16[80,640]{1,0:T(8,128)(2,1)S(1)}, bf16[80,640]{1,0:T(8,128)(2,1)S(1)}, u32[]{:S(2)}, u32[]{:S(2)}) collective-permute-start(bf16[80,640]{1,0:T(8,128)(2,1)S(1)} %fusion.c), channel_id=1, source_target_pairs={{0,56},{8,0},{16,8},{24,16},{32,24},{40,32},{48,40},{56,48},{1,57}... | collective-permute-start | bytes 307208 | tf_op jit(solution)/shard_map/ppermute | solution.py:27
  10.6 6.0 %collective-permute-start.12 = (bf16[80,640]{1,0:T(8,128)(2,1)S(1)}, bf16[80,640]{1,0:T(8,128)(2,1)S(1)}, u32[]{:S(2)}, u32[]{:S(2)}) collective-permute-start(bf16[80,640]{1,0:T(8,128)(2,1)S(1)} %fusion.c), channel_id=1, source_target_pairs={{0,8},{8,16},{16,24},{24,32},{32,40},{40,48},{48,56},{56,0},{1,9},... | collective-permute-start | bytes 307208 | tf_op jit(solution)/shard_map/ppermute | solution.py:27
  11.2 11.3 %collective-permute-start.2 = (bf16[688,128]{1,0:T(8,128)(2,1)S(1)}, bf16[688,128]{1,0:T(8,128)(2,1)S(1)}, u32[]{:S(2)}, u32[]{:S(2)}) collective-permute-start(bf16[688,128]{1,0:T(8,128)(2,1)S(1)} %get-tuple-element.37.own), channel_id=1, source_target_pairs={{0,8},{8,0},{16,24},{24,16},{32,40},{40,32},{48,56},{56,48},{1,9},... | collective-permute-start | bytes 528392 | tf_op jit(solution)/shard_map/ppermute | solution.py:23
  12.9 6.7 %collective-permute-start.16 = (bf16[80,640]{1,0:T(8,128)(2,1)S(1)}, bf16[80,640]{1,0:T(8,128)(2,1)S(1)}, u32[]{:S(2)}, u32[]{:S(2)}) collective-permute-start(bf16[80,640]{1,0:T(8,128)(2,1)S(1)} %collective-permute-done.14.d), channel_id=1, source_target_pairs={{0,56},{8,0},{16,8},{24,16},{32,24},{40,32},{48,40},{56,48},{1,57}... | collective-permute-start | bytes 307208 | tf_op jit(solution)/shard_map/ppermute | solution.py:27
  16.6 6.6 %collective-permute-start.13 = (bf16[80,640]{1,0:T(8,128)(2,1)S(1)}, bf16[80,640]{1,0:T(8,128)(2,1)S(1)}, u32[]{:S(2)}, u32[]{:S(2)}) collective-permute-start(bf16[80,640]{1,0:T(8,128)(2,1)S(1)} %collective-permute-done.12.b), channel_id=1, source_target_pairs={{0,8},{8,16},{16,24},{24,32},{32,40},{40,48},{48,56},{56,0},{1,9},... | collective-permute-start | bytes 307208 | tf_op jit(solution)/shard_map/ppermute | solution.py:27
  19.6 7.1 %collective-permute-start.17 = (bf16[80,640]{1,0:T(8,128)(2,1)S(1)}, bf16[80,640]{1,0:T(8,128)(2,1)S(1)}, u32[]{:S(2)}, u32[]{:S(2)}) collective-permute-start(bf16[80,640]{1,0:T(8,128)(2,1)S(1)} %collective-permute-done.16.a), channel_id=1, source_target_pairs={{0,56},{8,0},{16,8},{24,16},{32,24},{40,32},{48,40},{56,48},{1,57}... | collective-permute-start | bytes 307208 | tf_op jit(solution)/shard_map/ppermute | solution.py:27
  23.2 23.7 %collective-permute-start.27 = (bf16[320,640]{1,0:T(8,128)(2,1)S(1)}, bf16[320,640]{1,0:T(8,128)(2,1)S(1)}, u32[]{:S(2)}, u32[]{:S(2)}) collective-permute-start(bf16[320,640]{1,0:T(8,128)(2,1)S(1)} %shard_map.118.refs_2_), channel_id=1, source_target_pairs={{0,4},{4,0},{1,5},{5,1},{2,6},{6,2},{3,7},{7,3},{8,12},{12,8},{9,1... | collective-permute-start | bytes 1228808 | tf_op jit(solution)/shard_map/ppermute | solution.py:23
  23.3 23.6 %collective-permute-start.21 = (bf16[320,640]{1,0:T(8,128)(2,1)S(1)}, bf16[320,640]{1,0:T(8,128)(2,1)S(1)}, u32[]{:S(2)}, u32[]{:S(2)}) collective-permute-start(bf16[320,640]{1,0:T(8,128)(2,1)S(1)} %shard_map.118.refs_2_), channel_id=1, source_target_pairs={{0,192},{64,0},{128,64},{192,128},{1,193},{65,1},{129,65},{193,129... | collective-permute-start | bytes 1228808 | tf_op jit(solution)/shard_map/ppermute | solution.py:27
  24.2 22.9 %collective-permute-start.15 = (bf16[320,640]{1,0:T(8,128)(2,1)S(1)}, bf16[320,640]{1,0:T(8,128)(2,1)S(1)}, u32[]{:S(2)}, u32[]{:S(2)}) collective-permute-start(bf16[320,640]{1,0:T(8,128)(2,1)S(1)} %shard_map.118.refs_2_), channel_id=1, source_target_pairs={{0,64},{64,128},{128,192},{192,0},{1,65},{65,129},{129,193},{193,1... | collective-permute-start | bytes 1228808 | tf_op jit(solution)/shard_map/ppermute | solution.py:27
  26.7 5.9 %collective-permute-start.19 = (bf16[80,640]{1,0:T(8,128)(2,1)S(1)}, bf16[80,640]{1,0:T(8,128)(2,1)S(1)}, u32[]{:S(2)}, u32[]{:S(2)}) collective-permute-start(bf16[80,640]{1,0:T(8,128)(2,1)S(1)} %collective-permute-done.13.a), channel_id=1, source_target_pairs={{0,8},{8,16},{16,24},{24,32},{32,40},{40,48},{48,56},{56,0},{1,9},... | collective-permute-start | bytes 307208 | tf_op jit(solution)/shard_map/ppermute | solution.py:27
  28.6 6.0 %collective-permute-start.18 = (bf16[80,640]{1,0:T(8,128)(2,1)S(1)}, bf16[80,640]{1,0:T(8,128)(2,1)S(1)}, u32[]{:S(2)}, u32[]{:S(2)}) collective-permute-start(bf16[80,640]{1,0:T(8,128)(2,1)S(1)} %collective-permute-done.17.b), channel_id=1, source_target_pairs={{0,56},{8,0},{16,8},{24,16},{32,24},{40,32},{48,40},{56,48},{1,57}... | collective-permute-start | bytes 307208 | tf_op jit(solution)/shard_map/ppermute | solution.py:27
  32.5 9.9 %collective-permute-start.4 = (bf16[368,128]{1,0:T(8,128)(2,1)}, bf16[368,128]{1,0:T(8,128)(2,1)}, u32[]{:S(2)}, u32[]{:S(2)}) collective-permute-start(bf16[368,128]{1,0:T(8,128)(2,1)} %get-tuple-element.41.r_1_), channel_id=1, source_target_pairs={{0,32},{8,40},{16,48},{24,56},{32,0},{40,8},{48,16},{56,24},{1,33}... | collective-permute-start | bytes 282632 | tf_op jit(solution)/shard_map/ppermute | solution.py:23
  34.7 27.8 %collective-permute-start.22 = (bf16[320,640]{1,0:T(8,128)(2,1)S(1)}, bf16[320,640]{1,0:T(8,128)(2,1)S(1)}, u32[]{:S(2)}, u32[]{:S(2)}) collective-permute-start(bf16[320,640]{1,0:T(8,128)(2,1)S(1)} %shard_map.119.refs_3_), channel_id=1, source_target_pairs={{0,192},{64,0},{128,64},{192,128},{1,193},{65,1},{129,65},{193,129... | collective-permute-start | bytes 1228808 | tf_op jit(solution)/shard_map/ppermute | solution.py:27
  43.8 8.2 %collective-permute-start.7 = (bf16[368,128]{1,0:T(8,128)(2,1)S(1)}, bf16[368,128]{1,0:T(8,128)(2,1)S(1)}, u32[]{:S(2)}, u32[]{:S(2)}) collective-permute-start(bf16[368,128]{1,0:T(8,128)(2,1)S(1)} %get-tuple-element.43), channel_id=1, source_target_pairs={{0,192},{64,128},{128,64},{192,0},{1,193},{65,129},{129,65},{193,1... | collective-permute-start | bytes 282632 | tf_op jit(solution)/shard_map/ppermute | solution.py:23
  47.0 6.1 %collective-permute-start.6 = (bf16[368,128]{1,0:T(8,128)(2,1)S(1)}, bf16[368,128]{1,0:T(8,128)(2,1)S(1)}, u32[]{:S(2)}, u32[]{:S(2)}) collective-permute-start(bf16[368,128]{1,0:T(8,128)(2,1)S(1)} %get-tuple-element.43), channel_id=1, source_target_pairs={{0,128},{64,192},{128,0},{192,64},{1,129},{65,193},{129,1},{193,65... | collective-permute-start | bytes 282632 | tf_op jit(solution)/shard_map/ppermute | solution.py:23
  47.0 17.3 %collective-permute-start.28 = (bf16[320,640]{1,0:T(8,128)(2,1)S(1)}, bf16[320,640]{1,0:T(8,128)(2,1)S(1)}, u32[]{:S(2)}, u32[]{:S(2)}) collective-permute-start(bf16[320,640]{1,0:T(8,128)(2,1)S(1)} %shard_map.119.refs_3_), channel_id=1, source_target_pairs={{0,4},{4,0},{1,5},{5,1},{2,6},{6,2},{3,7},{7,3},{8,12},{12,8},{9,1... | collective-permute-start | bytes 1228808 | tf_op jit(solution)/shard_map/ppermute | solution.py:23
  47.1 18.1 %collective-permute-start.20 = (bf16[320,640]{1,0:T(8,128)(2,1)S(1)}, bf16[320,640]{1,0:T(8,128)(2,1)S(1)}, u32[]{:S(2)}, u32[]{:S(2)}) collective-permute-start(bf16[320,640]{1,0:T(8,128)(2,1)S(1)} %shard_map.119.refs_3_), channel_id=1, source_target_pairs={{0,64},{64,128},{128,192},{192,0},{1,65},{65,129},{129,193},{193,1... | collective-permute-start | bytes 1228808 | tf_op jit(solution)/shard_map/ppermute | solution.py:27
  51.9 9.8 %collective-permute-start.8 = (bf16[640,128]{1,0:T(8,128)(2,1)S(1)}, bf16[640,128]{1,0:T(8,128)(2,1)S(1)}, u32[]{:S(2)}, u32[]{:S(2)}) collective-permute-start(bf16[640,128]{1,0:T(8,128)(2,1)S(1)} %get-tuple-element.45), channel_id=1, source_target_pairs={{0,8},{8,0},{16,24},{24,16},{32,40},{40,32},{48,56},{56,48},{1,9},... | collective-permute-start | bytes 491528 | tf_op jit(solution)/shard_map/ppermute | solution.py:23
  53.1 8.6 %collective-permute-start.5 = (bf16[368,128]{1,0:T(8,128)(2,1)S(1)}, bf16[368,128]{1,0:T(8,128)(2,1)S(1)}, u32[]{:S(2)}, u32[]{:S(2)}) collective-permute-start(bf16[368,128]{1,0:T(8,128)(2,1)S(1)} %get-tuple-element.43), channel_id=1, source_target_pairs={{0,64},{64,0},{128,192},{192,128},{1,65},{65,1},{129,193},{193,129... | collective-permute-start | bytes 282632 | tf_op jit(solution)/shard_map/ppermute | solution.py:23
  61.7 8.8 %collective-permute-start.29 = (bf16[320,640]{1,0:T(8,128)(2,1)S(1)}, bf16[320,640]{1,0:T(8,128)(2,1)S(1)}, u32[]{:S(2)}, u32[]{:S(2)}) collective-permute-start(bf16[320,640]{1,0:T(8,128)(2,1)S(1)} %collective-permute-done.21.refs_4_), channel_id=1, source_target_pairs={{0,4},{4,0},{1,5},{5,1},{2,6},{6,2},{3,7},{7,3},{8,12},{12,8},{9,1... | collective-permute-start | bytes 1228808 | tf_op jit(solution)/shard_map/ppermute | solution.py:23
  61.7 11.9 %collective-permute-start.23 = (bf16[320,640]{1,0:T(8,128)(2,1)S(1)}, bf16[320,640]{1,0:T(8,128)(2,1)S(1)}, u32[]{:S(2)}, u32[]{:S(2)}) collective-permute-start(bf16[320,640]{1,0:T(8,128)(2,1)S(1)} %collective-permute-done.15.refs_0_), channel_id=1, source_target_pairs={{0,64},{64,128},{128,192},{192,0},{1,65},{65,129},{129,193},{193,1... | collective-permute-start | bytes 1228808 | tf_op jit(solution)/shard_map/ppermute | solution.py:27
  62.5 12.8 %collective-permute-start.24 = (bf16[320,640]{1,0:T(8,128)(2,1)S(1)}, bf16[320,640]{1,0:T(8,128)(2,1)S(1)}, u32[]{:S(2)}, u32[]{:S(2)}) collective-permute-start(bf16[320,640]{1,0:T(8,128)(2,1)S(1)} %collective-permute-done.22.refs_5_), channel_id=1, source_target_pairs={{0,192},{64,0},{128,64},{192,128},{1,193},{65,1},{129,65},{193,129... | collective-permute-start | bytes 1228808 | tf_op jit(solution)/shard_map/ppermute | solution.py:27
  64.3 6.1 %collective-permute-start.9 = (bf16[640,128]{1,0:T(8,128)(2,1)S(1)}, bf16[640,128]{1,0:T(8,128)(2,1)S(1)}, u32[]{:S(2)}, u32[]{:S(2)}) collective-permute-start(bf16[640,128]{1,0:T(8,128)(2,1)S(1)} %get-tuple-element.48.late), channel_id=1, source_target_pairs={{0,8},{8,0},{16,24},{24,16},{32,40},{40,32},{48,56},{56,48},{1,9},... | collective-permute-start | bytes 491528 | tf_op jit(solution)/shard_map/ppermute | solution.py:23
  65.2 14.0 %collective-permute-start.25 = (bf16[320,640]{1,0:T(8,128)(2,1)S(1)}, bf16[320,640]{1,0:T(8,128)(2,1)S(1)}, u32[]{:S(2)}, u32[]{:S(2)}) collective-permute-start(bf16[320,640]{1,0:T(8,128)(2,1)S(1)} %collective-permute-done.15.refs_0_), channel_id=1, source_target_pairs={{0,4},{4,0},{1,5},{5,1},{2,6},{6,2},{3,7},{7,3},{8,12},{12,8},{9,1... | collective-permute-start | bytes 1228808 | tf_op jit(solution)/shard_map/ppermute | solution.py:23
  70.5 10.4 %collective-permute-start.30 = (bf16[320,640]{1,0:T(8,128)(2,1)S(1)}, bf16[320,640]{1,0:T(8,128)(2,1)S(1)}, u32[]{:S(2)}, u32[]{:S(2)}) collective-permute-start(bf16[320,640]{1,0:T(8,128)(2,1)S(1)} %collective-permute-done.22.refs_5_), channel_id=1, source_target_pairs={{0,4},{4,0},{1,5},{5,1},{2,6},{6,2},{3,7},{7,3},{8,12},{12,8},{9,1... | collective-permute-start | bytes 1228808 | tf_op jit(solution)/shard_map/ppermute | solution.py:23
  70.5 10.4 %collective-permute-start.26 = (bf16[320,640]{1,0:T(8,128)(2,1)S(1)}, bf16[320,640]{1,0:T(8,128)(2,1)S(1)}, u32[]{:S(2)}, u32[]{:S(2)}) collective-permute-start(bf16[320,640]{1,0:T(8,128)(2,1)S(1)} %collective-permute-done.20.refs_1_), channel_id=1, source_target_pairs={{0,4},{4,0},{1,5},{5,1},{2,6},{6,2},{3,7},{7,3},{8,12},{12,8},{9,1... | collective-permute-start | bytes 1228808 | tf_op jit(solution)/shard_map/ppermute | solution.py:23
  73.6 7.3 %collective-permute-start.31 = (bf16[320,640]{1,0:T(8,128)(2,1)S(1)}, bf16[320,640]{1,0:T(8,128)(2,1)S(1)}, u32[]{:S(2)}, u32[]{:S(2)}) collective-permute-start(bf16[320,640]{1,0:T(8,128)(2,1)S(1)} %collective-permute-done.23.refs_6_), channel_id=1, source_target_pairs={{0,4},{4,0},{1,5},{5,1},{2,6},{6,2},{3,7},{7,3},{8,12},{12,8},{9,1... | collective-permute-start | bytes 1228808 | tf_op jit(solution)/shard_map/ppermute | solution.py:23
  75.3 5.6 %collective-permute-start.32 = (bf16[320,640]{1,0:T(8,128)(2,1)S(1)}, bf16[320,640]{1,0:T(8,128)(2,1)S(1)}, u32[]{:S(2)}, u32[]{:S(2)}) collective-permute-start(bf16[320,640]{1,0:T(8,128)(2,1)S(1)} %collective-permute-done.24.refs_7_), channel_id=1, source_target_pairs={{0,4},{4,0},{1,5},{5,1},{2,6},{6,2},{3,7},{7,3},{8,12},{12,8},{9,1... | collective-permute-start | bytes 1228808 | tf_op jit(solution)/shard_map/ppermute | solution.py:23
  84.6 8.0 %collective-permute-start.33 = (bf16[32,2688]{1,0:T(8,128)(2,1)S(1)}, bf16[32,2688]{1,0:T(8,128)(2,1)S(1)}, u32[]{:S(2)}, u32[]{:S(2)}) collective-permute-start(bf16[32,2688]{1,0:T(8,128)(2,1)S(1)} %get-tuple-element.54), channel_id=1, source_target_pairs={{0,1},{1,2},{2,3},{3,0},{4,5},{5,6},{6,7},{7,4},{8,9},{9,10},{10,1... | collective-permute-start | bytes 516104 | tf_op jit(solution)/shard_map/ppermute | solution.py:27
  86.3 11.2 %collective-permute-start.34 = (bf16[32,2688]{1,0:T(8,128)(2,1)S(1)}, bf16[32,2688]{1,0:T(8,128)(2,1)S(1)}, u32[]{:S(2)}, u32[]{:S(2)}) collective-permute-start(bf16[32,2688]{1,0:T(8,128)(2,1)S(1)} %get-tuple-element.55), channel_id=1, source_target_pairs={{0,2},{1,3},{2,0},{3,1},{4,6},{5,7},{6,4},{7,5},{8,10},{9,11},{10,... | collective-permute-start | bytes 516104 | tf_op jit(solution)/shard_map/ppermute | solution.py:27
  89.2 8.3 %collective-permute-start.35 = (bf16[32,2688]{1,0:T(8,128)(2,1)S(1)}, bf16[32,2688]{1,0:T(8,128)(2,1)S(1)}, u32[]{:S(2)}, u32[]{:S(2)}) collective-permute-start(bf16[32,2688]{1,0:T(8,128)(2,1)S(1)} %get-tuple-element.56), channel_id=1, source_target_pairs={{0,3},{1,0},{2,1},{3,2},{4,7},{5,4},{6,5},{7,6},{8,11},{9,8},{10,9... | collective-permute-start | bytes 516104 | tf_op jit(solution)/shard_map/ppermute | solution.py:27
  (20 other events, 41.3 us)

commit v2 on v1

--- a/solution.py
+++ b/solution.py
@@ -56,11 +56,6 @@
     return jnp.where(lane < 64, first, second)
 
 
-def padded(value, width=LANE):
-    zeros = jnp.zeros((value.shape[0], width - value.shape[1]), value.dtype)
-    return jnp.concatenate([value, zeros], axis=1)
-
-
 def put_totals(ref, at, size, totals):
     hi = totals.astype(BF)
     rest = totals - hi.astype(F32)
@@ -77,12 +72,13 @@
 
 
 def state_kernel(place, values, keys, log_decay, msg, cum_ref):
-    cum = padded(log_decay[...])
-    row, lane = rows(), lanes()
+    lane = lanes()
+    cum = jnp.concatenate([log_decay[...], jnp.zeros((4, TOK), F32)], axis=0)
     step = 1
     while step < TOK:
-        cum = cum + jnp.where(row >= step, pltpu.roll(cum, step, 0), 0.0)
+        cum = cum + jnp.where(lane[:24] >= step, pltpu.roll(cum, step, 1), 0.0)
         step *= 2
+    cum = jnp.concatenate([cum, jnp.zeros((TOK - 24, TOK), F32)], axis=0).T
     cum_ref[...] = cum
     total = cum[TOK - 1 : TOK, :]
     factor = jnp.exp(total - cum)
@@ -184,15 +180,21 @@
     picks = lax.broadcasted_iota(I32, (64, TOK), 0)
     onehot = (picks == lam_index[...]).astype(F32).astype(BF)
 
-    def level(number):
-        table = padded(lam_table[:, number, :])
+    tables = []
+    for first in (0, 4):
+        table = [jnp.concatenate([lam_table[:, first + i, :], jnp.zeros((12, 64), F32)], axis=0) for i in range(4)]
+        table = jnp.concatenate(table, axis=0)
         hi = table.astype(BF)
         rest = table - hi.astype(F32)
         mid = rest.astype(BF)
         low = (rest - mid.astype(F32)).astype(BF)
-        out = lax.dot_general(onehot, hi, TN, preferred_element_type=F32)
-        out = out + lax.dot_general(onehot, mid, TN, preferred_element_type=F32)
-        return out + lax.dot_general(onehot, low, TN, preferred_element_type=F32)
+        out = jnp.dot(hi, onehot, preferred_element_type=F32)
+        out = out + jnp.dot(mid, onehot, preferred_element_type=F32)
+        out = out + jnp.dot(low, onehot, preferred_element_type=F32)
+        tables.append(out.T)
+
+    def level(number):
+        return pltpu.roll(tables[number // 4], (LANE - 32 * (number % 4)) % LANE, 1)
 
     mine = jnp.zeros((TOK, LANE), F32)
     theirs = jnp.zeros((TOK, LANE), F32)
@@ -331,7 +333,7 @@
         v = gate[:, cols].astype(F32)
         gated = gated * (v / (1.0 + jnp.exp(-v)))
         squares = squares + gated * gated
-        y_ref[:, cols] = (gated * gain[:, cols]).astype(BF)
+        y_ref[:, cols] = (gated * gain[p : p + 1, :]).astype(BF)
     squares = jnp.sum(squares, axis=1, keepdims=True)
     hi = squares.astype(BF).astype(F32)
     mid = (squares - hi).astype(BF).astype(F32)
@@ -345,7 +347,7 @@
     def store(d, cols, value):
         for owner in range(NY):
 
-            @pl.when(lax.rem(y + d, NY) == owner)
+            @pl.when((y ^ d) == owner)
             def _():
                 out_refs[d][:, cols] = value[owner * part : (owner + 1) * part]
 
@@ -375,7 +377,7 @@
     for block in range(4):
         part = total(slice(block * HALF, (block + 1) * HALF)) * inv
         part = pltpu.roll(part, amount, 1)
-        at = pl.multiple_of(lax.rem(x + (NX - 1 + block), NX) * HALF, HALF)
+        at = pl.multiple_of((x ^ block) * HALF, HALF)
         out_ref[:, pl.ds(at, HALF)] = part.astype(BF)
 
 
@@ -397,14 +399,14 @@
     above4 = shift(above3, "z", -1, NZ)
     near = joined(below2, below1, mine, above1)
     far = joined(above2, above3, above4, below3)
-    near_left = shift(near, "x", 1, NX)
-    near_right = shift(near, "x", -1, NX)
-    far_left = shift(far, "x", 1, NX)
-    far_right = shift(far, "x", -1, NX)
-    near_across = shift(near_left, "x", 1, NX)
-    far_across = shift(far_right, "x", -1, NX)
-    own = [near_left, far_left, near, far, near_right, far_right, near_across, far_across]
-    order = (2, 3, 0, 4, 6, 1, 5, 7)
+    near_1 = flip(near, "x", 1, NX)
+    near_3 = flip(near, "x", 3, NX)
+    far_1 = flip(far, "x", 1, NX)
+    far_3 = flip(far, "x", 3, NX)
+    near_2 = flip(near_3, "x", 1, NX)
+    far_2 = flip(far_1, "x", 3, NX)
+    own = [near, far, near_1, far_1, near_2, far_2, near_3, far_3]
+    order = (0, 1, 2, 6, 4, 3, 7, 5)
     others = [None] * 8
     for at in order:
         others[at] = flip(own[at], "core", 1, 2)
@@ -427,7 +429,7 @@
     place = jnp.stack(places).astype(I32)
     own_w, other_w = gather_weights(out_proj)
     state, cum = call(
-        state_kernel, place, (values, key_rows, log_decay),
+        state_kernel, place, (values, key_rows, log_decay.T),
         [shaped(COLS + 96, NST), shaped(TOK, LANE, dtype=F32)],
         vmem=6,
     )
@@ -439,7 +441,7 @@
     msg2, p2 = call(chip_kernel, place, (msg1, got1), [quart, line])
     got2 = flip(msg2, "z", 2, NZ)
     msg3, p3 = call(lambda *r: merge_kernel(2, *r), place, (msg2, got2, p2), [quart, line])
-    got3 = flip(msg3, "z", 4, NZ)
+    got3 = flip(msg3, "z", 6, NZ)
     msg4, p4, side = call(
         lambda *r: merge_side_kernel(4, *r), place, (msg3, got3, p3, got2), [quart, line, shaped(HALF, NST)]
     )
@@ -452,7 +454,7 @@
         local_kernel, place,
         (
             queries, key_rows, values, cum, lam_index.reshape(1, TOK), segments.reshape(1, TOK),
-            lam_table, skip_gain.reshape(1, HEADS), got0,
+            lam_table.transpose(2, 1, 0), skip_gain.reshape(1, HEADS), got0,
         ),
         [shaped(TOK, COLS, dtype=F32), shaped(TOK, LANE, dtype=F32), shaped(3 * TOK, LANE)],
         flops=3 * 10**8,
@@ -478,15 +480,15 @@
     back = flip(back, "core", 1, 2)
     parts = call(
         project_kernel, place,
-        (base, own_cross, back, gate_rows, norm_gain.reshape(1, COLS), *own_w, *other_w),
+        (base, own_cross, back, gate_rows, norm_gain.reshape(10, LANE), *own_w, *other_w),
         [shaped(TOK // NY, 2688)] * NY,
         scratch=[pltpu.VMEM((TOK, COLS), BF)],
         flops=10**9,
         vmem=24,
     )
     arrived = [parts[0]]
-    for d in range(1, NY):
-        arrived.append(shift(parts[d], "y", d, NY))
+    for d in (2, 1, 3):
+        arrived.append(flip(parts[d], "y", d, NY))
     return call(finish_kernel, place, arrived, [shaped(TOK // NY, 2560)])[0]
 
 

time: 101 us -> 92.9 us (0.920)
  starting transfers between devices: 35 us -> 30.6 us
  local copies, waits for them, and re-layouts: 6.22 us -> 3.04 us
    ppermute x16 -> x7, starting transfers between devices: 26.3 us -> 14.2 us  [shift(): lax.ppermute(value, axis, [(i, (i + step) % size) for i in range(size)])]
    ppermute x20 -> x29, waiting for transfers between devices: 21.3 us -> 31.9 us  [flip(): return lax.ppermute(value, axis, [(i, i ^ mask) for i in range(size)])]
    ppermute x16 -> x7, waiting for transfers between devices: 17.3 us -> 7.36 us  [shift(): lax.ppermute(value, axis, [(i, (i + step) % size) for i in range(size)])]
    ppermute x20 -> x29, starting transfers between devices: 8.66 us -> 16.4 us  [flip(): return lax.ppermute(value, axis, [(i, i ^ mask) for i in range(size)])]
    unnamed x34 -> x24, local copies, waits for them, and re-layouts: 6.21 us -> 3.04 us
  transfers between devices with their start and end apart: 36 -> 36, of which waited for: 15 -> 15; matrix products, arithmetic and copies ran while one was open for 1% -> 0% of each run, Pallas kernels for 14% -> 14%
where the time goes in v2:
time: 92.9 us; the launch traced here: 91.4 us
  waiting for transfers between devices  39.2 us (42%)
  starting transfers between devices  30.6 us (33%)
  Pallas kernels  18.1 us (19%)
  local copies, waits for them, and re-layouts  3.04 us (3%)
    ppermute x29, waiting for transfers between devices, flip(): return lax.ppermute(value, axis, [(i, i ^ mask) for i in range(size)])  31.9 us
    pallas_call x13, Pallas kernels, call(): pl.pallas_call(body, out_shape=outs, in_specs=[pl.BlockSpec(memory_space=...  18.1 us
    ppermute x29, starting transfers between devices, flip(): return lax.ppermute(value, axis, [(i, i ^ mask) for i in range(size)])  16.4 us
    ppermute x7, starting transfers between devices, shift(): lax.ppermute(value, axis, [(i, (i + step) % size) for i in range(size)])  14.2 us
    ppermute x7, waiting for transfers between devices, shift(): lax.ppermute(value, axis, [(i, (i + step) % size) for i in range(size)])  7.36 us
    unnamed x24, local copies, waits for them, and re-layouts  3.04 us
  transfers between devices with their start and end apart: 36, of which 15 were waited for; matrix products, arithmetic and copies ran while one was open for 0% of the time, Pallas kernels for 14%

profile of v2, /device:TPU:6, one launch (start us, length us, event | category | flops | bytes accessed | tf_op | source)
XLA Modules:
  0.0 91.4 jit_solution(11956629093425524628)
XLA Ops:
  0.8 1.0 %copy-done.1 = bf16[128,1280]{1,0:T(8,128)(2,1)S(1)} copy-done((bf16[128,1280]{1,0:T(8,128)(2,1)S(1)}, bf16[128,1280]{1,0:T(8,128)(2,1)}, u32[]{:S(2)}) %copy-start.1) | copy-done | bytes 327704
  1.7 0.7 copy-done.5
  2.4 1.9 %shard_map.109 = (bf16[1376,128]{1,0:T(8,128)(2,1)S(1)}, f32[128,128]{1,0:T(8,128)S(1)}) custom-call(s32[4]{0:T(128)S(1)} %pad_add_fusion.place.r_0_, bf16[128,1280]{1,0:T(8,128)(2,1)S(1)} %copy-done.1, bf16[128,128]{1,0:T(8,128)(2,1)S(1)} %copy-done.4, f32[20,128]{1,0:T(8,128)S(1)} %bitcast.13), custom_call_target="tpu_custom_call" | custom-call | flops 100000000 | bytes 1048576 | tf_op jit(solution)/shard_map/pallas_call | solution.py:31
  4.5 5.9 %collective-permute-start.14 = (bf16[80,640]{1,0:T(8,128)(2,1)S(1)}, bf16[80,640]{1,0:T(8,128)(2,1)S(1)}, u32[]{:S(2)}, u32[]{:S(2)}) collective-permute-start(bf16[80,640]{1,0:T(8,128)(2,1)S(1)} %fusion.c), channel_id=1, source_target_pairs={{0,56},{8,0},{16,8},{24,16},{32,24},{40,32},{48,40},{56,48},{1,57}... | collective-permute-start | bytes 307208 | tf_op jit(solution)/shard_map/ppermute | solution.py:27
  11.2 2.0 %collective-permute-done.14.d = bf16[80,640]{1,0:T(8,128)(2,1)S(1)} collective-permute-done((bf16[80,640]{1,0:T(8,128)(2,1)S(1)}, bf16[80,640]{1,0:T(8,128)(2,1)S(1)}, u32[]{:S(2)}, u32[]{:S(2)}) %collective-permute-start.14) | collective-permute-done | bytes 102432 | tf_op jit(solution)/shard_map/ppermute | solution.py:27
  13.2 3.7 %collective-permute-start.15 = (bf16[80,640]{1,0:T(8,128)(2,1)S(1)}, bf16[80,640]{1,0:T(8,128)(2,1)S(1)}, u32[]{:S(2)}, u32[]{:S(2)}) collective-permute-start(bf16[80,640]{1,0:T(8,128)(2,1)S(1)} %collective-permute-done.14.d), channel_id=1, source_target_pairs={{0,56},{8,0},{16,8},{24,16},{32,24},{40,32},{48,40},{56,48},{1,57}... | collective-permute-start | bytes 307208 | tf_op jit(solution)/shard_map/ppermute | solution.py:27
  16.9 3.0 %collective-permute-done.15.a = bf16[80,640]{1,0:T(8,128)(2,1)S(1)} collective-permute-done((bf16[80,640]{1,0:T(8,128)(2,1)S(1)}, bf16[80,640]{1,0:T(8,128)(2,1)S(1)}, u32[]{:S(2)}, u32[]{:S(2)}) %collective-permute-start.15) | collective-permute-done | bytes 102432 | tf_op jit(solution)/shard_map/ppermute | solution.py:27
  19.9 2.9 %collective-permute-start.16 = (bf16[80,640]{1,0:T(8,128)(2,1)S(1)}, bf16[80,640]{1,0:T(8,128)(2,1)S(1)}, u32[]{:S(2)}, u32[]{:S(2)}) collective-permute-start(bf16[80,640]{1,0:T(8,128)(2,1)S(1)} %collective-permute-done.15.a), channel_id=1, source_target_pairs={{0,56},{8,0},{16,8},{24,16},{32,24},{40,32},{48,40},{56,48},{1,57}... | collective-permute-start | bytes 307208 | tf_op jit(solution)/shard_map/ppermute | solution.py:27
  24.2 0.9 collective-permute-start.19
  25.1 3.8 %collective-permute-done.3.r_2_.r_4_.got2 = bf16[368,128]{1,0:T(8,128)(2,1)S(1)} collective-permute-done((bf16[368,128]{1,0:T(8,128)(2,1)S(1)}, bf16[368,128]{1,0:T(8,128)(2,1)S(1)}, u32[]{:S(2)}, u32[]{:S(2)}) %collective-permute-start.3) | collective-permute-done | bytes 94240 | tf_op jit(solution)/shard_map/ppermute | solution.py:23
  28.9 1.7 %collective-permute-start.17 = (bf16[80,640]{1,0:T(8,128)(2,1)S(1)}, bf16[80,640]{1,0:T(8,128)(2,1)S(1)}, u32[]{:S(2)}, u32[]{:S(2)}) collective-permute-start(bf16[80,640]{1,0:T(8,128)(2,1)S(1)} %collective-permute-done.16.b), channel_id=1, source_target_pairs={{0,56},{8,0},{16,8},{24,16},{32,24},{40,32},{48,40},{56,48},{1,57}... | collective-permute-start | bytes 307208 | tf_op jit(solution)/shard_map/ppermute | solution.py:27
  31.3 1.1 %collective-permute-start.4 = (bf16[368,128]{1,0:T(8,128)(2,1)S(1)}, bf16[368,128]{1,0:T(8,128)(2,1)S(1)}, u32[]{:S(2)}, u32[]{:S(2)}) collective-permute-start(bf16[368,128]{1,0:T(8,128)(2,1)S(1)} %get-tuple-element.41.r_1_), channel_id=1, source_target_pairs={{0,48},{8,56},{16,32},{24,40},{32,16},{40,24},{48,0},{56,8},{1,49}... | collective-permute-start | bytes 282632 | tf_op jit(solution)/shard_map/ppermute | solution.py:23
  32.4 2.2 %collective-permute-done.17.c = bf16[80,640]{1,0:T(8,128)(2,1)S(1)} collective-permute-done((bf16[80,640]{1,0:T(8,128)(2,1)S(1)}, bf16[80,640]{1,0:T(8,128)(2,1)S(1)}, u32[]{:S(2)}, u32[]{:S(2)}) %collective-permute-start.17) | collective-permute-done | bytes 102432 | tf_op jit(solution)/shard_map/ppermute | solution.py:27
  34.7 0.8 collective-permute-start.20
  36.1 4.4 %shard_map.110 = (f32[128,1280]{1,0:T(8,128)S(1)}, f32[128,128]{1,0:T(8,128)S(1)}, bf16[384,128]{1,0:T(8,128)(2,1)S(1)}) custom-call(s32[4]{0:T(128)S(1)} %pad_add_fusion.place.r_0_, bf16[128,128]{1,0:T(8,128)(2,1)S(1)} %copy-done.3, bf16[128,128]{1,0:T(8,128)(2,1)S(1)} %copy-done.4, bf16[128,1280]{1,0:T(8,128)(2,1)S(1)} %copy-done.2, ...), custom_call_target="tpu_custom_call" | custom-call | flops 300000000 | bytes 1048576 | tf_op jit(solution)/shard_map/pallas_call | solution.py:31
  42.6 2.9 %collective-permute-start.6 = (bf16[368,128]{1,0:T(8,128)(2,1)S(1)}, bf16[368,128]{1,0:T(8,128)(2,1)S(1)}, u32[]{:S(2)}, u32[]{:S(2)}) collective-permute-start(bf16[368,128]{1,0:T(8,128)(2,1)S(1)} %get-tuple-element.43), channel_id=1, source_target_pairs={{0,128},{64,192},{128,0},{192,64},{1,129},{65,193},{129,1},{193,65... | collective-permute-start | bytes 282632 | tf_op jit(solution)/shard_map/ppermute | solution.py:23
  46.2 3.8 %collective-permute-done.7.r3 = bf16[368,128]{1,0:T(8,128)(2,1)S(1)} collective-permute-done((bf16[368,128]{1,0:T(8,128)(2,1)S(1)}, bf16[368,128]{1,0:T(8,128)(2,1)S(1)}, u32[]{:S(2)}, u32[]{:S(2)}) %collective-permute-start.7) | collective-permute-done | bytes 94240 | tf_op jit(solution)/shard_map/ppermute | solution.py:23
  50.0 0.8 collective-permute-start.8
  50.8 4.6 %collective-permute-done.5.r1 = bf16[368,128]{1,0:T(8,128)(2,1)S(1)} collective-permute-done((bf16[368,128]{1,0:T(8,128)(2,1)S(1)}, bf16[368,128]{1,0:T(8,128)(2,1)S(1)}, u32[]{:S(2)}, u32[]{:S(2)}) %collective-permute-start.5) | collective-permute-done | bytes 94240 | tf_op jit(solution)/shard_map/ppermute | solution.py:23
  56.0 0.8 collective-permute-start.23
  57.4 0.7 collective-permute-start.9
  58.7 5.1 %collective-permute-done.9.late_side = bf16[640,128]{1,0:T(8,128)(2,1)S(1)} collective-permute-done((bf16[640,128]{1,0:T(8,128)(2,1)S(1)}, bf16[640,128]{1,0:T(8,128)(2,1)S(1)}, u32[]{:S(2)}, u32[]{:S(2)}) %collective-permute-start.9) | collective-permute-done | bytes 163872 | tf_op jit(solution)/shard_map/ppermute | solution.py:23
  64.3 3.0 %collective-permute-done.22.refs_4_ = bf16[320,640]{1,0:T(8,128)(2,1)S(1)} collective-permute-done((bf16[320,640]{1,0:T(8,128)(2,1)S(1)}, bf16[320,640]{1,0:T(8,128)(2,1)S(1)}, u32[]{:S(2)}, u32[]{:S(2)}) %collective-permute-start.22) | collective-permute-done | bytes 409632 | tf_op jit(solution)/shard_map/ppermute | solution.py:23
  67.3 1.3 %collective-permute-done.23.refs_5_ = bf16[320,640]{1,0:T(8,128)(2,1)S(1)} collective-permute-done((bf16[320,640]{1,0:T(8,128)(2,1)S(1)}, bf16[320,640]{1,0:T(8,128)(2,1)S(1)}, u32[]{:S(2)}, u32[]{:S(2)}) %collective-permute-start.23) | collective-permute-done | bytes 409632 | tf_op jit(solution)/shard_map/ppermute | solution.py:23
  68.6 2.0 %shard_map.116 = (f32[128,640]{1,0:T(8,128)S(1)}, f32[128,640]{1,0:T(8,128)S(1)}, f32[128,128]{1,0:T(8,128)S(1)}, f32[128,128]{1,0:T(8,128)S(1)}) custom-call(s32[4]{0:T(128)S(1)} %pad_add_fusion.place.r_0_, bf16[128,128]{1,0:T(8,128)(2,1)S(1)} %copy-done.3, f32[128,128]{1,0:T(8,128)S(1)} %get-tuple-element.35.factors, ...), custom_call_target="tpu_custom_call" | custom-call | flops 100000000 | bytes 1048576 | tf_op jit(solution)/shard_map/pallas_call | solution.py:31
  70.6 1.5 %shard_map.117 = (f32[128,640]{1,0:T(8,128)S(1)}, bf16[128,640]{1,0:T(8,128)(2,1)S(1)}) custom-call(s32[4]{0:T(128)S(1)} %pad_add_fusion.place.r_0_, bf16[128,128]{1,0:T(8,128)(2,1)S(1)} %copy-done.3, bf16[384,128]{1,0:T(8,128)(2,1)S(1)} %collective-permute-done.1.mail, f32[128,128]{1,0:T(8,128)S(1)} %get-tuple-element.46.own_w, ...), custom_call_target="tpu_custom_call" | custom-call | flops 100000000 | bytes 1048576 | tf_op jit(solution)/shard_map/pallas_call | solution.py:31
  72.8 1.0 %collective-permute-done.10.back = bf16[128,640]{1,0:T(8,128)(2,1)S(1)} collective-permute-done((bf16[128,640]{1,0:T(8,128)(2,1)S(1)}, bf16[128,640]{1,0:T(8,128)(2,1)S(1)}, u32[]{:S(2)}, u32[]{:S(2)}) %collective-permute-start.10) | collective-permute-done | bytes 163872 | tf_op jit(solution)/shard_map/ppermute | solution.py:23
  73.8 3.7 %shard_map.120 = (bf16[32,2688]{1,0:T(8,128)(2,1)S(1)}, bf16[32,2688]{1,0:T(8,128)(2,1)S(1)}, bf16[32,2688]{1,0:T(8,128)(2,1)S(1)}, bf16[32,2688]{1,0:T(8,128)(2,1)S(1)}) custom-call(s32[4]{0:T(128)S(1)} %pad_add_fusion.place.r_0_, f32[128,1280]{1,0:T(8,128)S(1)} %get-tuple-element.33.base, f32[128,640]{1,0:T(8,128)S(1)} %get-tuple-element.51.own, ...), custom_call_target="tpu_custom_call" | custom-call | flops 1000000000 | bytes 1048576 | tf_op jit(solution)/shard_map/pallas_call | solution.py:31
  77.6 3.3 %collective-permute-start.33 = (bf16[32,2688]{1,0:T(8,128)(2,1)S(1)}, bf16[32,2688]{1,0:T(8,128)(2,1)S(1)}, u32[]{:S(2)}, u32[]{:S(2)}) collective-permute-start(bf16[32,2688]{1,0:T(8,128)(2,1)S(1)} %get-tuple-element.54), channel_id=1, source_target_pairs={{0,2},{1,3},{2,0},{3,1},{4,6},{5,7},{6,4},{7,5},{8,10},{9,11},{10,... | collective-permute-start | bytes 516104 | tf_op jit(solution)/shard_map/ppermute | solution.py:23
  81.9 4.5 %collective-permute-done.33.b_ref = bf16[32,2688]{1,0:T(8,128)(2,1)S(1)} collective-permute-done((bf16[32,2688]{1,0:T(8,128)(2,1)S(1)}, bf16[32,2688]{1,0:T(8,128)(2,1)S(1)}, u32[]{:S(2)}, u32[]{:S(2)}) %collective-permute-start.33) | collective-permute-done | bytes 172064 | tf_op jit(solution)/shard_map/ppermute | solution.py:23
  86.4 3.5 %collective-permute-done.34.c_ref = bf16[32,2688]{1,0:T(8,128)(2,1)S(1)} collective-permute-done((bf16[32,2688]{1,0:T(8,128)(2,1)S(1)}, bf16[32,2688]{1,0:T(8,128)(2,1)S(1)}, u32[]{:S(2)}, u32[]{:S(2)}) %collective-permute-start.34) | collective-permute-done | bytes 172064 | tf_op jit(solution)/shard_map/ppermute | solution.py:23
  89.9 1.5 %shard_map.121 = bf16[32,2560]{1,0:T(8,128)(2,1)} custom-call(s32[4]{0:T(128)S(1)} %pad_add_fusion.place.r_0_, bf16[32,2688]{1,0:T(8,128)(2,1)S(1)} %get-tuple-element.53.a_ref, bf16[32,2688]{1,0:T(8,128)(2,1)S(1)} %collective-permute-done.33.b_ref, bf16[32,2688]{1,0:T(8,128)(2,1)S(1)} %collective-permute-done.34.c_ref, ...), custom_call_target="tpu_custom_call" | custom-call | flops 100000000 | bytes 1048576 | tf_op jit(solution)/shard_map/pallas_call | solution.py:31
  (80 shorter events, 11.2 us)
Async XLA Ops:
  4.3 6.1 %collective-permute-start = (bf16[1376,128]{1,0:T(8,128)(2,1)S(1)}, bf16[1376,128]{1,0:T(8,128)(2,1)S(1)}, u32[]{:S(2)}, u32[]{:S(2)}) collective-permute-start(bf16[1376,128]{1,0:T(8,128)(2,1)S(1)} %get-tuple-element.32.own), channel_id=1, source_target_pairs={{0,4},{4,0},{1,5},{5,1},{2,6},{6,2},{3,7},{7,3},{8,12},{12,8},{9,1... | collective-permute-start | bytes 1056776 | tf_op jit(solution)/shard_map/ppermute | solution.py:23
  4.5 8.7 %collective-permute-start.14 = (bf16[80,640]{1,0:T(8,128)(2,1)S(1)}, bf16[80,640]{1,0:T(8,128)(2,1)S(1)}, u32[]{:S(2)}, u32[]{:S(2)}) collective-permute-start(bf16[80,640]{1,0:T(8,128)(2,1)S(1)} %fusion.c), channel_id=1, source_target_pairs={{0,56},{8,0},{16,8},{24,16},{32,24},{40,32},{48,40},{56,48},{1,57}... | collective-permute-start | bytes 307208 | tf_op jit(solution)/shard_map/ppermute | solution.py:27
  10.4 6.5 %collective-permute-start.12 = (bf16[80,640]{1,0:T(8,128)(2,1)S(1)}, bf16[80,640]{1,0:T(8,128)(2,1)S(1)}, u32[]{:S(2)}, u32[]{:S(2)}) collective-permute-start(bf16[80,640]{1,0:T(8,128)(2,1)S(1)} %fusion.c), channel_id=1, source_target_pairs={{0,8},{8,16},{16,24},{24,32},{32,40},{40,48},{48,56},{56,0},{1,9},... | collective-permute-start | bytes 307208 | tf_op jit(solution)/shard_map/ppermute | solution.py:27
  11.1 11.7 %collective-permute-start.2 = (bf16[688,128]{1,0:T(8,128)(2,1)S(1)}, bf16[688,128]{1,0:T(8,128)(2,1)S(1)}, u32[]{:S(2)}, u32[]{:S(2)}) collective-permute-start(bf16[688,128]{1,0:T(8,128)(2,1)S(1)} %get-tuple-element.37.own), channel_id=1, source_target_pairs={{0,8},{8,0},{16,24},{24,16},{32,40},{40,32},{48,56},{56,48},{1,9},... | collective-permute-start | bytes 528392 | tf_op jit(solution)/shard_map/ppermute | solution.py:23
  13.2 6.7 %collective-permute-start.15 = (bf16[80,640]{1,0:T(8,128)(2,1)S(1)}, bf16[80,640]{1,0:T(8,128)(2,1)S(1)}, u32[]{:S(2)}, u32[]{:S(2)}) collective-permute-start(bf16[80,640]{1,0:T(8,128)(2,1)S(1)} %collective-permute-done.14.d), channel_id=1, source_target_pairs={{0,56},{8,0},{16,8},{24,16},{32,24},{40,32},{48,40},{56,48},{1,57}... | collective-permute-start | bytes 307208 | tf_op jit(solution)/shard_map/ppermute | solution.py:27
  16.9 6.6 %collective-permute-start.13 = (bf16[80,640]{1,0:T(8,128)(2,1)S(1)}, bf16[80,640]{1,0:T(8,128)(2,1)S(1)}, u32[]{:S(2)}, u32[]{:S(2)}) collective-permute-start(bf16[80,640]{1,0:T(8,128)(2,1)S(1)} %collective-permute-done.12.b), channel_id=1, source_target_pairs={{0,8},{8,16},{16,24},{24,32},{32,40},{40,48},{48,56},{56,0},{1,9},... | collective-permute-start | bytes 307208 | tf_op jit(solution)/shard_map/ppermute | solution.py:27
  19.9 5.2 %collective-permute-start.16 = (bf16[80,640]{1,0:T(8,128)(2,1)S(1)}, bf16[80,640]{1,0:T(8,128)(2,1)S(1)}, u32[]{:S(2)}, u32[]{:S(2)}) collective-permute-start(bf16[80,640]{1,0:T(8,128)(2,1)S(1)} %collective-permute-done.15.a), channel_id=1, source_target_pairs={{0,56},{8,0},{16,8},{24,16},{32,24},{40,32},{48,40},{56,48},{1,57}... | collective-permute-start | bytes 307208 | tf_op jit(solution)/shard_map/ppermute | solution.py:27
  23.4 5.6 %collective-permute-start.3 = (bf16[368,128]{1,0:T(8,128)(2,1)S(1)}, bf16[368,128]{1,0:T(8,128)(2,1)S(1)}, u32[]{:S(2)}, u32[]{:S(2)}) collective-permute-start(bf16[368,128]{1,0:T(8,128)(2,1)S(1)} %get-tuple-element.39.r_1_), channel_id=1, source_target_pairs={{0,16},{8,24},{16,0},{24,8},{32,48},{40,56},{48,32},{56,40},{1,17}... | collective-permute-start | bytes 282632 | tf_op jit(solution)/shard_map/ppermute | solution.py:23
  23.5 19.1 %collective-permute-start.25 = (bf16[320,640]{1,0:T(8,128)(2,1)S(1)}, bf16[320,640]{1,0:T(8,128)(2,1)S(1)}, u32[]{:S(2)}, u32[]{:S(2)}) collective-permute-start(bf16[320,640]{1,0:T(8,128)(2,1)S(1)} %shard_map.118.refs_0_), channel_id=1, source_target_pairs={{0,4},{4,0},{1,5},{5,1},{2,6},{6,2},{3,7},{7,3},{8,12},{12,8},{9,1... | collective-permute-start | bytes 1228808 | tf_op jit(solution)/shard_map/ppermute | solution.py:23
  23.6 21.9 %collective-permute-start.21 = (bf16[320,640]{1,0:T(8,128)(2,1)S(1)}, bf16[320,640]{1,0:T(8,128)(2,1)S(1)}, u32[]{:S(2)}, u32[]{:S(2)}) collective-permute-start(bf16[320,640]{1,0:T(8,128)(2,1)S(1)} %shard_map.118.refs_0_), channel_id=1, source_target_pairs={{0,192},{64,128},{128,64},{192,0},{1,193},{65,129},{129,65},{193,1... | collective-permute-start | bytes 1228808 | tf_op jit(solution)/shard_map/ppermute | solution.py:23
  24.2 21.3 %collective-permute-start.19 = (bf16[320,640]{1,0:T(8,128)(2,1)S(1)}, bf16[320,640]{1,0:T(8,128)(2,1)S(1)}, u32[]{:S(2)}, u32[]{:S(2)}) collective-permute-start(bf16[320,640]{1,0:T(8,128)(2,1)S(1)} %shard_map.118.refs_0_), channel_id=1, source_target_pairs={{0,64},{64,0},{128,192},{192,128},{1,65},{65,1},{129,193},{193,129... | collective-permute-start | bytes 1228808 | tf_op jit(solution)/shard_map/ppermute | solution.py:23
  25.1 6.2 %collective-permute-start.18 = (bf16[80,640]{1,0:T(8,128)(2,1)S(1)}, bf16[80,640]{1,0:T(8,128)(2,1)S(1)}, u32[]{:S(2)}, u32[]{:S(2)}) collective-permute-start(bf16[80,640]{1,0:T(8,128)(2,1)S(1)} %collective-permute-done.13.a), channel_id=1, source_target_pairs={{0,8},{8,16},{16,24},{24,32},{32,40},{40,48},{48,56},{56,0},{1,9},... | collective-permute-start | bytes 307208 | tf_op jit(solution)/shard_map/ppermute | solution.py:27
  28.9 5.7 %collective-permute-start.17 = (bf16[80,640]{1,0:T(8,128)(2,1)S(1)}, bf16[80,640]{1,0:T(8,128)(2,1)S(1)}, u32[]{:S(2)}, u32[]{:S(2)}) collective-permute-start(bf16[80,640]{1,0:T(8,128)(2,1)S(1)} %collective-permute-done.16.b), channel_id=1, source_target_pairs={{0,56},{8,0},{16,8},{24,16},{32,24},{40,32},{48,40},{56,48},{1,57}... | collective-permute-start | bytes 307208 | tf_op jit(solution)/shard_map/ppermute | solution.py:27
  31.3 9.3 %collective-permute-start.4 = (bf16[368,128]{1,0:T(8,128)(2,1)S(1)}, bf16[368,128]{1,0:T(8,128)(2,1)S(1)}, u32[]{:S(2)}, u32[]{:S(2)}) collective-permute-start(bf16[368,128]{1,0:T(8,128)(2,1)S(1)} %get-tuple-element.41.r_1_), channel_id=1, source_target_pairs={{0,48},{8,56},{16,32},{24,40},{32,16},{40,24},{48,0},{56,8},{1,49}... | collective-permute-start | bytes 282632 | tf_op jit(solution)/shard_map/ppermute | solution.py:23
  34.7 21.3 %collective-permute-start.20 = (bf16[320,640]{1,0:T(8,128)(2,1)S(1)}, bf16[320,640]{1,0:T(8,128)(2,1)S(1)}, u32[]{:S(2)}, u32[]{:S(2)}) collective-permute-start(bf16[320,640]{1,0:T(8,128)(2,1)S(1)} %shard_map.119.refs_1_), channel_id=1, source_target_pairs={{0,64},{64,0},{128,192},{192,128},{1,65},{65,1},{129,193},{193,129... | collective-permute-start | bytes 1228808 | tf_op jit(solution)/shard_map/ppermute | solution.py:23
  41.9 8.1 %collective-permute-start.7 = (bf16[368,128]{1,0:T(8,128)(2,1)S(1)}, bf16[368,128]{1,0:T(8,128)(2,1)S(1)}, u32[]{:S(2)}, u32[]{:S(2)}) collective-permute-start(bf16[368,128]{1,0:T(8,128)(2,1)S(1)} %get-tuple-element.43), channel_id=1, source_target_pairs={{0,192},{64,128},{128,64},{192,0},{1,193},{65,129},{129,65},{193,1... | collective-permute-start | bytes 282632 | tf_op jit(solution)/shard_map/ppermute | solution.py:23
  42.6 8.2 %collective-permute-start.6 = (bf16[368,128]{1,0:T(8,128)(2,1)S(1)}, bf16[368,128]{1,0:T(8,128)(2,1)S(1)}, u32[]{:S(2)}, u32[]{:S(2)}) collective-permute-start(bf16[368,128]{1,0:T(8,128)(2,1)S(1)} %get-tuple-element.43), channel_id=1, source_target_pairs={{0,128},{64,192},{128,0},{192,64},{1,129},{65,193},{129,1},{193,65... | collective-permute-start | bytes 282632 | tf_op jit(solution)/shard_map/ppermute | solution.py:23
  45.5 11.8 %collective-permute-start.26 = (bf16[320,640]{1,0:T(8,128)(2,1)S(1)}, bf16[320,640]{1,0:T(8,128)(2,1)S(1)}, u32[]{:S(2)}, u32[]{:S(2)}) collective-permute-start(bf16[320,640]{1,0:T(8,128)(2,1)S(1)} %shard_map.119.refs_1_), channel_id=1, source_target_pairs={{0,4},{4,0},{1,5},{5,1},{2,6},{6,2},{3,7},{7,3},{8,12},{12,8},{9,1... | collective-permute-start | bytes 1228808 | tf_op jit(solution)/shard_map/ppermute | solution.py:23
  45.5 13.2 %collective-permute-start.24 = (bf16[320,640]{1,0:T(8,128)(2,1)S(1)}, bf16[320,640]{1,0:T(8,128)(2,1)S(1)}, u32[]{:S(2)}, u32[]{:S(2)}) collective-permute-start(bf16[320,640]{1,0:T(8,128)(2,1)S(1)} %shard_map.119.refs_1_), channel_id=1, source_target_pairs={{0,192},{64,128},{128,64},{192,0},{1,193},{65,129},{129,65},{193,1... | collective-permute-start | bytes 1228808 | tf_op jit(solution)/shard_map/ppermute | solution.py:23
  50.0 5.4 %collective-permute-start.8 = (bf16[640,128]{1,0:T(8,128)(2,1)S(1)}, bf16[640,128]{1,0:T(8,128)(2,1)S(1)}, u32[]{:S(2)}, u32[]{:S(2)}) collective-permute-start(bf16[640,128]{1,0:T(8,128)(2,1)S(1)} %get-tuple-element.45), channel_id=1, source_target_pairs={{0,8},{8,0},{16,24},{24,16},{32,40},{40,32},{48,56},{56,48},{1,9},... | collective-permute-start | bytes 491528 | tf_op jit(solution)/shard_map/ppermute | solution.py:23
  55.4 8.4 %collective-permute-start.31 = (bf16[320,640]{1,0:T(8,128)(2,1)S(1)}, bf16[320,640]{1,0:T(8,128)(2,1)S(1)}, u32[]{:S(2)}, u32[]{:S(2)}) collective-permute-start(bf16[320,640]{1,0:T(8,128)(2,1)S(1)} %collective-permute-done.21.refs_6_), channel_id=1, source_target_pairs={{0,4},{4,0},{1,5},{5,1},{2,6},{6,2},{3,7},{7,3},{8,12},{12,8},{9,1... | collective-permute-start | bytes 1228808 | tf_op jit(solution)/shard_map/ppermute | solution.py:23
  55.4 11.9 %collective-permute-start.22 = (bf16[320,640]{1,0:T(8,128)(2,1)S(1)}, bf16[320,640]{1,0:T(8,128)(2,1)S(1)}, u32[]{:S(2)}, u32[]{:S(2)}) collective-permute-start(bf16[320,640]{1,0:T(8,128)(2,1)S(1)} %collective-permute-done.21.refs_6_), channel_id=1, source_target_pairs={{0,64},{64,0},{128,192},{192,128},{1,65},{65,1},{129,193},{193,129... | collective-permute-start | bytes 1228808 | tf_op jit(solution)/shard_map/ppermute | solution.py:23
  56.0 12.6 %collective-permute-start.23 = (bf16[320,640]{1,0:T(8,128)(2,1)S(1)}, bf16[320,640]{1,0:T(8,128)(2,1)S(1)}, u32[]{:S(2)}, u32[]{:S(2)}) collective-permute-start(bf16[320,640]{1,0:T(8,128)(2,1)S(1)} %collective-permute-done.20.refs_3_), channel_id=1, source_target_pairs={{0,192},{64,128},{128,64},{192,0},{1,193},{65,129},{129,65},{193,1... | collective-permute-start | bytes 1228808 | tf_op jit(solution)/shard_map/ppermute | solution.py:23
  57.4 6.4 %collective-permute-start.9 = (bf16[640,128]{1,0:T(8,128)(2,1)S(1)}, bf16[640,128]{1,0:T(8,128)(2,1)S(1)}, u32[]{:S(2)}, u32[]{:S(2)}) collective-permute-start(bf16[640,128]{1,0:T(8,128)(2,1)S(1)} %get-tuple-element.48.late), channel_id=1, source_target_pairs={{0,8},{8,0},{16,24},{24,16},{32,40},{40,32},{48,56},{56,48},{1,9},... | collective-permute-start | bytes 491528 | tf_op jit(solution)/shard_map/ppermute | solution.py:23
  58.7 13.4 %collective-permute-start.27 = (bf16[320,640]{1,0:T(8,128)(2,1)S(1)}, bf16[320,640]{1,0:T(8,128)(2,1)S(1)}, u32[]{:S(2)}, u32[]{:S(2)}) collective-permute-start(bf16[320,640]{1,0:T(8,128)(2,1)S(1)} %collective-permute-done.19.refs_2_), channel_id=1, source_target_pairs={{0,4},{4,0},{1,5},{5,1},{2,6},{6,2},{3,7},{7,3},{8,12},{12,8},{9,1... | collective-permute-start | bytes 1228808 | tf_op jit(solution)/shard_map/ppermute | solution.py:23
  63.8 10.0 %collective-permute-start.28 = (bf16[320,640]{1,0:T(8,128)(2,1)S(1)}, bf16[320,640]{1,0:T(8,128)(2,1)S(1)}, u32[]{:S(2)}, u32[]{:S(2)}) collective-permute-start(bf16[320,640]{1,0:T(8,128)(2,1)S(1)} %collective-permute-done.20.refs_3_), channel_id=1, source_target_pairs={{0,4},{4,0},{1,5},{5,1},{2,6},{6,2},{3,7},{7,3},{8,12},{12,8},{9,1... | collective-permute-start | bytes 1228808 | tf_op jit(solution)/shard_map/ppermute | solution.py:23
  63.8 10.0 %collective-permute-start.32 = (bf16[320,640]{1,0:T(8,128)(2,1)S(1)}, bf16[320,640]{1,0:T(8,128)(2,1)S(1)}, u32[]{:S(2)}, u32[]{:S(2)}) collective-permute-start(bf16[320,640]{1,0:T(8,128)(2,1)S(1)} %collective-permute-done.24.refs_7_), channel_id=1, source_target_pairs={{0,4},{4,0},{1,5},{5,1},{2,6},{6,2},{3,7},{7,3},{8,12},{12,8},{9,1... | collective-permute-start | bytes 1228808 | tf_op jit(solution)/shard_map/ppermute | solution.py:23
  67.3 6.5 %collective-permute-start.29 = (bf16[320,640]{1,0:T(8,128)(2,1)S(1)}, bf16[320,640]{1,0:T(8,128)(2,1)S(1)}, u32[]{:S(2)}, u32[]{:S(2)}) collective-permute-start(bf16[320,640]{1,0:T(8,128)(2,1)S(1)} %collective-permute-done.22.refs_4_), channel_id=1, source_target_pairs={{0,4},{4,0},{1,5},{5,1},{2,6},{6,2},{3,7},{7,3},{8,12},{12,8},{9,1... | collective-permute-start | bytes 1228808 | tf_op jit(solution)/shard_map/ppermute | solution.py:23
  68.6 5.2 %collective-permute-start.30 = (bf16[320,640]{1,0:T(8,128)(2,1)S(1)}, bf16[320,640]{1,0:T(8,128)(2,1)S(1)}, u32[]{:S(2)}, u32[]{:S(2)}) collective-permute-start(bf16[320,640]{1,0:T(8,128)(2,1)S(1)} %collective-permute-done.23.refs_5_), channel_id=1, source_target_pairs={{0,4},{4,0},{1,5},{5,1},{2,6},{6,2},{3,7},{7,3},{8,12},{12,8},{9,1... | collective-permute-start | bytes 1228808 | tf_op jit(solution)/shard_map/ppermute | solution.py:23
  77.6 8.8 %collective-permute-start.33 = (bf16[32,2688]{1,0:T(8,128)(2,1)S(1)}, bf16[32,2688]{1,0:T(8,128)(2,1)S(1)}, u32[]{:S(2)}, u32[]{:S(2)}) collective-permute-start(bf16[32,2688]{1,0:T(8,128)(2,1)S(1)} %get-tuple-element.54), channel_id=1, source_target_pairs={{0,2},{1,3},{2,0},{3,1},{4,6},{5,7},{6,4},{7,5},{8,10},{9,11},{10,... | collective-permute-start | bytes 516104 | tf_op jit(solution)/shard_map/ppermute | solution.py:23
  80.8 9.0 %collective-permute-start.34 = (bf16[32,2688]{1,0:T(8,128)(2,1)S(1)}, bf16[32,2688]{1,0:T(8,128)(2,1)S(1)}, u32[]{:S(2)}, u32[]{:S(2)}) collective-permute-start(bf16[32,2688]{1,0:T(8,128)(2,1)S(1)} %get-tuple-element.55), channel_id=1, source_target_pairs={{0,1},{1,0},{2,3},{3,2},{4,5},{5,4},{6,7},{7,6},{8,9},{9,8},{10,11... | collective-permute-start | bytes 516104 | tf_op jit(solution)/shard_map/ppermute | solution.py:23
  81.5 8.4 %collective-permute-start.35 = (bf16[32,2688]{1,0:T(8,128)(2,1)S(1)}, bf16[32,2688]{1,0:T(8,128)(2,1)S(1)}, u32[]{:S(2)}, u32[]{:S(2)}) collective-permute-start(bf16[32,2688]{1,0:T(8,128)(2,1)S(1)} %get-tuple-element.56), channel_id=1, source_target_pairs={{0,3},{1,2},{2,1},{3,0},{4,7},{5,6},{6,5},{7,4},{8,11},{9,10},{10,... | collective-permute-start | bytes 516104 | tf_op jit(solution)/shard_map/ppermute | solution.py:23
  (16 other events, 37.3 us)

commit v3 on v2

--- a/solution.py
+++ b/solution.py
@@ -27,12 +27,12 @@
     return lax.ppermute(value, axis, [(i, (i + step) % size) for i in range(size)])
 
 
-def call(body, place, args, outs, scratch=(), flops=10**8, vmem=4):
+def call(body, place, args, outs, scratch=(), flops=10**8, vmem=4, space=pltpu.VMEM):
     return pl.pallas_call(
         body,
         out_shape=outs,
         in_specs=[pl.BlockSpec(memory_space=pltpu.SMEM)]
-        + [pl.BlockSpec(memory_space=pltpu.VMEM)] * len(args),
+        + [pl.BlockSpec(memory_space=space)] * len(args),
         out_specs=[pl.BlockSpec(memory_space=pltpu.VMEM)] * len(outs),
         scratch_shapes=list(scratch),
         compiler_params=pltpu.CompilerParams(vmem_limit_bytes=vmem << 20),
@@ -71,8 +71,16 @@
     return parts[:size] + parts[size : 2 * size] + parts[2 * size :]
 
 
-def state_kernel(place, values, keys, log_decay, msg, cum_ref):
+def state_kernel(place, values_hbm, keys_hbm, decay_hbm, msg, cum_ref, values, keys, log_decay, sems):
     lane = lanes()
+    copies = [
+        pltpu.make_async_copy(decay_hbm, log_decay, sems.at[0]),
+        pltpu.make_async_copy(keys_hbm, keys, sems.at[1]),
+        pltpu.make_async_copy(values_hbm, values, sems.at[2]),
+    ]
+    for copy in copies:
+        copy.start()
+    copies[0].wait()
     cum = jnp.concatenate([log_decay[...], jnp.zeros((4, TOK), F32)], axis=0)
     step = 1
     while step < TOK:
@@ -86,6 +94,8 @@
     spread = jnp.where(lane < 10, spread, pltpu.roll(spread, 6, 1))
     spread = jnp.where((lane < 10) | ((lane >= 16) & (lane < 26)), spread, 0.0)
     put_totals(msg, COLS, 32, spread.T[:32])
+    copies[1].wait()
+    copies[2].wait()
     key = keys[...]
     for p in range(10):
         cols = slice(p * LANE, (p + 1) * LANE)
@@ -431,7 +441,12 @@
     state, cum = call(
         state_kernel, place, (values, key_rows, log_decay.T),
         [shaped(COLS + 96, NST), shaped(TOK, LANE, dtype=F32)],
+        scratch=[
+            pltpu.VMEM((TOK, COLS), BF), pltpu.VMEM((TOK, NST), BF), pltpu.VMEM((HEADS, TOK), F32),
+            pltpu.SemaphoreType.DMA((3,)),
+        ],
         vmem=6,
+        space=pltpu.HBM,
     )
     got0 = flip(state, "core", 1, 2)
     quart = shaped(QUART + 48, NST)

time: 92.9 us -> 93.3 us (level)
  no operation moved by 1% of the time
where the time goes in v3:
time: 93.3 us; the launch traced here: 91.8 us
  waiting for transfers between devices  39.2 us (42%)
  starting transfers between devices  30.6 us (33%)
  Pallas kernels  18.6 us (20%)
  local copies, waits for them, and re-layouts  3.04 us (3%)
    ppermute x29, waiting for transfers between devices, flip(): return lax.ppermute(value, axis, [(i, i ^ mask) for i in range(size)])  31.9 us
    pallas_call x13, Pallas kernels, call(): pl.pallas_call(body, out_shape=outs, in_specs=[pl.BlockSpec(memory_space=...  18.6 us
    ppermute x29, starting transfers between devices, flip(): return lax.ppermute(value, axis, [(i, i ^ mask) for i in range(size)])  16.4 us
    ppermute x7, starting transfers between devices, shift(): lax.ppermute(value, axis, [(i, (i + step) % size) for i in range(size)])  14.2 us
    ppermute x7, waiting for transfers between devices, shift(): lax.ppermute(value, axis, [(i, (i + step) % size) for i in range(size)])  7.37 us
    unnamed x24, local copies, waits for them, and re-layouts  3.04 us
  transfers between devices with their start and end apart: 36, of which 15 were waited for; matrix products, arithmetic and copies ran while one was open for 0% of the time, Pallas kernels for 14%

profile of v3, /device:TPU:6, one launch (start us, length us, event | category | flops | bytes accessed | tf_op | source)
XLA Modules:
  0.0 91.8 jit_solution(463159389842279296)
XLA Ops:
  0.8 1.0 %copy-done.1 = bf16[128,1280]{1,0:T(8,128)(2,1)S(1)} copy-done((bf16[128,1280]{1,0:T(8,128)(2,1)S(1)}, bf16[128,1280]{1,0:T(8,128)(2,1)}, u32[]{:S(2)}) %copy-start.1) | copy-done | bytes 327704
  1.7 0.7 copy-done.5
  2.4 2.3 %shard_map.109 = (bf16[1376,128]{1,0:T(8,128)(2,1)S(1)}, f32[128,128]{1,0:T(8,128)S(1)}) custom-call(s32[4]{0:T(128)S(1)} %pad_add_fusion.place.r_0_, bf16[128,1280]{1,0:T(8,128)(2,1)S(1)} %copy-done.1, bf16[128,128]{1,0:T(8,128)(2,1)S(1)} %copy-done.4, f32[20,128]{1,0:T(8,128)S(1)} %bitcast.13), custom_call_target="tpu_custom_call" | custom-call | flops 100000000 | bytes 1048576 | tf_op jit(solution)/shard_map/pallas_call | solution.py:31
  5.0 5.9 %collective-permute-start.14 = (bf16[80,640]{1,0:T(8,128)(2,1)S(1)}, bf16[80,640]{1,0:T(8,128)(2,1)S(1)}, u32[]{:S(2)}, u32[]{:S(2)}) collective-permute-start(bf16[80,640]{1,0:T(8,128)(2,1)S(1)} %fusion.c), channel_id=1, source_target_pairs={{0,56},{8,0},{16,8},{24,16},{32,24},{40,32},{48,40},{56,48},{1,57}... | collective-permute-start | bytes 307208 | tf_op jit(solution)/shard_map/ppermute | solution.py:27
  11.6 2.0 %collective-permute-done.14.d = bf16[80,640]{1,0:T(8,128)(2,1)S(1)} collective-permute-done((bf16[80,640]{1,0:T(8,128)(2,1)S(1)}, bf16[80,640]{1,0:T(8,128)(2,1)S(1)}, u32[]{:S(2)}, u32[]{:S(2)}) %collective-permute-start.14) | collective-permute-done | bytes 102432 | tf_op jit(solution)/shard_map/ppermute | solution.py:27
  13.7 3.7 %collective-permute-start.15 = (bf16[80,640]{1,0:T(8,128)(2,1)S(1)}, bf16[80,640]{1,0:T(8,128)(2,1)S(1)}, u32[]{:S(2)}, u32[]{:S(2)}) collective-permute-start(bf16[80,640]{1,0:T(8,128)(2,1)S(1)} %collective-permute-done.14.d), channel_id=1, source_target_pairs={{0,56},{8,0},{16,8},{24,16},{32,24},{40,32},{48,40},{56,48},{1,57}... | collective-permute-start | bytes 307208 | tf_op jit(solution)/shard_map/ppermute | solution.py:27
  17.4 3.0 %collective-permute-done.15.a = bf16[80,640]{1,0:T(8,128)(2,1)S(1)} collective-permute-done((bf16[80,640]{1,0:T(8,128)(2,1)S(1)}, bf16[80,640]{1,0:T(8,128)(2,1)S(1)}, u32[]{:S(2)}, u32[]{:S(2)}) %collective-permute-start.15) | collective-permute-done | bytes 102432 | tf_op jit(solution)/shard_map/ppermute | solution.py:27
  20.4 2.9 %collective-permute-start.16 = (bf16[80,640]{1,0:T(8,128)(2,1)S(1)}, bf16[80,640]{1,0:T(8,128)(2,1)S(1)}, u32[]{:S(2)}, u32[]{:S(2)}) collective-permute-start(bf16[80,640]{1,0:T(8,128)(2,1)S(1)} %collective-permute-done.15.a), channel_id=1, source_target_pairs={{0,56},{8,0},{16,8},{24,16},{32,24},{40,32},{48,40},{56,48},{1,57}... | collective-permute-start | bytes 307208 | tf_op jit(solution)/shard_map/ppermute | solution.py:27
  24.6 0.9 collective-permute-start.19
  25.5 3.8 %collective-permute-done.3.r_2_.r_4_.got2 = bf16[368,128]{1,0:T(8,128)(2,1)S(1)} collective-permute-done((bf16[368,128]{1,0:T(8,128)(2,1)S(1)}, bf16[368,128]{1,0:T(8,128)(2,1)S(1)}, u32[]{:S(2)}, u32[]{:S(2)}) %collective-permute-start.3) | collective-permute-done | bytes 94240 | tf_op jit(solution)/shard_map/ppermute | solution.py:23
  29.4 1.7 %collective-permute-start.17 = (bf16[80,640]{1,0:T(8,128)(2,1)S(1)}, bf16[80,640]{1,0:T(8,128)(2,1)S(1)}, u32[]{:S(2)}, u32[]{:S(2)}) collective-permute-start(bf16[80,640]{1,0:T(8,128)(2,1)S(1)} %collective-permute-done.16.b), channel_id=1, source_target_pairs={{0,56},{8,0},{16,8},{24,16},{32,24},{40,32},{48,40},{56,48},{1,57}... | collective-permute-start | bytes 307208 | tf_op jit(solution)/shard_map/ppermute | solution.py:27
  31.7 1.1 %collective-permute-start.4 = (bf16[368,128]{1,0:T(8,128)(2,1)S(1)}, bf16[368,128]{1,0:T(8,128)(2,1)S(1)}, u32[]{:S(2)}, u32[]{:S(2)}) collective-permute-start(bf16[368,128]{1,0:T(8,128)(2,1)S(1)} %get-tuple-element.41.r_1_), channel_id=1, source_target_pairs={{0,48},{8,56},{16,32},{24,40},{32,16},{40,24},{48,0},{56,8},{1,49}... | collective-permute-start | bytes 282632 | tf_op jit(solution)/shard_map/ppermute | solution.py:23
  32.9 2.2 %collective-permute-done.17.c = bf16[80,640]{1,0:T(8,128)(2,1)S(1)} collective-permute-done((bf16[80,640]{1,0:T(8,128)(2,1)S(1)}, bf16[80,640]{1,0:T(8,128)(2,1)S(1)}, u32[]{:S(2)}, u32[]{:S(2)}) %collective-permute-start.17) | collective-permute-done | bytes 102432 | tf_op jit(solution)/shard_map/ppermute | solution.py:27
  35.1 0.8 collective-permute-start.20
  36.6 4.4 %shard_map.110 = (f32[128,1280]{1,0:T(8,128)S(1)}, f32[128,128]{1,0:T(8,128)S(1)}, bf16[384,128]{1,0:T(8,128)(2,1)S(1)}) custom-call(s32[4]{0:T(128)S(1)} %pad_add_fusion.place.r_0_, bf16[128,128]{1,0:T(8,128)(2,1)S(1)} %copy-done.3, bf16[128,128]{1,0:T(8,128)(2,1)S(1)} %copy-done.4, bf16[128,1280]{1,0:T(8,128)(2,1)S(1)} %copy-done.2, ...), custom_call_target="tpu_custom_call" | custom-call | flops 300000000 | bytes 1048576 | tf_op jit(solution)/shard_map/pallas_call | solution.py:31
  43.1 2.9 %collective-permute-start.6 = (bf16[368,128]{1,0:T(8,128)(2,1)S(1)}, bf16[368,128]{1,0:T(8,128)(2,1)S(1)}, u32[]{:S(2)}, u32[]{:S(2)}) collective-permute-start(bf16[368,128]{1,0:T(8,128)(2,1)S(1)} %get-tuple-element.43), channel_id=1, source_target_pairs={{0,128},{64,192},{128,0},{192,64},{1,129},{65,193},{129,1},{193,65... | collective-permute-start | bytes 282632 | tf_op jit(solution)/shard_map/ppermute | solution.py:23
  46.7 3.8 %collective-permute-done.7.r3 = bf16[368,128]{1,0:T(8,128)(2,1)S(1)} collective-permute-done((bf16[368,128]{1,0:T(8,128)(2,1)S(1)}, bf16[368,128]{1,0:T(8,128)(2,1)S(1)}, u32[]{:S(2)}, u32[]{:S(2)}) %collective-permute-start.7) | collective-permute-done | bytes 94240 | tf_op jit(solution)/shard_map/ppermute | solution.py:23
  50.5 0.8 collective-permute-start.8
  51.3 4.6 %collective-permute-done.5.r1 = bf16[368,128]{1,0:T(8,128)(2,1)S(1)} collective-permute-done((bf16[368,128]{1,0:T(8,128)(2,1)S(1)}, bf16[368,128]{1,0:T(8,128)(2,1)S(1)}, u32[]{:S(2)}, u32[]{:S(2)}) %collective-permute-start.5) | collective-permute-done | bytes 94240 | tf_op jit(solution)/shard_map/ppermute | solution.py:23
  56.4 0.8 collective-permute-start.23
  57.8 0.7 collective-permute-start.9
  59.2 5.1 %collective-permute-done.9.late_side = bf16[640,128]{1,0:T(8,128)(2,1)S(1)} collective-permute-done((bf16[640,128]{1,0:T(8,128)(2,1)S(1)}, bf16[640,128]{1,0:T(8,128)(2,1)S(1)}, u32[]{:S(2)}, u32[]{:S(2)}) %collective-permute-start.9) | collective-permute-done | bytes 163872 | tf_op jit(solution)/shard_map/ppermute | solution.py:23
  64.7 3.0 %collective-permute-done.22.refs_4_ = bf16[320,640]{1,0:T(8,128)(2,1)S(1)} collective-permute-done((bf16[320,640]{1,0:T(8,128)(2,1)S(1)}, bf16[320,640]{1,0:T(8,128)(2,1)S(1)}, u32[]{:S(2)}, u32[]{:S(2)}) %collective-permute-start.22) | collective-permute-done | bytes 409632 | tf_op jit(solution)/shard_map/ppermute | solution.py:23
  67.7 1.3 %collective-permute-done.23.refs_5_ = bf16[320,640]{1,0:T(8,128)(2,1)S(1)} collective-permute-done((bf16[320,640]{1,0:T(8,128)(2,1)S(1)}, bf16[320,640]{1,0:T(8,128)(2,1)S(1)}, u32[]{:S(2)}, u32[]{:S(2)}) %collective-permute-start.23) | collective-permute-done | bytes 409632 | tf_op jit(solution)/shard_map/ppermute | solution.py:23
  69.0 2.0 %shard_map.116 = (f32[128,640]{1,0:T(8,128)S(1)}, f32[128,640]{1,0:T(8,128)S(1)}, f32[128,128]{1,0:T(8,128)S(1)}, f32[128,128]{1,0:T(8,128)S(1)}) custom-call(s32[4]{0:T(128)S(1)} %pad_add_fusion.place.r_0_, bf16[128,128]{1,0:T(8,128)(2,1)S(1)} %copy-done.3, f32[128,128]{1,0:T(8,128)S(1)} %get-tuple-element.35.factors, ...), custom_call_target="tpu_custom_call" | custom-call | flops 100000000 | bytes 1048576 | tf_op jit(solution)/shard_map/pallas_call | solution.py:31
  71.1 1.5 %shard_map.117 = (f32[128,640]{1,0:T(8,128)S(1)}, bf16[128,640]{1,0:T(8,128)(2,1)S(1)}) custom-call(s32[4]{0:T(128)S(1)} %pad_add_fusion.place.r_0_, bf16[128,128]{1,0:T(8,128)(2,1)S(1)} %copy-done.3, bf16[384,128]{1,0:T(8,128)(2,1)S(1)} %collective-permute-done.1.mail, f32[128,128]{1,0:T(8,128)S(1)} %get-tuple-element.46.own_w, ...), custom_call_target="tpu_custom_call" | custom-call | flops 100000000 | bytes 1048576 | tf_op jit(solution)/shard_map/pallas_call | solution.py:31
  73.2 1.0 %collective-permute-done.10.back = bf16[128,640]{1,0:T(8,128)(2,1)S(1)} collective-permute-done((bf16[128,640]{1,0:T(8,128)(2,1)S(1)}, bf16[128,640]{1,0:T(8,128)(2,1)S(1)}, u32[]{:S(2)}, u32[]{:S(2)}) %collective-permute-start.10) | collective-permute-done | bytes 163872 | tf_op jit(solution)/shard_map/ppermute | solution.py:23
  74.3 3.7 %shard_map.120 = (bf16[32,2688]{1,0:T(8,128)(2,1)S(1)}, bf16[32,2688]{1,0:T(8,128)(2,1)S(1)}, bf16[32,2688]{1,0:T(8,128)(2,1)S(1)}, bf16[32,2688]{1,0:T(8,128)(2,1)S(1)}) custom-call(s32[4]{0:T(128)S(1)} %pad_add_fusion.place.r_0_, f32[128,1280]{1,0:T(8,128)S(1)} %get-tuple-element.33.base, f32[128,640]{1,0:T(8,128)S(1)} %get-tuple-element.51.own, ...), custom_call_target="tpu_custom_call" | custom-call | flops 1000000000 | bytes 1048576 | tf_op jit(solution)/shard_map/pallas_call | solution.py:31
  78.0 3.3 %collective-permute-start.33 = (bf16[32,2688]{1,0:T(8,128)(2,1)S(1)}, bf16[32,2688]{1,0:T(8,128)(2,1)S(1)}, u32[]{:S(2)}, u32[]{:S(2)}) collective-permute-start(bf16[32,2688]{1,0:T(8,128)(2,1)S(1)} %get-tuple-element.54), channel_id=1, source_target_pairs={{0,2},{1,3},{2,0},{3,1},{4,6},{5,7},{6,4},{7,5},{8,10},{9,11},{10,... | collective-permute-start | bytes 516104 | tf_op jit(solution)/shard_map/ppermute | solution.py:23
  82.4 4.5 %collective-permute-done.33.b_ref = bf16[32,2688]{1,0:T(8,128)(2,1)S(1)} collective-permute-done((bf16[32,2688]{1,0:T(8,128)(2,1)S(1)}, bf16[32,2688]{1,0:T(8,128)(2,1)S(1)}, u32[]{:S(2)}, u32[]{:S(2)}) %collective-permute-start.33) | collective-permute-done | bytes 172064 | tf_op jit(solution)/shard_map/ppermute | solution.py:23
  86.9 3.5 %collective-permute-done.34.c_ref = bf16[32,2688]{1,0:T(8,128)(2,1)S(1)} collective-permute-done((bf16[32,2688]{1,0:T(8,128)(2,1)S(1)}, bf16[32,2688]{1,0:T(8,128)(2,1)S(1)}, u32[]{:S(2)}, u32[]{:S(2)}) %collective-permute-start.34) | collective-permute-done | bytes 172064 | tf_op jit(solution)/shard_map/ppermute | solution.py:23
  90.3 1.5 %shard_map.121 = bf16[32,2560]{1,0:T(8,128)(2,1)} custom-call(s32[4]{0:T(128)S(1)} %pad_add_fusion.place.r_0_, bf16[32,2688]{1,0:T(8,128)(2,1)S(1)} %get-tuple-element.53.a_ref, bf16[32,2688]{1,0:T(8,128)(2,1)S(1)} %collective-permute-done.33.b_ref, bf16[32,2688]{1,0:T(8,128)(2,1)S(1)} %collective-permute-done.34.c_ref, ...), custom_call_target="tpu_custom_call" | custom-call | flops 100000000 | bytes 1048576 | tf_op jit(solution)/shard_map/pallas_call | solution.py:31
  (80 shorter events, 11.2 us)
Async XLA Ops:
  4.8 6.1 %collective-permute-start = (bf16[1376,128]{1,0:T(8,128)(2,1)S(1)}, bf16[1376,128]{1,0:T(8,128)(2,1)S(1)}, u32[]{:S(2)}, u32[]{:S(2)}) collective-permute-start(bf16[1376,128]{1,0:T(8,128)(2,1)S(1)} %get-tuple-element.32.own), channel_id=1, source_target_pairs={{0,4},{4,0},{1,5},{5,1},{2,6},{6,2},{3,7},{7,3},{8,12},{12,8},{9,1... | collective-permute-start | bytes 1056776 | tf_op jit(solution)/shard_map/ppermute | solution.py:23
  5.0 8.7 %collective-permute-start.14 = (bf16[80,640]{1,0:T(8,128)(2,1)S(1)}, bf16[80,640]{1,0:T(8,128)(2,1)S(1)}, u32[]{:S(2)}, u32[]{:S(2)}) collective-permute-start(bf16[80,640]{1,0:T(8,128)(2,1)S(1)} %fusion.c), channel_id=1, source_target_pairs={{0,56},{8,0},{16,8},{24,16},{32,24},{40,32},{48,40},{56,48},{1,57}... | collective-permute-start | bytes 307208 | tf_op jit(solution)/shard_map/ppermute | solution.py:27
  10.9 6.5 %collective-permute-start.12 = (bf16[80,640]{1,0:T(8,128)(2,1)S(1)}, bf16[80,640]{1,0:T(8,128)(2,1)S(1)}, u32[]{:S(2)}, u32[]{:S(2)}) collective-permute-start(bf16[80,640]{1,0:T(8,128)(2,1)S(1)} %fusion.c), channel_id=1, source_target_pairs={{0,8},{8,16},{16,24},{24,32},{32,40},{40,48},{48,56},{56,0},{1,9},... | collective-permute-start | bytes 307208 | tf_op jit(solution)/shard_map/ppermute | solution.py:27
  11.5 11.7 %collective-permute-start.2 = (bf16[688,128]{1,0:T(8,128)(2,1)S(1)}, bf16[688,128]{1,0:T(8,128)(2,1)S(1)}, u32[]{:S(2)}, u32[]{:S(2)}) collective-permute-start(bf16[688,128]{1,0:T(8,128)(2,1)S(1)} %get-tuple-element.37.own), channel_id=1, source_target_pairs={{0,8},{8,0},{16,24},{24,16},{32,40},{40,32},{48,56},{56,48},{1,9},... | collective-permute-start | bytes 528392 | tf_op jit(solution)/shard_map/ppermute | solution.py:23
  13.7 6.7 %collective-permute-start.15 = (bf16[80,640]{1,0:T(8,128)(2,1)S(1)}, bf16[80,640]{1,0:T(8,128)(2,1)S(1)}, u32[]{:S(2)}, u32[]{:S(2)}) collective-permute-start(bf16[80,640]{1,0:T(8,128)(2,1)S(1)} %collective-permute-done.14.d), channel_id=1, source_target_pairs={{0,56},{8,0},{16,8},{24,16},{32,24},{40,32},{48,40},{56,48},{1,57}... | collective-permute-start | bytes 307208 | tf_op jit(solution)/shard_map/ppermute | solution.py:27
  17.4 6.6 %collective-permute-start.13 = (bf16[80,640]{1,0:T(8,128)(2,1)S(1)}, bf16[80,640]{1,0:T(8,128)(2,1)S(1)}, u32[]{:S(2)}, u32[]{:S(2)}) collective-permute-start(bf16[80,640]{1,0:T(8,128)(2,1)S(1)} %collective-permute-done.12.b), channel_id=1, source_target_pairs={{0,8},{8,16},{16,24},{24,32},{32,40},{40,48},{48,56},{56,0},{1,9},... | collective-permute-start | bytes 307208 | tf_op jit(solution)/shard_map/ppermute | solution.py:27
  20.4 5.2 %collective-permute-start.16 = (bf16[80,640]{1,0:T(8,128)(2,1)S(1)}, bf16[80,640]{1,0:T(8,128)(2,1)S(1)}, u32[]{:S(2)}, u32[]{:S(2)}) collective-permute-start(bf16[80,640]{1,0:T(8,128)(2,1)S(1)} %collective-permute-done.15.a), channel_id=1, source_target_pairs={{0,56},{8,0},{16,8},{24,16},{32,24},{40,32},{48,40},{56,48},{1,57}... | collective-permute-start | bytes 307208 | tf_op jit(solution)/shard_map/ppermute | solution.py:27
  23.8 5.6 %collective-permute-start.3 = (bf16[368,128]{1,0:T(8,128)(2,1)S(1)}, bf16[368,128]{1,0:T(8,128)(2,1)S(1)}, u32[]{:S(2)}, u32[]{:S(2)}) collective-permute-start(bf16[368,128]{1,0:T(8,128)(2,1)S(1)} %get-tuple-element.39.r_1_), channel_id=1, source_target_pairs={{0,16},{8,24},{16,0},{24,8},{32,48},{40,56},{48,32},{56,40},{1,17}... | collective-permute-start | bytes 282632 | tf_op jit(solution)/shard_map/ppermute | solution.py:23
  24.0 19.1 %collective-permute-start.25 = (bf16[320,640]{1,0:T(8,128)(2,1)S(1)}, bf16[320,640]{1,0:T(8,128)(2,1)S(1)}, u32[]{:S(2)}, u32[]{:S(2)}) collective-permute-start(bf16[320,640]{1,0:T(8,128)(2,1)S(1)} %shard_map.118.refs_0_), channel_id=1, source_target_pairs={{0,4},{4,0},{1,5},{5,1},{2,6},{6,2},{3,7},{7,3},{8,12},{12,8},{9,1... | collective-permute-start | bytes 1228808 | tf_op jit(solution)/shard_map/ppermute | solution.py:23
  24.1 21.9 %collective-permute-start.21 = (bf16[320,640]{1,0:T(8,128)(2,1)S(1)}, bf16[320,640]{1,0:T(8,128)(2,1)S(1)}, u32[]{:S(2)}, u32[]{:S(2)}) collective-permute-start(bf16[320,640]{1,0:T(8,128)(2,1)S(1)} %shard_map.118.refs_0_), channel_id=1, source_target_pairs={{0,192},{64,128},{128,64},{192,0},{1,193},{65,129},{129,65},{193,1... | collective-permute-start | bytes 1228808 | tf_op jit(solution)/shard_map/ppermute | solution.py:23
  24.6 21.3 %collective-permute-start.19 = (bf16[320,640]{1,0:T(8,128)(2,1)S(1)}, bf16[320,640]{1,0:T(8,128)(2,1)S(1)}, u32[]{:S(2)}, u32[]{:S(2)}) collective-permute-start(bf16[320,640]{1,0:T(8,128)(2,1)S(1)} %shard_map.118.refs_0_), channel_id=1, source_target_pairs={{0,64},{64,0},{128,192},{192,128},{1,65},{65,1},{129,193},{193,129... | collective-permute-start | bytes 1228808 | tf_op jit(solution)/shard_map/ppermute | solution.py:23
  25.5 6.2 %collective-permute-start.18 = (bf16[80,640]{1,0:T(8,128)(2,1)S(1)}, bf16[80,640]{1,0:T(8,128)(2,1)S(1)}, u32[]{:S(2)}, u32[]{:S(2)}) collective-permute-start(bf16[80,640]{1,0:T(8,128)(2,1)S(1)} %collective-permute-done.13.a), channel_id=1, source_target_pairs={{0,8},{8,16},{16,24},{24,32},{32,40},{40,48},{48,56},{56,0},{1,9},... | collective-permute-start | bytes 307208 | tf_op jit(solution)/shard_map/ppermute | solution.py:27
  29.4 5.7 %collective-permute-start.17 = (bf16[80,640]{1,0:T(8,128)(2,1)S(1)}, bf16[80,640]{1,0:T(8,128)(2,1)S(1)}, u32[]{:S(2)}, u32[]{:S(2)}) collective-permute-start(bf16[80,640]{1,0:T(8,128)(2,1)S(1)} %collective-permute-done.16.b), channel_id=1, source_target_pairs={{0,56},{8,0},{16,8},{24,16},{32,24},{40,32},{48,40},{56,48},{1,57}... | collective-permute-start | bytes 307208 | tf_op jit(solution)/shard_map/ppermute | solution.py:27
  31.7 9.3 %collective-permute-start.4 = (bf16[368,128]{1,0:T(8,128)(2,1)S(1)}, bf16[368,128]{1,0:T(8,128)(2,1)S(1)}, u32[]{:S(2)}, u32[]{:S(2)}) collective-permute-start(bf16[368,128]{1,0:T(8,128)(2,1)S(1)} %get-tuple-element.41.r_1_), channel_id=1, source_target_pairs={{0,48},{8,56},{16,32},{24,40},{32,16},{40,24},{48,0},{56,8},{1,49}... | collective-permute-start | bytes 282632 | tf_op jit(solution)/shard_map/ppermute | solution.py:23
  35.1 21.3 %collective-permute-start.20 = (bf16[320,640]{1,0:T(8,128)(2,1)S(1)}, bf16[320,640]{1,0:T(8,128)(2,1)S(1)}, u32[]{:S(2)}, u32[]{:S(2)}) collective-permute-start(bf16[320,640]{1,0:T(8,128)(2,1)S(1)} %shard_map.119.refs_1_), channel_id=1, source_target_pairs={{0,64},{64,0},{128,192},{192,128},{1,65},{65,1},{129,193},{193,129... | collective-permute-start | bytes 1228808 | tf_op jit(solution)/shard_map/ppermute | solution.py:23
  42.4 8.1 %collective-permute-start.7 = (bf16[368,128]{1,0:T(8,128)(2,1)S(1)}, bf16[368,128]{1,0:T(8,128)(2,1)S(1)}, u32[]{:S(2)}, u32[]{:S(2)}) collective-permute-start(bf16[368,128]{1,0:T(8,128)(2,1)S(1)} %get-tuple-element.43), channel_id=1, source_target_pairs={{0,192},{64,128},{128,64},{192,0},{1,193},{65,129},{129,65},{193,1... | collective-permute-start | bytes 282632 | tf_op jit(solution)/shard_map/ppermute | solution.py:23
  43.1 8.2 %collective-permute-start.6 = (bf16[368,128]{1,0:T(8,128)(2,1)S(1)}, bf16[368,128]{1,0:T(8,128)(2,1)S(1)}, u32[]{:S(2)}, u32[]{:S(2)}) collective-permute-start(bf16[368,128]{1,0:T(8,128)(2,1)S(1)} %get-tuple-element.43), channel_id=1, source_target_pairs={{0,128},{64,192},{128,0},{192,64},{1,129},{65,193},{129,1},{193,65... | collective-permute-start | bytes 282632 | tf_op jit(solution)/shard_map/ppermute | solution.py:23
  46.0 11.8 %collective-permute-start.26 = (bf16[320,640]{1,0:T(8,128)(2,1)S(1)}, bf16[320,640]{1,0:T(8,128)(2,1)S(1)}, u32[]{:S(2)}, u32[]{:S(2)}) collective-permute-start(bf16[320,640]{1,0:T(8,128)(2,1)S(1)} %shard_map.119.refs_1_), channel_id=1, source_target_pairs={{0,4},{4,0},{1,5},{5,1},{2,6},{6,2},{3,7},{7,3},{8,12},{12,8},{9,1... | collective-permute-start | bytes 1228808 | tf_op jit(solution)/shard_map/ppermute | solution.py:23
  46.0 13.2 %collective-permute-start.24 = (bf16[320,640]{1,0:T(8,128)(2,1)S(1)}, bf16[320,640]{1,0:T(8,128)(2,1)S(1)}, u32[]{:S(2)}, u32[]{:S(2)}) collective-permute-start(bf16[320,640]{1,0:T(8,128)(2,1)S(1)} %shard_map.119.refs_1_), channel_id=1, source_target_pairs={{0,192},{64,128},{128,64},{192,0},{1,193},{65,129},{129,65},{193,1... | collective-permute-start | bytes 1228808 | tf_op jit(solution)/shard_map/ppermute | solution.py:23
  50.5 5.4 %collective-permute-start.8 = (bf16[640,128]{1,0:T(8,128)(2,1)S(1)}, bf16[640,128]{1,0:T(8,128)(2,1)S(1)}, u32[]{:S(2)}, u32[]{:S(2)}) collective-permute-start(bf16[640,128]{1,0:T(8,128)(2,1)S(1)} %get-tuple-element.45), channel_id=1, source_target_pairs={{0,8},{8,0},{16,24},{24,16},{32,40},{40,32},{48,56},{56,48},{1,9},... | collective-permute-start | bytes 491528 | tf_op jit(solution)/shard_map/ppermute | solution.py:23
  55.9 8.4 %collective-permute-start.31 = (bf16[320,640]{1,0:T(8,128)(2,1)S(1)}, bf16[320,640]{1,0:T(8,128)(2,1)S(1)}, u32[]{:S(2)}, u32[]{:S(2)}) collective-permute-start(bf16[320,640]{1,0:T(8,128)(2,1)S(1)} %collective-permute-done.21.refs_6_), channel_id=1, source_target_pairs={{0,4},{4,0},{1,5},{5,1},{2,6},{6,2},{3,7},{7,3},{8,12},{12,8},{9,1... | collective-permute-start | bytes 1228808 | tf_op jit(solution)/shard_map/ppermute | solution.py:23
  55.9 11.9 %collective-permute-start.22 = (bf16[320,640]{1,0:T(8,128)(2,1)S(1)}, bf16[320,640]{1,0:T(8,128)(2,1)S(1)}, u32[]{:S(2)}, u32[]{:S(2)}) collective-permute-start(bf16[320,640]{1,0:T(8,128)(2,1)S(1)} %collective-permute-done.21.refs_6_), channel_id=1, source_target_pairs={{0,64},{64,0},{128,192},{192,128},{1,65},{65,1},{129,193},{193,129... | collective-permute-start | bytes 1228808 | tf_op jit(solution)/shard_map/ppermute | solution.py:23
  56.4 12.6 %collective-permute-start.23 = (bf16[320,640]{1,0:T(8,128)(2,1)S(1)}, bf16[320,640]{1,0:T(8,128)(2,1)S(1)}, u32[]{:S(2)}, u32[]{:S(2)}) collective-permute-start(bf16[320,640]{1,0:T(8,128)(2,1)S(1)} %collective-permute-done.20.refs_3_), channel_id=1, source_target_pairs={{0,192},{64,128},{128,64},{192,0},{1,193},{65,129},{129,65},{193,1... | collective-permute-start | bytes 1228808 | tf_op jit(solution)/shard_map/ppermute | solution.py:23
  57.8 6.4 %collective-permute-start.9 = (bf16[640,128]{1,0:T(8,128)(2,1)S(1)}, bf16[640,128]{1,0:T(8,128)(2,1)S(1)}, u32[]{:S(2)}, u32[]{:S(2)}) collective-permute-start(bf16[640,128]{1,0:T(8,128)(2,1)S(1)} %get-tuple-element.48.late), channel_id=1, source_target_pairs={{0,8},{8,0},{16,24},{24,16},{32,40},{40,32},{48,56},{56,48},{1,9},... | collective-permute-start | bytes 491528 | tf_op jit(solution)/shard_map/ppermute | solution.py:23
  59.2 13.4 %collective-permute-start.27 = (bf16[320,640]{1,0:T(8,128)(2,1)S(1)}, bf16[320,640]{1,0:T(8,128)(2,1)S(1)}, u32[]{:S(2)}, u32[]{:S(2)}) collective-permute-start(bf16[320,640]{1,0:T(8,128)(2,1)S(1)} %collective-permute-done.19.refs_2_), channel_id=1, source_target_pairs={{0,4},{4,0},{1,5},{5,1},{2,6},{6,2},{3,7},{7,3},{8,12},{12,8},{9,1... | collective-permute-start | bytes 1228808 | tf_op jit(solution)/shard_map/ppermute | solution.py:23
  64.2 10.0 %collective-permute-start.28 = (bf16[320,640]{1,0:T(8,128)(2,1)S(1)}, bf16[320,640]{1,0:T(8,128)(2,1)S(1)}, u32[]{:S(2)}, u32[]{:S(2)}) collective-permute-start(bf16[320,640]{1,0:T(8,128)(2,1)S(1)} %collective-permute-done.20.refs_3_), channel_id=1, source_target_pairs={{0,4},{4,0},{1,5},{5,1},{2,6},{6,2},{3,7},{7,3},{8,12},{12,8},{9,1... | collective-permute-start | bytes 1228808 | tf_op jit(solution)/shard_map/ppermute | solution.py:23
  64.2 10.0 %collective-permute-start.32 = (bf16[320,640]{1,0:T(8,128)(2,1)S(1)}, bf16[320,640]{1,0:T(8,128)(2,1)S(1)}, u32[]{:S(2)}, u32[]{:S(2)}) collective-permute-start(bf16[320,640]{1,0:T(8,128)(2,1)S(1)} %collective-permute-done.24.refs_7_), channel_id=1, source_target_pairs={{0,4},{4,0},{1,5},{5,1},{2,6},{6,2},{3,7},{7,3},{8,12},{12,8},{9,1... | collective-permute-start | bytes 1228808 | tf_op jit(solution)/shard_map/ppermute | solution.py:23
  67.7 6.5 %collective-permute-start.29 = (bf16[320,640]{1,0:T(8,128)(2,1)S(1)}, bf16[320,640]{1,0:T(8,128)(2,1)S(1)}, u32[]{:S(2)}, u32[]{:S(2)}) collective-permute-start(bf16[320,640]{1,0:T(8,128)(2,1)S(1)} %collective-permute-done.22.refs_4_), channel_id=1, source_target_pairs={{0,4},{4,0},{1,5},{5,1},{2,6},{6,2},{3,7},{7,3},{8,12},{12,8},{9,1... | collective-permute-start | bytes 1228808 | tf_op jit(solution)/shard_map/ppermute | solution.py:23
  69.0 5.2 %collective-permute-start.30 = (bf16[320,640]{1,0:T(8,128)(2,1)S(1)}, bf16[320,640]{1,0:T(8,128)(2,1)S(1)}, u32[]{:S(2)}, u32[]{:S(2)}) collective-permute-start(bf16[320,640]{1,0:T(8,128)(2,1)S(1)} %collective-permute-done.23.refs_5_), channel_id=1, source_target_pairs={{0,4},{4,0},{1,5},{5,1},{2,6},{6,2},{3,7},{7,3},{8,12},{12,8},{9,1... | collective-permute-start | bytes 1228808 | tf_op jit(solution)/shard_map/ppermute | solution.py:23
  78.0 8.8 %collective-permute-start.33 = (bf16[32,2688]{1,0:T(8,128)(2,1)S(1)}, bf16[32,2688]{1,0:T(8,128)(2,1)S(1)}, u32[]{:S(2)}, u32[]{:S(2)}) collective-permute-start(bf16[32,2688]{1,0:T(8,128)(2,1)S(1)} %get-tuple-element.54), channel_id=1, source_target_pairs={{0,2},{1,3},{2,0},{3,1},{4,6},{5,7},{6,4},{7,5},{8,10},{9,11},{10,... | collective-permute-start | bytes 516104 | tf_op jit(solution)/shard_map/ppermute | solution.py:23
  81.3 9.0 %collective-permute-start.34 = (bf16[32,2688]{1,0:T(8,128)(2,1)S(1)}, bf16[32,2688]{1,0:T(8,128)(2,1)S(1)}, u32[]{:S(2)}, u32[]{:S(2)}) collective-permute-start(bf16[32,2688]{1,0:T(8,128)(2,1)S(1)} %get-tuple-element.55), channel_id=1, source_target_pairs={{0,1},{1,0},{2,3},{3,2},{4,5},{5,4},{6,7},{7,6},{8,9},{9,8},{10,11... | collective-permute-start | bytes 516104 | tf_op jit(solution)/shard_map/ppermute | solution.py:23
  82.0 8.4 %collective-permute-start.35 = (bf16[32,2688]{1,0:T(8,128)(2,1)S(1)}, bf16[32,2688]{1,0:T(8,128)(2,1)S(1)}, u32[]{:S(2)}, u32[]{:S(2)}) collective-permute-start(bf16[32,2688]{1,0:T(8,128)(2,1)S(1)} %get-tuple-element.56), channel_id=1, source_target_pairs={{0,3},{1,2},{2,1},{3,0},{4,7},{5,6},{6,5},{7,4},{8,11},{9,10},{10,... | collective-permute-start | bytes 516104 | tf_op jit(solution)/shard_map/ppermute | solution.py:23
  (16 other events, 38.2 us)

commit v4 on v2

--- a/solution.py
+++ b/solution.py
@@ -169,14 +169,10 @@
         ).astype(BF)
 
 
-def local_kernel(
-    place, queries, keys, values, cum_ref, lam_index, segments, lam_table, skip, got, base, factors, mail
-):
+def prep_kernel(place, queries, cum_ref, lam_index, lam_table, factors, mail, levels):
     core = place[0]
-    row, lane = rows(), lanes()
-    cum = cum_ref[...]
-    cum_t = cum.T
-    grow = jnp.exp(cum)
+    lane = lanes()
+    grow = jnp.exp(cum_ref[...])
     picks = lax.broadcasted_iota(I32, (64, TOK), 0)
     onehot = (picks == lam_index[...]).astype(F32).astype(BF)
 
@@ -211,14 +207,22 @@
     mail[TOK : 2 * TOK, :] = hi
     mail[2 * TOK :, :] = (theirs - hi.astype(F32)).astype(BF)
 
-    zero_level = jnp.where(core == 1, level(2) * grow, 0.0)
-    near, far = level(0), level(1)
+    levels[0] = level(0)
+    levels[1] = level(1)
+    levels[2] = jnp.where(core == 1, level(2) * grow, 0.0)
+
+
+def local_kernel(side, place, queries, keys, values, cum_ref, segments, levels, skip, got, base):
+    row, lane = rows(), lanes()
+    cum = cum_ref[...]
+    cum_t = cum.T
+    near, far, zero_level = levels[0], levels[1], levels[2]
     q = queries[...]
     scores = lax.dot_general(q, keys[...], NT, preferred_element_type=F32)
     seg_row = jnp.broadcast_to(segments[...].astype(F32), (TOK, LANE))
     same = seg_row == seg_row.T
     causal = row >= lane
-    for p in range(10):
+    for p in range(side * 5, side * 5 + 5):
         cols = slice(p * LANE, (p + 1) * LANE)
         pieces = []
         for h in (2 * p, 2 * p + 1):
@@ -231,7 +235,8 @@
         read = lax.dot_general(q, got[cols, :], NT, preferred_element_type=F32)
         read = read * two_heads(zero_level[:, 2 * p : 2 * p + 1], zero_level[:, 2 * p + 1 : 2 * p + 2], lane)
         gain = two_heads(skip[:, 2 * p : 2 * p + 1], skip[:, 2 * p + 1 : 2 * p + 2], lane)
-        base[:, cols] = jnp.concatenate(pieces, axis=1) + read + gain * values[:, cols].astype(F32)
+        out = slice((p % 5) * LANE, (p % 5) * LANE + LANE)
+        base[:, out] = jnp.concatenate(pieces, axis=1) + read + gain * values[:, cols].astype(F32)
 
 
 def level_weights(place, factors, mail, first_total, prefixes):
@@ -319,17 +324,40 @@
     )
 
 
-def project_kernel(place, base, own, back, gate, gain, *refs):
+def project_blocks(place, y_ref, w_refs, out_refs):
     core, y = place[0], place[1]
-    w_refs, out_refs, y_ref = refs[:16], refs[16:20], refs[20]
+    y_mine = y_ref[:, pl.ds(pl.multiple_of(core * HALF, HALF), HALF)]
+    y_rest = y_ref[:, pl.ds(pl.multiple_of((1 - core) * HALF, HALF), HALF)]
+    count = len(w_refs) // 4
+    for block in range(count):
+        mine_w = jnp.concatenate([w_refs[2 * block][...], w_refs[2 * block + 1][...]], axis=0)
+        at = 2 * (count + block)
+        rest_w = jnp.concatenate([w_refs[at][...], w_refs[at + 1][...]], axis=0)
+        total = lax.dot_general(y_mine, mine_w, NT, preferred_element_type=F32)
+        total = total + lax.dot_general(y_rest, rest_w, NT, preferred_element_type=F32)
+        store(y, out_refs, slice(block * HALF, (block + 1) * HALF), total.astype(BF))
+
+
+def store(y, out_refs, cols, value):
     part = TOK // NY
+    for d in range(NY):
+        for owner in range(NY):
+
+            @pl.when((y ^ d) == owner)
+            def _():
+                out_refs[d][:, cols] = value[owner * part : (owner + 1) * part]
+
+
+def first_kernel(place, low, high, own, back, gate, gain, *refs):
+    core, y = place[0], place[1]
+    w_refs, y_ref, out_refs = refs[:8], refs[8], refs[9:]
     lane = lanes()
     squares = jnp.zeros((TOK, LANE), F32)
     for p in range(10):
         cols = slice(p * LANE, (p + 1) * LANE)
         inner = slice((p % 5) * LANE, (p % 5) * LANE + LANE)
         cross = jnp.where(core == p // 5, own[:, inner], back[:, inner].astype(F32))
-        gated = base[:, cols] + cross
+        gated = (low if p < 5 else high)[:, inner] + cross
         v = gate[:, cols].astype(F32)
         gated = gated * (v / (1.0 + jnp.exp(-v)))
         squares = squares + gated * gated
@@ -339,43 +367,29 @@
     mid = (squares - hi).astype(BF).astype(F32)
     low = squares - hi - mid
     squares = jnp.where(lane == 0, hi, jnp.where(lane == 1, mid, jnp.where(lane == 2, low, 0.0)))
-    squares = squares.astype(BF)
-    mine = pl.ds(pl.multiple_of(core * HALF, HALF), HALF)
-    rest = pl.ds(pl.multiple_of((1 - core) * HALF, HALF), HALF)
-    y_mine, y_rest = y_ref[:, mine], y_ref[:, rest]
-
-    def store(d, cols, value):
-        for owner in range(NY):
-
-            @pl.when((y ^ d) == owner)
-            def _():
-                out_refs[d][:, cols] = value[owner * part : (owner + 1) * part]
-
-    for d in range(NY):
-        store(d, slice(2560, 2688), squares)
-    for block in range(4):
-        mine_w = jnp.concatenate([w_refs[2 * block][...], w_refs[2 * block + 1][...]], axis=0)
-        rest_w = jnp.concatenate([w_refs[8 + 2 * block][...], w_refs[9 + 2 * block][...]], axis=0)
-        total = lax.dot_general(y_mine, mine_w, NT, preferred_element_type=F32)
-        total = total + lax.dot_general(y_rest, rest_w, NT, preferred_element_type=F32)
-        total = total.astype(BF)
-        for d in range(NY):
-            store(d, slice(block * HALF, (block + 1) * HALF), total)
-
-
-def finish_kernel(place, a_ref, b_ref, c_ref, d_ref, out_ref):
+    store(y, out_refs, slice(2 * HALF, 2 * HALF + LANE), squares.astype(BF))
+    project_blocks(place, y_ref, w_refs, out_refs)
+
+
+def second_kernel(place, y_ref, *refs):
+    project_blocks(place, y_ref, refs[:8], refs[8:])
+
+
+def finish_kernel(place, *refs):
     x, z = place[2], place[3]
-
-    def total(cols):
-        left = a_ref[:, cols].astype(F32) + b_ref[:, cols].astype(F32)
-        return left + (c_ref[:, cols].astype(F32) + d_ref[:, cols].astype(F32))
-
-    squares = total(slice(2560, 2688))
+    firsts, seconds, out_ref = refs[:4], refs[4:8], refs[8]
+
+    def total(parts, cols):
+        left = parts[0][:, cols].astype(F32) + parts[1][:, cols].astype(F32)
+        return left + (parts[2][:, cols].astype(F32) + parts[3][:, cols].astype(F32))
+
+    squares = total(firsts, slice(2 * HALF, 2 * HALF + LANE))
     squares = squares[:, 0:1] + squares[:, 1:2] + squares[:, 2:3]
     inv = lax.rsqrt(squares / DI + EPS)
     amount = lax.rem(z + (NZ - 2), NZ) * 80
     for block in range(4):
-        part = total(slice(block * HALF, (block + 1) * HALF)) * inv
+        parts = firsts if block < 2 else seconds
+        part = total(parts, slice((block % 2) * HALF, (block % 2 + 1) * HALF)) * inv
         part = pltpu.roll(part, amount, 1)
         at = pl.multiple_of((x ^ block) * HALF, HALF)
         out_ref[:, pl.ds(at, HALF)] = part.astype(BF)
@@ -450,18 +464,22 @@
     r2 = flip(msg4, "x", 2, NX)
     side = flip(side, "z", 1, NZ)
 
-    base, factors, mail = call(
-        local_kernel, place,
-        (
-            queries, key_rows, values, cum, lam_index.reshape(1, TOK), segments.reshape(1, TOK),
-            lam_table.transpose(2, 1, 0), skip_gain.reshape(1, HEADS), got0,
-        ),
-        [shaped(TOK, COLS, dtype=F32), shaped(TOK, LANE, dtype=F32), shaped(3 * TOK, LANE)],
-        flops=3 * 10**8,
-        vmem=12,
-    )
+    half = shaped(TOK, HALF, dtype=F32)
+    factors, mail, levels = call(
+        prep_kernel, place,
+        (queries, cum, lam_index.reshape(1, TOK), lam_table.transpose(2, 1, 0)),
+        [shaped(TOK, LANE, dtype=F32), shaped(3 * TOK, LANE), shaped(3, TOK, LANE, dtype=F32)],
+    )
+    bases = [
+        call(
+            lambda *r, side=side: local_kernel(side, *r), place,
+            (queries, key_rows, values, cum, segments.reshape(1, TOK), levels, skip_gain.reshape(1, HEADS), got0),
+            [half],
+            vmem=6,
+        )[0]
+        for side in range(2)
+    ]
     mail = flip(mail, "core", 1, 2)
-    half = shaped(TOK, HALF, dtype=F32)
     late, p5 = call(lines_kernel, place, (r1, r2, r3, p4), [shaped(HALF, NST), line])
     late_side = flip(late, "z", 1, NZ)
     square = shaped(TOK, LANE, dtype=F32)
@@ -478,18 +496,26 @@
         vmem=8,
     )
     back = flip(back, "core", 1, 2)
-    parts = call(
-        project_kernel, place,
-        (base, own_cross, back, gate_rows, norm_gain.reshape(10, LANE), *own_w, *other_w),
-        [shaped(TOK // NY, 2688)] * NY,
-        scratch=[pltpu.VMEM((TOK, COLS), BF)],
-        flops=10**9,
-        vmem=24,
-    )
-    arrived = [parts[0]]
-    for d in (2, 1, 3):
-        arrived.append(flip(parts[d], "y", d, NY))
-    return call(finish_kernel, place, arrived, [shaped(TOK // NY, 2560)])[0]
+    part = TOK // NY
+    scaled, *firsts = call(
+        first_kernel, place,
+        (*bases, own_cross, back, gate_rows, norm_gain.reshape(10, LANE), *own_w[:4], *other_w[:4]),
+        [shaped(TOK, COLS)] + [shaped(part, 2 * HALF + LANE)] * NY,
+        flops=5 * 10**8,
+        vmem=12,
+    )
+    seconds = call(
+        second_kernel, place, (scaled, *own_w[4:], *other_w[4:]),
+        [shaped(part, 2 * HALF)] * NY,
+        flops=5 * 10**8,
+        vmem=12,
+    )
+    arrived = []
+    for parts in (firsts, seconds):
+        arrived.append(parts[0])
+        for d in (2, 1, 3):
+            arrived.append(flip(parts[d], "y", d, NY))
+    return call(finish_kernel, place, arrived, [shaped(part, 2560)])[0]
 
 
 def solution(mesh):

time: 92.9 us -> 110 us (1.18)
  starting transfers between devices: 30.6 us -> 43.4 us
  waiting for transfers between devices: 39.2 us -> 41.8 us
  Pallas kernels: 18.1 us -> 19.9 us
    ppermute x29 -> x32, starting transfers between devices: 16.4 us -> 30.3 us  [flip(): return lax.ppermute(value, axis, [(i, i ^ mask) for i in range(size)])]
    ppermute x29 -> x32, waiting for transfers between devices: 31.9 us -> 37.7 us  [flip(): return lax.ppermute(value, axis, [(i, i ^ mask) for i in range(size)])]
    ppermute x7, waiting for transfers between devices: 7.36 us -> 4.1 us  [shift(): lax.ppermute(value, axis, [(i, (i + step) % size) for i in range(size)])]
    pallas_call x13 -> x16, Pallas kernels: 18.1 us -> 19.9 us  [call(): pl.pallas_call(body, out_shape=outs, in_specs=[pl.BlockSpec(memory_space=...]
  transfers between devices with their start and end apart: 36 -> 39, of which waited for: 15 -> 17; matrix products, arithmetic and copies ran while one was open for 0% -> 0% of each run, Pallas kernels for 14% -> 16%
where the time goes in v4:
time: 110 us; the launch traced here: 109 us
  starting transfers between devices  43.4 us (39%)
  waiting for transfers between devices  41.8 us (38%)
  Pallas kernels  19.9 us (18%)
  local copies, waits for them, and re-layouts  3.7 us (3%)
    ppermute x32, waiting for transfers between devices, flip(): return lax.ppermute(value, axis, [(i, i ^ mask) for i in range(size)])  37.7 us
    ppermute x32, starting transfers between devices, flip(): return lax.ppermute(value, axis, [(i, i ^ mask) for i in range(size)])  30.3 us
    pallas_call x16, Pallas kernels, call(): pl.pallas_call(body, out_shape=outs, in_specs=[pl.BlockSpec(memory_space=...  19.9 us
    ppermute x7, starting transfers between devices, shift(): lax.ppermute(value, axis, [(i, (i + step) % size) for i in range(size)])  13.1 us
    ppermute x7, waiting for transfers between devices, shift(): lax.ppermute(value, axis, [(i, (i + step) % size) for i in range(size)])  4.1 us
    unnamed x24, local copies, waits for them, and re-layouts  3.7 us
  transfers between devices with their start and end apart: 39, of which 17 were waited for; matrix products, arithmetic and copies ran while one was open for 0% of the time, Pallas kernels for 16%

profile of v4, /device:TPU:6, one launch (start us, length us, event | category | flops | bytes accessed | tf_op | source)
XLA Modules:
  0.0 109.2 jit_solution(10139106180059548993)
XLA Ops:
  2.4 1.9 %shard_map.109 = (bf16[1376,128]{1,0:T(8,128)(2,1)S(1)}, f32[128,128]{1,0:T(8,128)S(1)}) custom-call(s32[4]{0:T(128)S(1)} %pad_add_fusion.place.r_0_, bf16[128,1280]{1,0:T(8,128)(2,1)S(1)} %copy-done, bf16[128,128]{1,0:T(8,128)(2,1)S(1)} %copy-done.4, f32[20,128]{1,0:T(8,128)S(1)} %bitcast.13), custom_call_target="tpu_custom_call" | custom-call | flops 100000000 | bytes 1048576 | tf_op jit(solution)/shard_map/pallas_call | solution.py:31
  4.5 1.6 %collective-permute-done.r_8_.got = bf16[1376,128]{1,0:T(8,128)(2,1)S(1)} collective-permute-done((bf16[1376,128]{1,0:T(8,128)(2,1)S(1)}, bf16[1376,128]{1,0:T(8,128)(2,1)S(1)}, u32[]{:S(2)}, u32[]{:S(2)}) %collective-permute-start) | collective-permute-done | bytes 352288 | tf_op jit(solution)/shard_map/ppermute | solution.py:23
  6.7 2.0 %collective-permute-start.2 = (bf16[688,128]{1,0:T(8,128)(2,1)S(1)}, bf16[688,128]{1,0:T(8,128)(2,1)S(1)}, u32[]{:S(2)}, u32[]{:S(2)}) collective-permute-start(bf16[688,128]{1,0:T(8,128)(2,1)S(1)} %get-tuple-element.42.own), channel_id=1, source_target_pairs={{0,8},{8,0},{16,24},{24,16},{32,40},{40,32},{48,56},{56,48},{1,9},... | collective-permute-start | bytes 528392 | tf_op jit(solution)/shard_map/ppermute | solution.py:23
  8.7 5.0 %collective-permute-start.14 = (bf16[80,640]{1,0:T(8,128)(2,1)S(1)}, bf16[80,640]{1,0:T(8,128)(2,1)S(1)}, u32[]{:S(2)}, u32[]{:S(2)}) collective-permute-start(bf16[80,640]{1,0:T(8,128)(2,1)S(1)} %fusion.c), channel_id=1, source_target_pairs={{0,56},{8,0},{16,8},{24,16},{32,24},{40,32},{48,40},{56,48},{1,57}... | collective-permute-start | bytes 307208 | tf_op jit(solution)/shard_map/ppermute | solution.py:27
  13.7 2.2 %collective-permute-done.14.d = bf16[80,640]{1,0:T(8,128)(2,1)S(1)} collective-permute-done((bf16[80,640]{1,0:T(8,128)(2,1)S(1)}, bf16[80,640]{1,0:T(8,128)(2,1)S(1)}, u32[]{:S(2)}, u32[]{:S(2)}) %collective-permute-start.14) | collective-permute-done | bytes 102432 | tf_op jit(solution)/shard_map/ppermute | solution.py:27
  16.0 3.9 %collective-permute-start.15 = (bf16[80,640]{1,0:T(8,128)(2,1)S(1)}, bf16[80,640]{1,0:T(8,128)(2,1)S(1)}, u32[]{:S(2)}, u32[]{:S(2)}) collective-permute-start(bf16[80,640]{1,0:T(8,128)(2,1)S(1)} %collective-permute-done.14.d), channel_id=1, source_target_pairs={{0,56},{8,0},{16,8},{24,16},{32,24},{40,32},{48,40},{56,48},{1,57}... | collective-permute-start | bytes 307208 | tf_op jit(solution)/shard_map/ppermute | solution.py:27
  22.1 3.6 %collective-permute-start.16 = (bf16[80,640]{1,0:T(8,128)(2,1)S(1)}, bf16[80,640]{1,0:T(8,128)(2,1)S(1)}, u32[]{:S(2)}, u32[]{:S(2)}) collective-permute-start(bf16[80,640]{1,0:T(8,128)(2,1)S(1)} %collective-permute-done.15.a), channel_id=1, source_target_pairs={{0,56},{8,0},{16,8},{24,16},{32,24},{40,32},{48,40},{56,48},{1,57}... | collective-permute-start | bytes 307208 | tf_op jit(solution)/shard_map/ppermute | solution.py:27
  25.7 2.2 %collective-permute-done.3.r_2_.r_4_.got2 = bf16[368,128]{1,0:T(8,128)(2,1)S(1)} collective-permute-done((bf16[368,128]{1,0:T(8,128)(2,1)S(1)}, bf16[368,128]{1,0:T(8,128)(2,1)S(1)}, u32[]{:S(2)}, u32[]{:S(2)}) %collective-permute-start.3) | collective-permute-done | bytes 94240 | tf_op jit(solution)/shard_map/ppermute | solution.py:23
  28.5 3.1 %collective-permute-start.4 = (bf16[368,128]{1,0:T(8,128)(2,1)S(1)}, bf16[368,128]{1,0:T(8,128)(2,1)S(1)}, u32[]{:S(2)}, u32[]{:S(2)}) collective-permute-start(bf16[368,128]{1,0:T(8,128)(2,1)S(1)} %get-tuple-element.46.r_1_), channel_id=1, source_target_pairs={{0,48},{8,56},{16,32},{24,40},{32,16},{40,24},{48,0},{56,8},{1,49}... | collective-permute-start | bytes 282632 | tf_op jit(solution)/shard_map/ppermute | solution.py:23
  37.0 1.4 %collective-permute-done.17.c = bf16[80,640]{1,0:T(8,128)(2,1)S(1)} collective-permute-done((bf16[80,640]{1,0:T(8,128)(2,1)S(1)}, bf16[80,640]{1,0:T(8,128)(2,1)S(1)}, u32[]{:S(2)}, u32[]{:S(2)}) %collective-permute-start.17) | collective-permute-done | bytes 102432 | tf_op jit(solution)/shard_map/ppermute | solution.py:27
  40.5 3.4 %collective-permute-done.5.r1 = bf16[368,128]{1,0:T(8,128)(2,1)S(1)} collective-permute-done((bf16[368,128]{1,0:T(8,128)(2,1)S(1)}, bf16[368,128]{1,0:T(8,128)(2,1)S(1)}, u32[]{:S(2)}, u32[]{:S(2)}) %collective-permute-start.5) | collective-permute-done | bytes 94240 | tf_op jit(solution)/shard_map/ppermute | solution.py:23
  44.0 1.4 %collective-permute-start.6 = (bf16[368,128]{1,0:T(8,128)(2,1)S(1)}, bf16[368,128]{1,0:T(8,128)(2,1)S(1)}, u32[]{:S(2)}, u32[]{:S(2)}) collective-permute-start(bf16[368,128]{1,0:T(8,128)(2,1)S(1)} %get-tuple-element.48), channel_id=1, source_target_pairs={{0,128},{64,192},{128,0},{192,64},{1,129},{65,193},{129,1},{193,65... | collective-permute-start | bytes 282632 | tf_op jit(solution)/shard_map/ppermute | solution.py:23
  45.4 8.9 %collective-permute-done.6.r2 = bf16[368,128]{1,0:T(8,128)(2,1)S(1)} collective-permute-done((bf16[368,128]{1,0:T(8,128)(2,1)S(1)}, bf16[368,128]{1,0:T(8,128)(2,1)S(1)}, u32[]{:S(2)}, u32[]{:S(2)}) %collective-permute-start.6) | collective-permute-done | bytes 94240 | tf_op jit(solution)/shard_map/ppermute | solution.py:23
  54.2 2.1 %collective-permute-start.7 = (bf16[368,128]{1,0:T(8,128)(2,1)S(1)}, bf16[368,128]{1,0:T(8,128)(2,1)S(1)}, u32[]{:S(2)}, u32[]{:S(2)}) collective-permute-start(bf16[368,128]{1,0:T(8,128)(2,1)S(1)} %get-tuple-element.48), channel_id=1, source_target_pairs={{0,192},{64,128},{128,64},{192,0},{1,193},{65,129},{129,65},{193,1... | collective-permute-start | bytes 282632 | tf_op jit(solution)/shard_map/ppermute | solution.py:23
  56.4 3.7 %collective-permute-done.7.r3 = bf16[368,128]{1,0:T(8,128)(2,1)S(1)} collective-permute-done((bf16[368,128]{1,0:T(8,128)(2,1)S(1)}, bf16[368,128]{1,0:T(8,128)(2,1)S(1)}, u32[]{:S(2)}, u32[]{:S(2)}) %collective-permute-start.7) | collective-permute-done | bytes 94240 | tf_op jit(solution)/shard_map/ppermute | solution.py:23
  60.0 1.6 %collective-permute-start.8 = (bf16[640,128]{1,0:T(8,128)(2,1)S(1)}, bf16[640,128]{1,0:T(8,128)(2,1)S(1)}, u32[]{:S(2)}, u32[]{:S(2)}) collective-permute-start(bf16[640,128]{1,0:T(8,128)(2,1)S(1)} %get-tuple-element.50), channel_id=1, source_target_pairs={{0,8},{8,0},{16,24},{24,16},{32,40},{40,32},{48,56},{56,48},{1,9},... | collective-permute-start | bytes 491528 | tf_op jit(solution)/shard_map/ppermute | solution.py:23
  62.9 2.1 %collective-permute-start.31 = (bf16[320,640]{1,0:T(8,128)(2,1)S(1)}, bf16[320,640]{1,0:T(8,128)(2,1)S(1)}, u32[]{:S(2)}, u32[]{:S(2)}) collective-permute-start(bf16[320,640]{1,0:T(8,128)(2,1)S(1)} %shard_map.121.refs_1_), channel_id=1, source_target_pairs={{0,192},{64,128},{128,64},{192,0},{1,193},{65,129},{129,65},{193,1... | collective-permute-start | bytes 1228808 | tf_op jit(solution)/shard_map/ppermute | solution.py:23
  65.5 3.4 %collective-permute-done.9.late_side = bf16[640,128]{1,0:T(8,128)(2,1)S(1)} collective-permute-done((bf16[640,128]{1,0:T(8,128)(2,1)S(1)}, bf16[640,128]{1,0:T(8,128)(2,1)S(1)}, u32[]{:S(2)}, u32[]{:S(2)}) %collective-permute-start.9) | collective-permute-done | bytes 163872 | tf_op jit(solution)/shard_map/ppermute | solution.py:23
  68.9 2.1 %collective-permute-start.30 = (bf16[320,640]{1,0:T(8,128)(2,1)S(1)}, bf16[320,640]{1,0:T(8,128)(2,1)S(1)}, u32[]{:S(2)}, u32[]{:S(2)}) collective-permute-start(bf16[320,640]{1,0:T(8,128)(2,1)S(1)} %collective-permute-done.20.refs_3_), channel_id=1, source_target_pairs={{0,192},{64,128},{128,64},{192,0},{1,193},{65,129},{129,65},{193,1... | collective-permute-start | bytes 1228808 | tf_op jit(solution)/shard_map/ppermute | solution.py:23
  71.0 2.0 %shard_map.118 = (f32[128,640]{1,0:T(8,128)S(1)}, f32[128,640]{1,0:T(8,128)S(1)}, f32[128,128]{1,0:T(8,128)S(1)}, f32[128,128]{1,0:T(8,128)S(1)}) custom-call(s32[4]{0:T(128)S(1)} %pad_add_fusion.place.r_0_, bf16[128,128]{1,0:T(8,128)(2,1)S(1)} %copy-done.2, f32[128,128]{1,0:T(8,128)S(1)} %get-tuple-element.40.factors, ...), custom_call_target="tpu_custom_call" | custom-call | flops 100000000 | bytes 1048576 | tf_op jit(solution)/shard_map/pallas_call | solution.py:31
  73.0 1.5 %shard_map.119 = (f32[128,640]{1,0:T(8,128)S(1)}, bf16[128,640]{1,0:T(8,128)(2,1)S(1)}) custom-call(s32[4]{0:T(128)S(1)} %pad_add_fusion.place.r_0_, bf16[128,128]{1,0:T(8,128)(2,1)S(1)} %copy-done.2, bf16[384,128]{1,0:T(8,128)(2,1)S(1)} %collective-permute-done.1.mail, f32[128,128]{1,0:T(8,128)S(1)} %get-tuple-element.51.own_w, ...), custom_call_target="tpu_custom_call" | custom-call | flops 100000000 | bytes 1048576 | tf_op jit(solution)/shard_map/pallas_call | solution.py:31
  74.6 1.8 %collective-permute-done.31.refs_3_ = bf16[320,640]{1,0:T(8,128)(2,1)S(1)} collective-permute-done((bf16[320,640]{1,0:T(8,128)(2,1)S(1)}, bf16[320,640]{1,0:T(8,128)(2,1)S(1)}, u32[]{:S(2)}, u32[]{:S(2)}) %collective-permute-start.31) | collective-permute-done | bytes 409632 | tf_op jit(solution)/shard_map/ppermute | solution.py:23
  77.9 6.5 %collective-permute-done.30.refs_1_ = bf16[320,640]{1,0:T(8,128)(2,1)S(1)} collective-permute-done((bf16[320,640]{1,0:T(8,128)(2,1)S(1)}, bf16[320,640]{1,0:T(8,128)(2,1)S(1)}, u32[]{:S(2)}, u32[]{:S(2)}) %collective-permute-start.30) | collective-permute-done | bytes 409632 | tf_op jit(solution)/shard_map/ppermute | solution.py:23
  85.0 2.2 %shard_map.112.high = f32[128,640]{1,0:T(8,128)S(1)} custom-call(s32[4]{0:T(128)S(1)} %pad_add_fusion.place.r_0_, bf16[128,128]{1,0:T(8,128)(2,1)S(1)} %copy-done.2, bf16[128,128]{1,0:T(8,128)(2,1)S(1)} %copy-done.4, bf16[128,1280]{1,0:T(8,128)(2,1)S(1)} %copy-done.1, f32[128,128]{1,0:T(8,128)S(1)} %get-tuple-element.36.cum_ref.r_4_, s32[1,128]{1,0:T(1,128)S(1)} %bitcast.15, ...), custom_call_target="tpu_custom_call" | custom-call | flops 100000000 | bytes 1048576 | tf_op jit(solution)/shard_map/pallas_call | solution.py:31
  87.3 2.3 %shard_map.111.low = f32[128,640]{1,0:T(8,128)S(1)} custom-call(s32[4]{0:T(128)S(1)} %pad_add_fusion.place.r_0_, bf16[128,128]{1,0:T(8,128)(2,1)S(1)} %copy-done.2, bf16[128,128]{1,0:T(8,128)(2,1)S(1)} %copy-done.4, bf16[128,1280]{1,0:T(8,128)(2,1)S(1)} %copy-done.1, f32[128,128]{1,0:T(8,128)S(1)} %get-tuple-element.36.cum_ref.r_4_, s32[1,128]{1,0:T(1,128)S(1)} %bitcast.16, ...), custom_call_target="tpu_custom_call" | custom-call | flops 100000000 | bytes 1048576 | tf_op jit(solution)/shard_map/pallas_call | solution.py:31
  89.6 2.4 %shard_map.122 = (bf16[128,1280]{1,0:T(8,128)(2,1)S(1)}, bf16[32,1408]{1,0:T(8,128)(2,1)S(1)}, bf16[32,1408]{1,0:T(8,128)(2,1)S(1)}, bf16[32,1408]{1,0:T(8,128)(2,1)S(1)}, bf16[32,1408]{1,0:T(8,128)(2,1)S(1)}) custom-call(s32[4]{0:T(128)S(1)} %pad_add_fusion.place.r_0_, f32[128,640]{1,0:T(8,128)S(1)} %shard_map.111.low, f32[128,640]{1,0:T(8,128)S(1)} %shard_map.112.high, ...), custom_call_target="tpu_custom_call" | custom-call | flops 500000000 | bytes 1048576 | tf_op jit(solution)/shard_map/pallas_call | solution.py:31
  92.0 3.3 %collective-permute-start.25 = (bf16[32,1408]{1,0:T(8,128)(2,1)S(1)}, bf16[32,1408]{1,0:T(8,128)(2,1)S(1)}, u32[]{:S(2)}, u32[]{:S(2)}) collective-permute-start(bf16[32,1408]{1,0:T(8,128)(2,1)S(1)} %get-tuple-element.59), channel_id=1, source_target_pairs={{0,2},{1,3},{2,0},{3,1},{4,6},{5,7},{6,4},{7,5},{8,10},{9,11},{10,... | collective-permute-start | bytes 270344 | tf_op jit(solution)/shard_map/ppermute | solution.py:23
  96.4 1.9 %shard_map.123 = (bf16[32,1280]{1,0:T(8,128)(2,1)S(1)}, bf16[32,1280]{1,0:T(8,128)(2,1)S(1)}, bf16[32,1280]{1,0:T(8,128)(2,1)S(1)}, bf16[32,1280]{1,0:T(8,128)(2,1)S(1)}) custom-call(s32[4]{0:T(128)S(1)} %pad_add_fusion.place.r_0_, bf16[128,1280]{1,0:T(8,128)(2,1)S(1)} %get-tuple-element.62.y_ref, bf16[320,640]{1,0:T(8,128)(2,1)S(1)} %collective-permute-done.29.refs_0_, ...), custom_call_target="tpu_custom_call" | custom-call | flops 500000000 | bytes 1048576 | tf_op jit(solution)/shard_map/pallas_call | solution.py:31
  98.3 3.0 %collective-permute-start.36 = (bf16[32,1280]{1,0:T(8,128)(2,1)S(1)}, bf16[32,1280]{1,0:T(8,128)(2,1)S(1)}, u32[]{:S(2)}, u32[]{:S(2)}) collective-permute-start(bf16[32,1280]{1,0:T(8,128)(2,1)S(1)} %get-tuple-element.64), channel_id=1, source_target_pairs={{0,2},{1,3},{2,0},{3,1},{4,6},{5,7},{6,4},{7,5},{8,10},{9,11},{10,... | collective-permute-start | bytes 245768 | tf_op jit(solution)/shard_map/ppermute | solution.py:23
  102.5 2.4 %collective-permute-done.36.refs_5_ = bf16[32,1280]{1,0:T(8,128)(2,1)S(1)} collective-permute-done((bf16[32,1280]{1,0:T(8,128)(2,1)S(1)}, bf16[32,1280]{1,0:T(8,128)(2,1)S(1)}, u32[]{:S(2)}, u32[]{:S(2)}) %collective-permute-start.36) | collective-permute-done | bytes 81952 | tf_op jit(solution)/shard_map/ppermute | solution.py:23
  106.0 1.7 %collective-permute-done.38.refs_7_ = bf16[32,1280]{1,0:T(8,128)(2,1)S(1)} collective-permute-done((bf16[32,1280]{1,0:T(8,128)(2,1)S(1)}, bf16[32,1280]{1,0:T(8,128)(2,1)S(1)}, u32[]{:S(2)}, u32[]{:S(2)}) %collective-permute-start.38) | collective-permute-done | bytes 81952 | tf_op jit(solution)/shard_map/ppermute | solution.py:23
  107.7 1.5 %shard_map.124 = bf16[32,2560]{1,0:T(8,128)(2,1)} custom-call(s32[4]{0:T(128)S(1)} %pad_add_fusion.place.r_0_, bf16[32,1408]{1,0:T(8,128)(2,1)S(1)} %get-tuple-element.58.refs_0_, bf16[32,1408]{1,0:T(8,128)(2,1)S(1)} %collective-permute-done.25.refs_1_, bf16[32,1408]{1,0:T(8,128)(2,1)S(1)} %collective-permute-done.26.refs_2_, ...), custom_call_target="tpu_custom_call" | custom-call | flops 100000000 | bytes 1048576 | tf_op jit(solution)/shard_map/pallas_call | solution.py:31
  (89 shorter events, 20.9 us)
Async XLA Ops:
  6.7 13.2 %collective-permute-start.2 = (bf16[688,128]{1,0:T(8,128)(2,1)S(1)}, bf16[688,128]{1,0:T(8,128)(2,1)S(1)}, u32[]{:S(2)}, u32[]{:S(2)}) collective-permute-start(bf16[688,128]{1,0:T(8,128)(2,1)S(1)} %get-tuple-element.42.own), channel_id=1, source_target_pairs={{0,8},{8,0},{16,24},{24,16},{32,40},{40,32},{48,56},{56,48},{1,9},... | collective-permute-start | bytes 528392 | tf_op jit(solution)/shard_map/ppermute | solution.py:23
  8.7 7.3 %collective-permute-start.14 = (bf16[80,640]{1,0:T(8,128)(2,1)S(1)}, bf16[80,640]{1,0:T(8,128)(2,1)S(1)}, u32[]{:S(2)}, u32[]{:S(2)}) collective-permute-start(bf16[80,640]{1,0:T(8,128)(2,1)S(1)} %fusion.c), channel_id=1, source_target_pairs={{0,56},{8,0},{16,8},{24,16},{32,24},{40,32},{48,40},{56,48},{1,57}... | collective-permute-start | bytes 307208 | tf_op jit(solution)/shard_map/ppermute | solution.py:27
  13.7 6.1 %collective-permute-start.12 = (bf16[80,640]{1,0:T(8,128)(2,1)S(1)}, bf16[80,640]{1,0:T(8,128)(2,1)S(1)}, u32[]{:S(2)}, u32[]{:S(2)}) collective-permute-start(bf16[80,640]{1,0:T(8,128)(2,1)S(1)} %fusion.c), channel_id=1, source_target_pairs={{0,8},{8,16},{16,24},{24,32},{32,40},{40,48},{48,56},{56,0},{1,9},... | collective-permute-start | bytes 307208 | tf_op jit(solution)/shard_map/ppermute | solution.py:27
  16.0 6.1 %collective-permute-start.15 = (bf16[80,640]{1,0:T(8,128)(2,1)S(1)}, bf16[80,640]{1,0:T(8,128)(2,1)S(1)}, u32[]{:S(2)}, u32[]{:S(2)}) collective-permute-start(bf16[80,640]{1,0:T(8,128)(2,1)S(1)} %collective-permute-done.14.d), channel_id=1, source_target_pairs={{0,56},{8,0},{16,8},{24,16},{32,24},{40,32},{48,40},{56,48},{1,57}... | collective-permute-start | bytes 307208 | tf_op jit(solution)/shard_map/ppermute | solution.py:27
  19.9 5.9 %collective-permute-start.13 = (bf16[80,640]{1,0:T(8,128)(2,1)S(1)}, bf16[80,640]{1,0:T(8,128)(2,1)S(1)}, u32[]{:S(2)}, u32[]{:S(2)}) collective-permute-start(bf16[80,640]{1,0:T(8,128)(2,1)S(1)} %collective-permute-done.12.b), channel_id=1, source_target_pairs={{0,8},{8,16},{16,24},{24,32},{32,40},{40,48},{48,56},{56,0},{1,9},... | collective-permute-start | bytes 307208 | tf_op jit(solution)/shard_map/ppermute | solution.py:27
  20.5 7.5 %collective-permute-start.3 = (bf16[368,128]{1,0:T(8,128)(2,1)S(1)}, bf16[368,128]{1,0:T(8,128)(2,1)S(1)}, u32[]{:S(2)}, u32[]{:S(2)}) collective-permute-start(bf16[368,128]{1,0:T(8,128)(2,1)S(1)} %get-tuple-element.44.r_1_), channel_id=1, source_target_pairs={{0,16},{8,24},{16,0},{24,8},{32,48},{40,56},{48,32},{56,40},{1,17}... | collective-permute-start | bytes 282632 | tf_op jit(solution)/shard_map/ppermute | solution.py:23
  22.1 10.5 %collective-permute-start.16 = (bf16[80,640]{1,0:T(8,128)(2,1)S(1)}, bf16[80,640]{1,0:T(8,128)(2,1)S(1)}, u32[]{:S(2)}, u32[]{:S(2)}) collective-permute-start(bf16[80,640]{1,0:T(8,128)(2,1)S(1)} %collective-permute-done.15.a), channel_id=1, source_target_pairs={{0,56},{8,0},{16,8},{24,16},{32,24},{40,32},{48,40},{56,48},{1,57}... | collective-permute-start | bytes 307208 | tf_op jit(solution)/shard_map/ppermute | solution.py:27
  25.7 9.2 %collective-permute-start.18 = (bf16[80,640]{1,0:T(8,128)(2,1)S(1)}, bf16[80,640]{1,0:T(8,128)(2,1)S(1)}, u32[]{:S(2)}, u32[]{:S(2)}) collective-permute-start(bf16[80,640]{1,0:T(8,128)(2,1)S(1)} %collective-permute-done.13.a), channel_id=1, source_target_pairs={{0,8},{8,16},{16,24},{24,32},{32,40},{40,48},{48,56},{56,0},{1,9},... | collective-permute-start | bytes 307208 | tf_op jit(solution)/shard_map/ppermute | solution.py:27
  28.5 6.9 %collective-permute-start.4 = (bf16[368,128]{1,0:T(8,128)(2,1)S(1)}, bf16[368,128]{1,0:T(8,128)(2,1)S(1)}, u32[]{:S(2)}, u32[]{:S(2)}) collective-permute-start(bf16[368,128]{1,0:T(8,128)(2,1)S(1)} %get-tuple-element.46.r_1_), channel_id=1, source_target_pairs={{0,48},{8,56},{16,32},{24,40},{32,16},{40,24},{48,0},{56,8},{1,49}... | collective-permute-start | bytes 282632 | tf_op jit(solution)/shard_map/ppermute | solution.py:23
  31.7 30.5 %collective-permute-start.19 = (bf16[320,640]{1,0:T(8,128)(2,1)S(1)}, bf16[320,640]{1,0:T(8,128)(2,1)S(1)}, u32[]{:S(2)}, u32[]{:S(2)}) collective-permute-start(bf16[320,640]{1,0:T(8,128)(2,1)S(1)} %shard_map.120.refs_0_), channel_id=1, source_target_pairs={{0,64},{64,0},{128,192},{192,128},{1,65},{65,1},{129,193},{193,129... | collective-permute-start | bytes 1228808 | tf_op jit(solution)/shard_map/ppermute | solution.py:23
  32.6 29.7 %collective-permute-start.21 = (bf16[320,640]{1,0:T(8,128)(2,1)S(1)}, bf16[320,640]{1,0:T(8,128)(2,1)S(1)}, u32[]{:S(2)}, u32[]{:S(2)}) collective-permute-start(bf16[320,640]{1,0:T(8,128)(2,1)S(1)} %shard_map.120.refs_0_), channel_id=1, source_target_pairs={{0,4},{4,0},{1,5},{5,1},{2,6},{6,2},{3,7},{7,3},{8,12},{12,8},{9,1... | collective-permute-start | bytes 1228808 | tf_op jit(solution)/shard_map/ppermute | solution.py:23
  32.6 5.8 %collective-permute-start.17 = (bf16[80,640]{1,0:T(8,128)(2,1)S(1)}, bf16[80,640]{1,0:T(8,128)(2,1)S(1)}, u32[]{:S(2)}, u32[]{:S(2)}) collective-permute-start(bf16[80,640]{1,0:T(8,128)(2,1)S(1)} %collective-permute-done.16.b), channel_id=1, source_target_pairs={{0,56},{8,0},{16,8},{24,16},{32,24},{40,32},{48,40},{56,48},{1,57}... | collective-permute-start | bytes 307208 | tf_op jit(solution)/shard_map/ppermute | solution.py:27
  35.4 27.4 %collective-permute-start.28 = (bf16[320,640]{1,0:T(8,128)(2,1)S(1)}, bf16[320,640]{1,0:T(8,128)(2,1)S(1)}, u32[]{:S(2)}, u32[]{:S(2)}) collective-permute-start(bf16[320,640]{1,0:T(8,128)(2,1)S(1)} %shard_map.120.refs_0_), channel_id=1, source_target_pairs={{0,192},{64,128},{128,64},{192,0},{1,193},{65,129},{129,65},{193,1... | collective-permute-start | bytes 1228808 | tf_op jit(solution)/shard_map/ppermute | solution.py:23
  39.4 26.1 %collective-permute-start.20 = (bf16[320,640]{1,0:T(8,128)(2,1)S(1)}, bf16[320,640]{1,0:T(8,128)(2,1)S(1)}, u32[]{:S(2)}, u32[]{:S(2)}) collective-permute-start(bf16[320,640]{1,0:T(8,128)(2,1)S(1)} %shard_map.121.refs_1_), channel_id=1, source_target_pairs={{0,64},{64,0},{128,192},{192,128},{1,65},{65,1},{129,193},{193,129... | collective-permute-start | bytes 1228808 | tf_op jit(solution)/shard_map/ppermute | solution.py:23
  44.0 10.3 %collective-permute-start.6 = (bf16[368,128]{1,0:T(8,128)(2,1)S(1)}, bf16[368,128]{1,0:T(8,128)(2,1)S(1)}, u32[]{:S(2)}, u32[]{:S(2)}) collective-permute-start(bf16[368,128]{1,0:T(8,128)(2,1)S(1)} %get-tuple-element.48), channel_id=1, source_target_pairs={{0,128},{64,192},{128,0},{192,64},{1,129},{65,193},{129,1},{193,65... | collective-permute-start | bytes 282632 | tf_op jit(solution)/shard_map/ppermute | solution.py:23
  54.2 5.8 %collective-permute-start.7 = (bf16[368,128]{1,0:T(8,128)(2,1)S(1)}, bf16[368,128]{1,0:T(8,128)(2,1)S(1)}, u32[]{:S(2)}, u32[]{:S(2)}) collective-permute-start(bf16[368,128]{1,0:T(8,128)(2,1)S(1)} %get-tuple-element.48), channel_id=1, source_target_pairs={{0,192},{64,128},{128,64},{192,0},{1,193},{65,129},{129,65},{193,1... | collective-permute-start | bytes 282632 | tf_op jit(solution)/shard_map/ppermute | solution.py:23
  62.2 12.3 %collective-permute-start.22 = (bf16[320,640]{1,0:T(8,128)(2,1)S(1)}, bf16[320,640]{1,0:T(8,128)(2,1)S(1)}, u32[]{:S(2)}, u32[]{:S(2)}) collective-permute-start(bf16[320,640]{1,0:T(8,128)(2,1)S(1)} %shard_map.121.refs_1_), channel_id=1, source_target_pairs={{0,4},{4,0},{1,5},{5,1},{2,6},{6,2},{3,7},{7,3},{8,12},{12,8},{9,1... | collective-permute-start | bytes 1228808 | tf_op jit(solution)/shard_map/ppermute | solution.py:23
  62.3 6.6 %collective-permute-start.9 = (bf16[640,128]{1,0:T(8,128)(2,1)S(1)}, bf16[640,128]{1,0:T(8,128)(2,1)S(1)}, u32[]{:S(2)}, u32[]{:S(2)}) collective-permute-start(bf16[640,128]{1,0:T(8,128)(2,1)S(1)} %get-tuple-element.53.late), channel_id=1, source_target_pairs={{0,8},{8,0},{16,24},{24,16},{32,40},{40,32},{48,56},{56,48},{1,9},... | collective-permute-start | bytes 491528 | tf_op jit(solution)/shard_map/ppermute | solution.py:23
  62.9 13.6 %collective-permute-start.31 = (bf16[320,640]{1,0:T(8,128)(2,1)S(1)}, bf16[320,640]{1,0:T(8,128)(2,1)S(1)}, u32[]{:S(2)}, u32[]{:S(2)}) collective-permute-start(bf16[320,640]{1,0:T(8,128)(2,1)S(1)} %shard_map.121.refs_1_), channel_id=1, source_target_pairs={{0,192},{64,128},{128,64},{192,0},{1,193},{65,129},{129,65},{193,1... | collective-permute-start | bytes 1228808 | tf_op jit(solution)/shard_map/ppermute | solution.py:23
  65.5 10.9 %collective-permute-start.23 = (bf16[320,640]{1,0:T(8,128)(2,1)S(1)}, bf16[320,640]{1,0:T(8,128)(2,1)S(1)}, u32[]{:S(2)}, u32[]{:S(2)}) collective-permute-start(bf16[320,640]{1,0:T(8,128)(2,1)S(1)} %collective-permute-done.19.refs_2_), channel_id=1, source_target_pairs={{0,4},{4,0},{1,5},{5,1},{2,6},{6,2},{3,7},{7,3},{8,12},{12,8},{9,1... | collective-permute-start | bytes 1228808 | tf_op jit(solution)/shard_map/ppermute | solution.py:23
  65.5 11.9 %collective-permute-start.29 = (bf16[320,640]{1,0:T(8,128)(2,1)S(1)}, bf16[320,640]{1,0:T(8,128)(2,1)S(1)}, u32[]{:S(2)}, u32[]{:S(2)}) collective-permute-start(bf16[320,640]{1,0:T(8,128)(2,1)S(1)} %collective-permute-done.28.refs_2_), channel_id=1, source_target_pairs={{0,64},{64,0},{128,192},{192,128},{1,65},{65,1},{129,193},{193,129... | collective-permute-start | bytes 1228808 | tf_op jit(solution)/shard_map/ppermute | solution.py:23
  68.9 15.5 %collective-permute-start.30 = (bf16[320,640]{1,0:T(8,128)(2,1)S(1)}, bf16[320,640]{1,0:T(8,128)(2,1)S(1)}, u32[]{:S(2)}, u32[]{:S(2)}) collective-permute-start(bf16[320,640]{1,0:T(8,128)(2,1)S(1)} %collective-permute-done.20.refs_3_), channel_id=1, source_target_pairs={{0,192},{64,128},{128,64},{192,0},{1,193},{65,129},{129,65},{193,1... | collective-permute-start | bytes 1228808 | tf_op jit(solution)/shard_map/ppermute | solution.py:23
  76.4 13.2 %collective-permute-start.24 = (bf16[320,640]{1,0:T(8,128)(2,1)S(1)}, bf16[320,640]{1,0:T(8,128)(2,1)S(1)}, u32[]{:S(2)}, u32[]{:S(2)}) collective-permute-start(bf16[320,640]{1,0:T(8,128)(2,1)S(1)} %collective-permute-done.20.refs_3_), channel_id=1, source_target_pairs={{0,4},{4,0},{1,5},{5,1},{2,6},{6,2},{3,7},{7,3},{8,12},{12,8},{9,1... | collective-permute-start | bytes 1228808 | tf_op jit(solution)/shard_map/ppermute | solution.py:23
  76.4 18.8 %collective-permute-start.34 = (bf16[320,640]{1,0:T(8,128)(2,1)S(1)}, bf16[320,640]{1,0:T(8,128)(2,1)S(1)}, u32[]{:S(2)}, u32[]{:S(2)}) collective-permute-start(bf16[320,640]{1,0:T(8,128)(2,1)S(1)} %collective-permute-done.28.refs_2_), channel_id=1, source_target_pairs={{0,4},{4,0},{1,5},{5,1},{2,6},{6,2},{3,7},{7,3},{8,12},{12,8},{9,1... | collective-permute-start | bytes 1228808 | tf_op jit(solution)/shard_map/ppermute | solution.py:23
  77.4 18.6 %collective-permute-start.35 = (bf16[320,640]{1,0:T(8,128)(2,1)S(1)}, bf16[320,640]{1,0:T(8,128)(2,1)S(1)}, u32[]{:S(2)}, u32[]{:S(2)}) collective-permute-start(bf16[320,640]{1,0:T(8,128)(2,1)S(1)} %collective-permute-done.31.refs_3_), channel_id=1, source_target_pairs={{0,4},{4,0},{1,5},{5,1},{2,6},{6,2},{3,7},{7,3},{8,12},{12,8},{9,1... | collective-permute-start | bytes 1228808 | tf_op jit(solution)/shard_map/ppermute | solution.py:23
  77.4 19.0 %collective-permute-start.32 = (bf16[320,640]{1,0:T(8,128)(2,1)S(1)}, bf16[320,640]{1,0:T(8,128)(2,1)S(1)}, u32[]{:S(2)}, u32[]{:S(2)}) collective-permute-start(bf16[320,640]{1,0:T(8,128)(2,1)S(1)} %collective-permute-done.29.refs_0_), channel_id=1, source_target_pairs={{0,4},{4,0},{1,5},{5,1},{2,6},{6,2},{3,7},{7,3},{8,12},{12,8},{9,1... | collective-permute-start | bytes 1228808 | tf_op jit(solution)/shard_map/ppermute | solution.py:23
  84.3 12.1 %collective-permute-start.33 = (bf16[320,640]{1,0:T(8,128)(2,1)S(1)}, bf16[320,640]{1,0:T(8,128)(2,1)S(1)}, u32[]{:S(2)}, u32[]{:S(2)}) collective-permute-start(bf16[320,640]{1,0:T(8,128)(2,1)S(1)} %collective-permute-done.30.refs_1_), channel_id=1, source_target_pairs={{0,4},{4,0},{1,5},{5,1},{2,6},{6,2},{3,7},{7,3},{8,12},{12,8},{9,1... | collective-permute-start | bytes 1228808 | tf_op jit(solution)/shard_map/ppermute | solution.py:23
  92.0 10.1 %collective-permute-start.25 = (bf16[32,1408]{1,0:T(8,128)(2,1)S(1)}, bf16[32,1408]{1,0:T(8,128)(2,1)S(1)}, u32[]{:S(2)}, u32[]{:S(2)}) collective-permute-start(bf16[32,1408]{1,0:T(8,128)(2,1)S(1)} %get-tuple-element.59), channel_id=1, source_target_pairs={{0,2},{1,3},{2,0},{3,1},{4,6},{5,7},{6,4},{7,5},{8,10},{9,11},{10,... | collective-permute-start | bytes 270344 | tf_op jit(solution)/shard_map/ppermute | solution.py:23
  95.2 7.3 %collective-permute-start.26 = (bf16[32,1408]{1,0:T(8,128)(2,1)S(1)}, bf16[32,1408]{1,0:T(8,128)(2,1)S(1)}, u32[]{:S(2)}, u32[]{:S(2)}) collective-permute-start(bf16[32,1408]{1,0:T(8,128)(2,1)S(1)} %get-tuple-element.60), channel_id=1, source_target_pairs={{0,1},{1,0},{2,3},{3,2},{4,5},{5,4},{6,7},{7,6},{8,9},{9,8},{10,11... | collective-permute-start | bytes 270344 | tf_op jit(solution)/shard_map/ppermute | solution.py:23
  95.9 6.6 %collective-permute-start.27 = (bf16[32,1408]{1,0:T(8,128)(2,1)S(1)}, bf16[32,1408]{1,0:T(8,128)(2,1)S(1)}, u32[]{:S(2)}, u32[]{:S(2)}) collective-permute-start(bf16[32,1408]{1,0:T(8,128)(2,1)S(1)} %get-tuple-element.61), channel_id=1, source_target_pairs={{0,3},{1,2},{2,1},{3,0},{4,7},{5,6},{6,5},{7,4},{8,11},{9,10},{10,... | collective-permute-start | bytes 270344 | tf_op jit(solution)/shard_map/ppermute | solution.py:23
  98.3 6.6 %collective-permute-start.36 = (bf16[32,1280]{1,0:T(8,128)(2,1)S(1)}, bf16[32,1280]{1,0:T(8,128)(2,1)S(1)}, u32[]{:S(2)}, u32[]{:S(2)}) collective-permute-start(bf16[32,1280]{1,0:T(8,128)(2,1)S(1)} %get-tuple-element.64), channel_id=1, source_target_pairs={{0,2},{1,3},{2,0},{3,1},{4,6},{5,7},{6,4},{7,5},{8,10},{9,11},{10,... | collective-permute-start | bytes 245768 | tf_op jit(solution)/shard_map/ppermute | solution.py:23
  102.0 5.7 %collective-permute-start.38 = (bf16[32,1280]{1,0:T(8,128)(2,1)S(1)}, bf16[32,1280]{1,0:T(8,128)(2,1)S(1)}, u32[]{:S(2)}, u32[]{:S(2)}) collective-permute-start(bf16[32,1280]{1,0:T(8,128)(2,1)S(1)} %get-tuple-element.66), channel_id=1, source_target_pairs={{0,3},{1,2},{2,1},{3,0},{4,7},{5,6},{6,5},{7,4},{8,11},{9,10},{10,... | collective-permute-start | bytes 245768 | tf_op jit(solution)/shard_map/ppermute | solution.py:23
  (19 other events, 60.7 us)

commit v5 on v2

--- a/solution.py
+++ b/solution.py
@@ -169,14 +169,10 @@
         ).astype(BF)
 
 
-def local_kernel(
-    place, queries, keys, values, cum_ref, lam_index, segments, lam_table, skip, got, base, factors, mail
-):
+def prep_kernel(place, queries, cum_ref, lam_index, lam_table, factors, mail, levels):
     core = place[0]
-    row, lane = rows(), lanes()
-    cum = cum_ref[...]
-    cum_t = cum.T
-    grow = jnp.exp(cum)
+    lane = lanes()
+    grow = jnp.exp(cum_ref[...])
     picks = lax.broadcasted_iota(I32, (64, TOK), 0)
     onehot = (picks == lam_index[...]).astype(F32).astype(BF)
 
@@ -211,14 +207,22 @@
     mail[TOK : 2 * TOK, :] = hi
     mail[2 * TOK :, :] = (theirs - hi.astype(F32)).astype(BF)
 
-    zero_level = jnp.where(core == 1, level(2) * grow, 0.0)
-    near, far = level(0), level(1)
+    levels[0] = level(0)
+    levels[1] = level(1)
+    levels[2] = jnp.where(core == 1, level(2) * grow, 0.0)
+
+
+def local_kernel(side, place, queries, keys, values, cum_ref, segments, levels, skip, got, base):
+    row, lane = rows(), lanes()
+    cum = cum_ref[...]
+    cum_t = cum.T
+    near, far, zero_level = levels[0], levels[1], levels[2]
     q = queries[...]
     scores = lax.dot_general(q, keys[...], NT, preferred_element_type=F32)
     seg_row = jnp.broadcast_to(segments[...].astype(F32), (TOK, LANE))
     same = seg_row == seg_row.T
     causal = row >= lane
-    for p in range(10):
+    for p in range(side * 5, side * 5 + 5):
         cols = slice(p * LANE, (p + 1) * LANE)
         pieces = []
         for h in (2 * p, 2 * p + 1):
@@ -231,7 +235,8 @@
         read = lax.dot_general(q, got[cols, :], NT, preferred_element_type=F32)
         read = read * two_heads(zero_level[:, 2 * p : 2 * p + 1], zero_level[:, 2 * p + 1 : 2 * p + 2], lane)
         gain = two_heads(skip[:, 2 * p : 2 * p + 1], skip[:, 2 * p + 1 : 2 * p + 2], lane)
-        base[:, cols] = jnp.concatenate(pieces, axis=1) + read + gain * values[:, cols].astype(F32)
+        out = slice((p % 5) * LANE, (p % 5) * LANE + LANE)
+        base[:, out] = jnp.concatenate(pieces, axis=1) + read + gain * values[:, cols].astype(F32)
 
 
 def level_weights(place, factors, mail, first_total, prefixes):
@@ -319,7 +324,7 @@
     )
 
 
-def project_kernel(place, base, own, back, gate, gain, *refs):
+def project_kernel(place, low, high, own, back, gate, gain, *refs):
     core, y = place[0], place[1]
     w_refs, out_refs, y_ref = refs[:16], refs[16:20], refs[20]
     part = TOK // NY
@@ -329,7 +334,7 @@
         cols = slice(p * LANE, (p + 1) * LANE)
         inner = slice((p % 5) * LANE, (p % 5) * LANE + LANE)
         cross = jnp.where(core == p // 5, own[:, inner], back[:, inner].astype(F32))
-        gated = base[:, cols] + cross
+        gated = (low if p < 5 else high)[:, inner] + cross
         v = gate[:, cols].astype(F32)
         gated = gated * (v / (1.0 + jnp.exp(-v)))
         squares = squares + gated * gated
@@ -450,18 +455,22 @@
     r2 = flip(msg4, "x", 2, NX)
     side = flip(side, "z", 1, NZ)
 
-    base, factors, mail = call(
-        local_kernel, place,
-        (
-            queries, key_rows, values, cum, lam_index.reshape(1, TOK), segments.reshape(1, TOK),
-            lam_table.transpose(2, 1, 0), skip_gain.reshape(1, HEADS), got0,
-        ),
-        [shaped(TOK, COLS, dtype=F32), shaped(TOK, LANE, dtype=F32), shaped(3 * TOK, LANE)],
-        flops=3 * 10**8,
-        vmem=12,
-    )
+    half = shaped(TOK, HALF, dtype=F32)
+    factors, mail, levels = call(
+        prep_kernel, place,
+        (queries, cum, lam_index.reshape(1, TOK), lam_table.transpose(2, 1, 0)),
+        [shaped(TOK, LANE, dtype=F32), shaped(3 * TOK, LANE), shaped(3, TOK, LANE, dtype=F32)],
+    )
+    bases = [
+        call(
+            lambda *r, side=side: local_kernel(side, *r), place,
+            (queries, key_rows, values, cum, segments.reshape(1, TOK), levels, skip_gain.reshape(1, HEADS), got0),
+            [half],
+            vmem=6,
+        )[0]
+        for side in range(2)
+    ]
     mail = flip(mail, "core", 1, 2)
-    half = shaped(TOK, HALF, dtype=F32)
     late, p5 = call(lines_kernel, place, (r1, r2, r3, p4), [shaped(HALF, NST), line])
     late_side = flip(late, "z", 1, NZ)
     square = shaped(TOK, LANE, dtype=F32)
@@ -480,7 +489,7 @@
     back = flip(back, "core", 1, 2)
     parts = call(
         project_kernel, place,
-        (base, own_cross, back, gate_rows, norm_gain.reshape(10, LANE), *own_w, *other_w),
+        (*bases, own_cross, back, gate_rows, norm_gain.reshape(10, LANE), *own_w, *other_w),
         [shaped(TOK // NY, 2688)] * NY,
         scratch=[pltpu.VMEM((TOK, COLS), BF)],
         flops=10**9,

time: 92.9 us -> 95.8 us (1.031)
  the two profiles are of different devices: /device:TPU:6 before, /device:TPU:1 now
where the time goes in v5:
time: 95.8 us; the launch traced here: 95.5 us
  starting transfers between devices  43.8 us (46%)
  waiting for transfers between devices  29 us (30%)
  Pallas kernels  19.3 us (20%)
  local copies, waits for them, and re-layouts  3.01 us (3%)
    ppermute x29, starting transfers between devices, flip(): return lax.ppermute(value, axis, [(i, i ^ mask) for i in range(size)])  33.1 us
    ppermute x29, waiting for transfers between devices, flip(): return lax.ppermute(value, axis, [(i, i ^ mask) for i in range(size)])  22.7 us
    pallas_call x15, Pallas kernels, call(): pl.pallas_call(body, out_shape=outs, in_specs=[pl.BlockSpec(memory_space=...  19.3 us
    ppermute x7, starting transfers between devices, shift(): lax.ppermute(value, axis, [(i, (i + step) % size) for i in range(size)])  10.7 us
    ppermute x7, waiting for transfers between devices, shift(): lax.ppermute(value, axis, [(i, (i + step) % size) for i in range(size)])  6.25 us
    unnamed x24, local copies, waits for them, and re-layouts  3.01 us
  transfers between devices with their start and end apart: 36, of which 13 were waited for; matrix products, arithmetic and copies ran while one was open for 0% of the time, Pallas kernels for 15%

profile of v5, /device:TPU:1, one launch (start us, length us, event | category | flops | bytes accessed | tf_op | source)
XLA Modules:
  0.0 95.5 jit_solution(13362761033521757865)
XLA Ops:
  0.0 3.2 %collective-permute-start.11 = (bf16[40,1280]{1,0:T(8,128)(2,1)}, bf16[40,1280]{1,0:T(8,128)(2,1)S(1)}, u32[]{:S(2)}, u32[]{:S(2)}) collective-permute-start(bf16[40,1280]{1,0:T(8,128)(2,1)} %bitcast.21), channel_id=1, source_target_pairs={{0,4},{4,0},{1,5},{5,1},{2,6},{6,2},{3,7},{7,3},{8,12},{12,8},{9,1... | collective-permute-start | bytes 307208 | tf_op jit(solution)/shard_map/ppermute | solution.py:23
  5.0 1.9 %shard_map.109 = (bf16[1376,128]{1,0:T(8,128)(2,1)S(1)}, f32[128,128]{1,0:T(8,128)S(1)}) custom-call(s32[4]{0:T(128)S(1)} %pad_add_fusion.place.r_0_, bf16[128,1280]{1,0:T(8,128)(2,1)S(1)} %copy-done, bf16[128,128]{1,0:T(8,128)(2,1)S(1)} %copy-done.4, f32[20,128]{1,0:T(8,128)S(1)} %bitcast.13), custom_call_target="tpu_custom_call" | custom-call | flops 100000000 | bytes 1048576 | tf_op jit(solution)/shard_map/pallas_call | solution.py:31
  7.7 3.9 %collective-permute-start.14 = (bf16[80,640]{1,0:T(8,128)(2,1)S(1)}, bf16[80,640]{1,0:T(8,128)(2,1)S(1)}, u32[]{:S(2)}, u32[]{:S(2)}) collective-permute-start(bf16[80,640]{1,0:T(8,128)(2,1)S(1)} %fusion.c), channel_id=1, source_target_pairs={{0,56},{8,0},{16,8},{24,16},{32,24},{40,32},{48,40},{56,48},{1,57}... | collective-permute-start | bytes 307208 | tf_op jit(solution)/shard_map/ppermute | solution.py:27
  12.3 1.5 %collective-permute-done.14.d = bf16[80,640]{1,0:T(8,128)(2,1)S(1)} collective-permute-done((bf16[80,640]{1,0:T(8,128)(2,1)S(1)}, bf16[80,640]{1,0:T(8,128)(2,1)S(1)}, u32[]{:S(2)}, u32[]{:S(2)}) %collective-permute-start.14) | collective-permute-done | bytes 102432 | tf_op jit(solution)/shard_map/ppermute | solution.py:27
  13.8 3.4 %collective-permute-start.15 = (bf16[80,640]{1,0:T(8,128)(2,1)S(1)}, bf16[80,640]{1,0:T(8,128)(2,1)S(1)}, u32[]{:S(2)}, u32[]{:S(2)}) collective-permute-start(bf16[80,640]{1,0:T(8,128)(2,1)S(1)} %collective-permute-done.14.d), channel_id=1, source_target_pairs={{0,56},{8,0},{16,8},{24,16},{32,24},{40,32},{48,40},{56,48},{1,57}... | collective-permute-start | bytes 307208 | tf_op jit(solution)/shard_map/ppermute | solution.py:27
  17.2 3.0 %collective-permute-done.15.a = bf16[80,640]{1,0:T(8,128)(2,1)S(1)} collective-permute-done((bf16[80,640]{1,0:T(8,128)(2,1)S(1)}, bf16[80,640]{1,0:T(8,128)(2,1)S(1)}, u32[]{:S(2)}, u32[]{:S(2)}) %collective-permute-start.15) | collective-permute-done | bytes 102432 | tf_op jit(solution)/shard_map/ppermute | solution.py:27
  20.2 1.7 %collective-permute-start.16 = (bf16[80,640]{1,0:T(8,128)(2,1)S(1)}, bf16[80,640]{1,0:T(8,128)(2,1)S(1)}, u32[]{:S(2)}, u32[]{:S(2)}) collective-permute-start(bf16[80,640]{1,0:T(8,128)(2,1)S(1)} %collective-permute-done.15.a), channel_id=1, source_target_pairs={{0,56},{8,0},{16,8},{24,16},{32,24},{40,32},{48,40},{56,48},{1,57}... | collective-permute-start | bytes 307208 | tf_op jit(solution)/shard_map/ppermute | solution.py:27
  22.7 2.4 %collective-permute-start.25 = (bf16[320,640]{1,0:T(8,128)(2,1)S(1)}, bf16[320,640]{1,0:T(8,128)(2,1)S(1)}, u32[]{:S(2)}, u32[]{:S(2)}) collective-permute-start(bf16[320,640]{1,0:T(8,128)(2,1)S(1)} %shard_map.120.refs_0_), channel_id=1, source_target_pairs={{0,4},{4,0},{1,5},{5,1},{2,6},{6,2},{3,7},{7,3},{8,12},{12,8},{9,1... | collective-permute-start | bytes 1228808 | tf_op jit(solution)/shard_map/ppermute | solution.py:23
  25.1 2.5 %collective-permute-start.21 = (bf16[320,640]{1,0:T(8,128)(2,1)S(1)}, bf16[320,640]{1,0:T(8,128)(2,1)S(1)}, u32[]{:S(2)}, u32[]{:S(2)}) collective-permute-start(bf16[320,640]{1,0:T(8,128)(2,1)S(1)} %shard_map.120.refs_0_), channel_id=1, source_target_pairs={{0,192},{64,128},{128,64},{192,0},{1,193},{65,129},{129,65},{193,1... | collective-permute-start | bytes 1228808 | tf_op jit(solution)/shard_map/ppermute | solution.py:23
  28.7 1.6 %collective-permute-start.17 = (bf16[80,640]{1,0:T(8,128)(2,1)S(1)}, bf16[80,640]{1,0:T(8,128)(2,1)S(1)}, u32[]{:S(2)}, u32[]{:S(2)}) collective-permute-start(bf16[80,640]{1,0:T(8,128)(2,1)S(1)} %collective-permute-done.16.b), channel_id=1, source_target_pairs={{0,56},{8,0},{16,8},{24,16},{32,24},{40,32},{48,40},{56,48},{1,57}... | collective-permute-start | bytes 307208 | tf_op jit(solution)/shard_map/ppermute | solution.py:27
  30.9 1.8 %collective-permute-done.18.d = bf16[80,640]{1,0:T(8,128)(2,1)S(1)} collective-permute-done((bf16[80,640]{1,0:T(8,128)(2,1)S(1)}, bf16[80,640]{1,0:T(8,128)(2,1)S(1)}, u32[]{:S(2)}, u32[]{:S(2)}) %collective-permute-start.18) | collective-permute-done | bytes 102432 | tf_op jit(solution)/shard_map/ppermute | solution.py:27
  33.4 1.5 %collective-permute-start.20 = (bf16[320,640]{1,0:T(8,128)(2,1)S(1)}, bf16[320,640]{1,0:T(8,128)(2,1)S(1)}, u32[]{:S(2)}, u32[]{:S(2)}) collective-permute-start(bf16[320,640]{1,0:T(8,128)(2,1)S(1)} %shard_map.121.refs_1_), channel_id=1, source_target_pairs={{0,64},{64,0},{128,192},{192,128},{1,65},{65,1},{129,193},{193,129... | collective-permute-start | bytes 1228808 | tf_op jit(solution)/shard_map/ppermute | solution.py:23
  35.5 1.1 %shard_map.110 = (f32[128,128]{1,0:T(8,128)S(1)}, bf16[384,128]{1,0:T(8,128)(2,1)S(1)}, f32[3,128,128]{2,1,0:T(8,128)S(1)}) custom-call(s32[4]{0:T(128)S(1)} %pad_add_fusion.place.r_0_, bf16[128,128]{1,0:T(8,128)(2,1)S(1)} %copy-done.2, f32[128,128]{1,0:T(8,128)S(1)} %get-tuple-element.31.cum_ref.r_4_, s32[1,128]{1,0:T(1,128)S(1)} %bitcast.20, ...), custom_call_target="tpu_custom_call" | custom-call | flops 100000000 | bytes 1048576 | tf_op jit(solution)/shard_map/pallas_call | solution.py:31
  36.7 1.6 %collective-permute-done.4.r_2_.got3 = bf16[368,128]{1,0:T(8,128)(2,1)S(1)} collective-permute-done((bf16[368,128]{1,0:T(8,128)(2,1)S(1)}, bf16[368,128]{1,0:T(8,128)(2,1)S(1)}, u32[]{:S(2)}, u32[]{:S(2)}) %collective-permute-start.4) | collective-permute-done | bytes 94240 | tf_op jit(solution)/shard_map/ppermute | solution.py:23
  38.3 2.5 %collective-permute-start.1 = (bf16[384,128]{1,0:T(8,128)(2,1)S(1)}, bf16[384,128]{1,0:T(8,128)(2,1)S(1)}, u32[]{:S(2)}, u32[]{:S(2)}) collective-permute-start(bf16[384,128]{1,0:T(8,128)(2,1)S(1)} %get-tuple-element.34), channel_id=1, source_target_pairs={{0,4},{4,0},{1,5},{5,1},{2,6},{6,2},{3,7},{7,3},{8,12},{12,8},{9,1... | collective-permute-start | bytes 294920 | tf_op jit(solution)/shard_map/ppermute | solution.py:23
  41.7 1.2 %collective-permute-start.7 = (bf16[368,128]{1,0:T(8,128)(2,1)S(1)}, bf16[368,128]{1,0:T(8,128)(2,1)S(1)}, u32[]{:S(2)}, u32[]{:S(2)}) collective-permute-start(bf16[368,128]{1,0:T(8,128)(2,1)S(1)} %get-tuple-element.43), channel_id=1, source_target_pairs={{0,192},{64,128},{128,64},{192,0},{1,193},{65,129},{129,65},{193,1... | collective-permute-start | bytes 282632 | tf_op jit(solution)/shard_map/ppermute | solution.py:23
  42.9 2.1 %collective-permute-start.6 = (bf16[368,128]{1,0:T(8,128)(2,1)S(1)}, bf16[368,128]{1,0:T(8,128)(2,1)S(1)}, u32[]{:S(2)}, u32[]{:S(2)}) collective-permute-start(bf16[368,128]{1,0:T(8,128)(2,1)S(1)} %get-tuple-element.43), channel_id=1, source_target_pairs={{0,128},{64,192},{128,0},{192,64},{1,129},{65,193},{129,1},{193,65... | collective-permute-start | bytes 282632 | tf_op jit(solution)/shard_map/ppermute | solution.py:23
  46.9 3.5 %collective-permute-start.8 = (bf16[640,128]{1,0:T(8,128)(2,1)S(1)}, bf16[640,128]{1,0:T(8,128)(2,1)S(1)}, u32[]{:S(2)}, u32[]{:S(2)}) collective-permute-start(bf16[640,128]{1,0:T(8,128)(2,1)S(1)} %get-tuple-element.45), channel_id=1, source_target_pairs={{0,8},{8,0},{16,24},{24,16},{32,40},{40,32},{48,56},{56,48},{1,9},... | collective-permute-start | bytes 491528 | tf_op jit(solution)/shard_map/ppermute | solution.py:23
  50.4 3.7 %collective-permute-done.5.r1 = bf16[368,128]{1,0:T(8,128)(2,1)S(1)} collective-permute-done((bf16[368,128]{1,0:T(8,128)(2,1)S(1)}, bf16[368,128]{1,0:T(8,128)(2,1)S(1)}, u32[]{:S(2)}, u32[]{:S(2)}) %collective-permute-start.5) | collective-permute-done | bytes 94240 | tf_op jit(solution)/shard_map/ppermute | solution.py:23
  54.1 2.7 %collective-permute-start.31 = (bf16[320,640]{1,0:T(8,128)(2,1)S(1)}, bf16[320,640]{1,0:T(8,128)(2,1)S(1)}, u32[]{:S(2)}, u32[]{:S(2)}) collective-permute-start(bf16[320,640]{1,0:T(8,128)(2,1)S(1)} %collective-permute-done.21.refs_6_), channel_id=1, source_target_pairs={{0,4},{4,0},{1,5},{5,1},{2,6},{6,2},{3,7},{7,3},{8,12},{12,8},{9,1... | collective-permute-start | bytes 1228808 | tf_op jit(solution)/shard_map/ppermute | solution.py:23
  59.0 4.6 %collective-permute-done.9.late_side = bf16[640,128]{1,0:T(8,128)(2,1)S(1)} collective-permute-done((bf16[640,128]{1,0:T(8,128)(2,1)S(1)}, bf16[640,128]{1,0:T(8,128)(2,1)S(1)}, u32[]{:S(2)}, u32[]{:S(2)}) %collective-permute-start.9) | collective-permute-done | bytes 163872 | tf_op jit(solution)/shard_map/ppermute | solution.py:23
  63.6 1.2 %collective-permute-start.28 = (bf16[320,640]{1,0:T(8,128)(2,1)S(1)}, bf16[320,640]{1,0:T(8,128)(2,1)S(1)}, u32[]{:S(2)}, u32[]{:S(2)}) collective-permute-start(bf16[320,640]{1,0:T(8,128)(2,1)S(1)} %collective-permute-done.20.refs_3_), channel_id=1, source_target_pairs={{0,4},{4,0},{1,5},{5,1},{2,6},{6,2},{3,7},{7,3},{8,12},{12,8},{9,1... | collective-permute-start | bytes 1228808 | tf_op jit(solution)/shard_map/ppermute | solution.py:23
  64.7 3.1 %collective-permute-done.22.refs_4_ = bf16[320,640]{1,0:T(8,128)(2,1)S(1)} collective-permute-done((bf16[320,640]{1,0:T(8,128)(2,1)S(1)}, bf16[320,640]{1,0:T(8,128)(2,1)S(1)}, u32[]{:S(2)}, u32[]{:S(2)}) %collective-permute-start.22) | collective-permute-done | bytes 409632 | tf_op jit(solution)/shard_map/ppermute | solution.py:23
  70.0 2.0 %shard_map.118 = (f32[128,640]{1,0:T(8,128)S(1)}, f32[128,640]{1,0:T(8,128)S(1)}, f32[128,128]{1,0:T(8,128)S(1)}, f32[128,128]{1,0:T(8,128)S(1)}) custom-call(s32[4]{0:T(128)S(1)} %pad_add_fusion.place.r_0_, bf16[128,128]{1,0:T(8,128)(2,1)S(1)} %copy-done.2, f32[128,128]{1,0:T(8,128)S(1)} %get-tuple-element.35.factors, ...), custom_call_target="tpu_custom_call" | custom-call | flops 100000000 | bytes 1048576 | tf_op jit(solution)/shard_map/pallas_call | solution.py:31
  72.0 1.5 %shard_map.119 = (f32[128,640]{1,0:T(8,128)S(1)}, bf16[128,640]{1,0:T(8,128)(2,1)S(1)}) custom-call(s32[4]{0:T(128)S(1)} %pad_add_fusion.place.r_0_, bf16[128,128]{1,0:T(8,128)(2,1)S(1)} %copy-done.2, bf16[384,128]{1,0:T(8,128)(2,1)S(1)} %collective-permute-done.1.mail, f32[128,128]{1,0:T(8,128)S(1)} %get-tuple-element.46.own_w, ...), custom_call_target="tpu_custom_call" | custom-call | flops 100000000 | bytes 1048576 | tf_op jit(solution)/shard_map/pallas_call | solution.py:31
  74.6 2.2 %shard_map.112.high = f32[128,640]{1,0:T(8,128)S(1)} custom-call(s32[4]{0:T(128)S(1)} %pad_add_fusion.place.r_0_, bf16[128,128]{1,0:T(8,128)(2,1)S(1)} %copy-done.2, bf16[128,128]{1,0:T(8,128)(2,1)S(1)} %copy-done.4, bf16[128,1280]{1,0:T(8,128)(2,1)S(1)} %copy-done.1, f32[128,128]{1,0:T(8,128)S(1)} %get-tuple-element.31.cum_ref.r_4_, s32[1,128]{1,0:T(1,128)S(1)} %bitcast.15, ...), custom_call_target="tpu_custom_call" | custom-call | flops 100000000 | bytes 1048576 | tf_op jit(solution)/shard_map/pallas_call | solution.py:31
  76.8 2.3 %shard_map.111.low = f32[128,640]{1,0:T(8,128)S(1)} custom-call(s32[4]{0:T(128)S(1)} %pad_add_fusion.place.r_0_, bf16[128,128]{1,0:T(8,128)(2,1)S(1)} %copy-done.2, bf16[128,128]{1,0:T(8,128)(2,1)S(1)} %copy-done.4, bf16[128,1280]{1,0:T(8,128)(2,1)S(1)} %copy-done.1, f32[128,128]{1,0:T(8,128)S(1)} %get-tuple-element.31.cum_ref.r_4_, s32[1,128]{1,0:T(1,128)S(1)} %bitcast.16, ...), custom_call_target="tpu_custom_call" | custom-call | flops 100000000 | bytes 1048576 | tf_op jit(solution)/shard_map/pallas_call | solution.py:31
  79.2 3.7 %shard_map.122 = (bf16[32,2688]{1,0:T(8,128)(2,1)S(1)}, bf16[32,2688]{1,0:T(8,128)(2,1)S(1)}, bf16[32,2688]{1,0:T(8,128)(2,1)S(1)}, bf16[32,2688]{1,0:T(8,128)(2,1)S(1)}) custom-call(s32[4]{0:T(128)S(1)} %pad_add_fusion.place.r_0_, f32[128,640]{1,0:T(8,128)S(1)} %shard_map.111.low, f32[128,640]{1,0:T(8,128)S(1)} %shard_map.112.high, ...), custom_call_target="tpu_custom_call" | custom-call | flops 1000000000 | bytes 1048576 | tf_op jit(solution)/shard_map/pallas_call | solution.py:31
  82.9 3.0 %collective-permute-start.33 = (bf16[32,2688]{1,0:T(8,128)(2,1)S(1)}, bf16[32,2688]{1,0:T(8,128)(2,1)S(1)}, u32[]{:S(2)}, u32[]{:S(2)}) collective-permute-start(bf16[32,2688]{1,0:T(8,128)(2,1)S(1)} %get-tuple-element.54), channel_id=1, source_target_pairs={{0,2},{1,3},{2,0},{3,1},{4,6},{5,7},{6,4},{7,5},{8,10},{9,11},{10,... | collective-permute-start | bytes 516104 | tf_op jit(solution)/shard_map/ppermute | solution.py:23
  86.7 3.2 %collective-permute-done.33.b_ref = bf16[32,2688]{1,0:T(8,128)(2,1)S(1)} collective-permute-done((bf16[32,2688]{1,0:T(8,128)(2,1)S(1)}, bf16[32,2688]{1,0:T(8,128)(2,1)S(1)}, u32[]{:S(2)}, u32[]{:S(2)}) %collective-permute-start.33) | collective-permute-done | bytes 172064 | tf_op jit(solution)/shard_map/ppermute | solution.py:23
  90.0 4.1 %collective-permute-done.34.c_ref = bf16[32,2688]{1,0:T(8,128)(2,1)S(1)} collective-permute-done((bf16[32,2688]{1,0:T(8,128)(2,1)S(1)}, bf16[32,2688]{1,0:T(8,128)(2,1)S(1)}, u32[]{:S(2)}, u32[]{:S(2)}) %collective-permute-start.34) | collective-permute-done | bytes 172064 | tf_op jit(solution)/shard_map/ppermute | solution.py:23
  94.0 1.5 %shard_map.123 = bf16[32,2560]{1,0:T(8,128)(2,1)} custom-call(s32[4]{0:T(128)S(1)} %pad_add_fusion.place.r_0_, bf16[32,2688]{1,0:T(8,128)(2,1)S(1)} %get-tuple-element.53.a_ref, bf16[32,2688]{1,0:T(8,128)(2,1)S(1)} %collective-permute-done.33.b_ref, bf16[32,2688]{1,0:T(8,128)(2,1)S(1)} %collective-permute-done.34.c_ref, ...), custom_call_target="tpu_custom_call" | custom-call | flops 100000000 | bytes 1048576 | tf_op jit(solution)/shard_map/pallas_call | solution.py:31
  (82 shorter events, 16.0 us)
Async XLA Ops:
  0.0 7.6 %collective-permute-start.11 = (bf16[40,1280]{1,0:T(8,128)(2,1)}, bf16[40,1280]{1,0:T(8,128)(2,1)S(1)}, u32[]{:S(2)}, u32[]{:S(2)}) collective-permute-start(bf16[40,1280]{1,0:T(8,128)(2,1)} %bitcast.21), channel_id=1, source_target_pairs={{0,4},{4,0},{1,5},{5,1},{2,6},{6,2},{3,7},{7,3},{8,12},{12,8},{9,1... | collective-permute-start | bytes 307208 | tf_op jit(solution)/shard_map/ppermute | solution.py:23
  7.7 6.2 %collective-permute-start.14 = (bf16[80,640]{1,0:T(8,128)(2,1)S(1)}, bf16[80,640]{1,0:T(8,128)(2,1)S(1)}, u32[]{:S(2)}, u32[]{:S(2)}) collective-permute-start(bf16[80,640]{1,0:T(8,128)(2,1)S(1)} %fusion.c), channel_id=1, source_target_pairs={{0,56},{8,0},{16,8},{24,16},{32,24},{40,32},{48,40},{56,48},{1,57}... | collective-permute-start | bytes 307208 | tf_op jit(solution)/shard_map/ppermute | solution.py:27
  11.6 5.6 %collective-permute-start.12 = (bf16[80,640]{1,0:T(8,128)(2,1)S(1)}, bf16[80,640]{1,0:T(8,128)(2,1)S(1)}, u32[]{:S(2)}, u32[]{:S(2)}) collective-permute-start(bf16[80,640]{1,0:T(8,128)(2,1)S(1)} %fusion.c), channel_id=1, source_target_pairs={{0,8},{8,16},{16,24},{24,32},{32,40},{40,48},{48,56},{56,0},{1,9},... | collective-permute-start | bytes 307208 | tf_op jit(solution)/shard_map/ppermute | solution.py:27
  12.2 9.7 %collective-permute-start.2 = (bf16[688,128]{1,0:T(8,128)(2,1)S(1)}, bf16[688,128]{1,0:T(8,128)(2,1)S(1)}, u32[]{:S(2)}, u32[]{:S(2)}) collective-permute-start(bf16[688,128]{1,0:T(8,128)(2,1)S(1)} %get-tuple-element.37.own), channel_id=1, source_target_pairs={{0,8},{8,0},{16,24},{24,16},{32,40},{40,32},{48,56},{56,48},{1,9},... | collective-permute-start | bytes 528392 | tf_op jit(solution)/shard_map/ppermute | solution.py:23
  13.8 6.4 %collective-permute-start.15 = (bf16[80,640]{1,0:T(8,128)(2,1)S(1)}, bf16[80,640]{1,0:T(8,128)(2,1)S(1)}, u32[]{:S(2)}, u32[]{:S(2)}) collective-permute-start(bf16[80,640]{1,0:T(8,128)(2,1)S(1)} %collective-permute-done.14.d), channel_id=1, source_target_pairs={{0,56},{8,0},{16,8},{24,16},{32,24},{40,32},{48,40},{56,48},{1,57}... | collective-permute-start | bytes 307208 | tf_op jit(solution)/shard_map/ppermute | solution.py:27
  17.2 5.4 %collective-permute-start.13 = (bf16[80,640]{1,0:T(8,128)(2,1)S(1)}, bf16[80,640]{1,0:T(8,128)(2,1)S(1)}, u32[]{:S(2)}, u32[]{:S(2)}) collective-permute-start(bf16[80,640]{1,0:T(8,128)(2,1)S(1)} %collective-permute-done.12.b), channel_id=1, source_target_pairs={{0,8},{8,16},{16,24},{24,32},{32,40},{40,48},{48,56},{56,0},{1,9},... | collective-permute-start | bytes 307208 | tf_op jit(solution)/shard_map/ppermute | solution.py:27
  20.2 7.4 %collective-permute-start.16 = (bf16[80,640]{1,0:T(8,128)(2,1)S(1)}, bf16[80,640]{1,0:T(8,128)(2,1)S(1)}, u32[]{:S(2)}, u32[]{:S(2)}) collective-permute-start(bf16[80,640]{1,0:T(8,128)(2,1)S(1)} %collective-permute-done.15.a), channel_id=1, source_target_pairs={{0,56},{8,0},{16,8},{24,16},{32,24},{40,32},{48,40},{56,48},{1,57}... | collective-permute-start | bytes 307208 | tf_op jit(solution)/shard_map/ppermute | solution.py:27
  22.5 6.1 %collective-permute-start.3 = (bf16[368,128]{1,0:T(8,128)(2,1)S(1)}, bf16[368,128]{1,0:T(8,128)(2,1)S(1)}, u32[]{:S(2)}, u32[]{:S(2)}) collective-permute-start(bf16[368,128]{1,0:T(8,128)(2,1)S(1)} %get-tuple-element.39.r_1_), channel_id=1, source_target_pairs={{0,16},{8,24},{16,0},{24,8},{32,48},{40,56},{48,32},{56,40},{1,17}... | collective-permute-start | bytes 282632 | tf_op jit(solution)/shard_map/ppermute | solution.py:23
  22.7 20.2 %collective-permute-start.25 = (bf16[320,640]{1,0:T(8,128)(2,1)S(1)}, bf16[320,640]{1,0:T(8,128)(2,1)S(1)}, u32[]{:S(2)}, u32[]{:S(2)}) collective-permute-start(bf16[320,640]{1,0:T(8,128)(2,1)S(1)} %shard_map.120.refs_0_), channel_id=1, source_target_pairs={{0,4},{4,0},{1,5},{5,1},{2,6},{6,2},{3,7},{7,3},{8,12},{12,8},{9,1... | collective-permute-start | bytes 1228808 | tf_op jit(solution)/shard_map/ppermute | solution.py:23
  25.1 19.9 %collective-permute-start.21 = (bf16[320,640]{1,0:T(8,128)(2,1)S(1)}, bf16[320,640]{1,0:T(8,128)(2,1)S(1)}, u32[]{:S(2)}, u32[]{:S(2)}) collective-permute-start(bf16[320,640]{1,0:T(8,128)(2,1)S(1)} %shard_map.120.refs_0_), channel_id=1, source_target_pairs={{0,192},{64,128},{128,64},{192,0},{1,193},{65,129},{129,65},{193,1... | collective-permute-start | bytes 1228808 | tf_op jit(solution)/shard_map/ppermute | solution.py:23
  27.6 18.4 %collective-permute-start.19 = (bf16[320,640]{1,0:T(8,128)(2,1)S(1)}, bf16[320,640]{1,0:T(8,128)(2,1)S(1)}, u32[]{:S(2)}, u32[]{:S(2)}) collective-permute-start(bf16[320,640]{1,0:T(8,128)(2,1)S(1)} %shard_map.120.refs_0_), channel_id=1, source_target_pairs={{0,64},{64,0},{128,192},{192,128},{1,65},{65,1},{129,193},{193,129... | collective-permute-start | bytes 1228808 | tf_op jit(solution)/shard_map/ppermute | solution.py:23
  27.6 5.1 %collective-permute-start.18 = (bf16[80,640]{1,0:T(8,128)(2,1)S(1)}, bf16[80,640]{1,0:T(8,128)(2,1)S(1)}, u32[]{:S(2)}, u32[]{:S(2)}) collective-permute-start(bf16[80,640]{1,0:T(8,128)(2,1)S(1)} %collective-permute-done.13.a), channel_id=1, source_target_pairs={{0,8},{8,16},{16,24},{24,32},{32,40},{40,48},{48,56},{56,0},{1,9},... | collective-permute-start | bytes 307208 | tf_op jit(solution)/shard_map/ppermute | solution.py:27
  32.7 5.6 %collective-permute-start.4 = (bf16[368,128]{1,0:T(8,128)(2,1)S(1)}, bf16[368,128]{1,0:T(8,128)(2,1)S(1)}, u32[]{:S(2)}, u32[]{:S(2)}) collective-permute-start(bf16[368,128]{1,0:T(8,128)(2,1)S(1)} %get-tuple-element.41.r_1_), channel_id=1, source_target_pairs={{0,48},{8,56},{16,32},{24,40},{32,16},{40,24},{48,0},{56,8},{1,49}... | collective-permute-start | bytes 282632 | tf_op jit(solution)/shard_map/ppermute | solution.py:23
  33.4 23.5 %collective-permute-start.20 = (bf16[320,640]{1,0:T(8,128)(2,1)S(1)}, bf16[320,640]{1,0:T(8,128)(2,1)S(1)}, u32[]{:S(2)}, u32[]{:S(2)}) collective-permute-start(bf16[320,640]{1,0:T(8,128)(2,1)S(1)} %shard_map.121.refs_1_), channel_id=1, source_target_pairs={{0,64},{64,0},{128,192},{192,128},{1,65},{65,1},{129,193},{193,129... | collective-permute-start | bytes 1228808 | tf_op jit(solution)/shard_map/ppermute | solution.py:23
  41.7 5.1 %collective-permute-start.7 = (bf16[368,128]{1,0:T(8,128)(2,1)S(1)}, bf16[368,128]{1,0:T(8,128)(2,1)S(1)}, u32[]{:S(2)}, u32[]{:S(2)}) collective-permute-start(bf16[368,128]{1,0:T(8,128)(2,1)S(1)} %get-tuple-element.43), channel_id=1, source_target_pairs={{0,192},{64,128},{128,64},{192,0},{1,193},{65,129},{129,65},{193,1... | collective-permute-start | bytes 282632 | tf_op jit(solution)/shard_map/ppermute | solution.py:23
  42.9 7.5 %collective-permute-start.6 = (bf16[368,128]{1,0:T(8,128)(2,1)S(1)}, bf16[368,128]{1,0:T(8,128)(2,1)S(1)}, u32[]{:S(2)}, u32[]{:S(2)}) collective-permute-start(bf16[368,128]{1,0:T(8,128)(2,1)S(1)} %get-tuple-element.43), channel_id=1, source_target_pairs={{0,128},{64,192},{128,0},{192,64},{1,129},{65,193},{129,1},{193,65... | collective-permute-start | bytes 282632 | tf_op jit(solution)/shard_map/ppermute | solution.py:23
  45.0 13.0 %collective-permute-start.26 = (bf16[320,640]{1,0:T(8,128)(2,1)S(1)}, bf16[320,640]{1,0:T(8,128)(2,1)S(1)}, u32[]{:S(2)}, u32[]{:S(2)}) collective-permute-start(bf16[320,640]{1,0:T(8,128)(2,1)S(1)} %shard_map.121.refs_1_), channel_id=1, source_target_pairs={{0,4},{4,0},{1,5},{5,1},{2,6},{6,2},{3,7},{7,3},{8,12},{12,8},{9,1... | collective-permute-start | bytes 1228808 | tf_op jit(solution)/shard_map/ppermute | solution.py:23
  45.9 12.2 %collective-permute-start.24 = (bf16[320,640]{1,0:T(8,128)(2,1)S(1)}, bf16[320,640]{1,0:T(8,128)(2,1)S(1)}, u32[]{:S(2)}, u32[]{:S(2)}) collective-permute-start(bf16[320,640]{1,0:T(8,128)(2,1)S(1)} %shard_map.121.refs_1_), channel_id=1, source_target_pairs={{0,192},{64,128},{128,64},{192,0},{1,193},{65,129},{129,65},{193,1... | collective-permute-start | bytes 1228808 | tf_op jit(solution)/shard_map/ppermute | solution.py:23
  46.9 10.0 %collective-permute-start.8 = (bf16[640,128]{1,0:T(8,128)(2,1)S(1)}, bf16[640,128]{1,0:T(8,128)(2,1)S(1)}, u32[]{:S(2)}, u32[]{:S(2)}) collective-permute-start(bf16[640,128]{1,0:T(8,128)(2,1)S(1)} %get-tuple-element.45), channel_id=1, source_target_pairs={{0,8},{8,0},{16,24},{24,16},{32,40},{40,32},{48,56},{56,48},{1,9},... | collective-permute-start | bytes 491528 | tf_op jit(solution)/shard_map/ppermute | solution.py:23
  54.1 10.6 %collective-permute-start.31 = (bf16[320,640]{1,0:T(8,128)(2,1)S(1)}, bf16[320,640]{1,0:T(8,128)(2,1)S(1)}, u32[]{:S(2)}, u32[]{:S(2)}) collective-permute-start(bf16[320,640]{1,0:T(8,128)(2,1)S(1)} %collective-permute-done.21.refs_6_), channel_id=1, source_target_pairs={{0,4},{4,0},{1,5},{5,1},{2,6},{6,2},{3,7},{7,3},{8,12},{12,8},{9,1... | collective-permute-start | bytes 1228808 | tf_op jit(solution)/shard_map/ppermute | solution.py:23
  56.8 11.0 %collective-permute-start.22 = (bf16[320,640]{1,0:T(8,128)(2,1)S(1)}, bf16[320,640]{1,0:T(8,128)(2,1)S(1)}, u32[]{:S(2)}, u32[]{:S(2)}) collective-permute-start(bf16[320,640]{1,0:T(8,128)(2,1)S(1)} %collective-permute-done.21.refs_6_), channel_id=1, source_target_pairs={{0,64},{64,0},{128,192},{192,128},{1,65},{65,1},{129,193},{193,129... | collective-permute-start | bytes 1228808 | tf_op jit(solution)/shard_map/ppermute | solution.py:23
  56.8 12.3 %collective-permute-start.23 = (bf16[320,640]{1,0:T(8,128)(2,1)S(1)}, bf16[320,640]{1,0:T(8,128)(2,1)S(1)}, u32[]{:S(2)}, u32[]{:S(2)}) collective-permute-start(bf16[320,640]{1,0:T(8,128)(2,1)S(1)} %collective-permute-done.20.refs_3_), channel_id=1, source_target_pairs={{0,192},{64,128},{128,64},{192,0},{1,193},{65,129},{129,65},{193,1... | collective-permute-start | bytes 1228808 | tf_op jit(solution)/shard_map/ppermute | solution.py:23
  58.0 5.5 %collective-permute-start.9 = (bf16[640,128]{1,0:T(8,128)(2,1)S(1)}, bf16[640,128]{1,0:T(8,128)(2,1)S(1)}, u32[]{:S(2)}, u32[]{:S(2)}) collective-permute-start(bf16[640,128]{1,0:T(8,128)(2,1)S(1)} %get-tuple-element.48.late), channel_id=1, source_target_pairs={{0,8},{8,0},{16,24},{24,16},{32,40},{40,32},{48,56},{56,48},{1,9},... | collective-permute-start | bytes 491528 | tf_op jit(solution)/shard_map/ppermute | solution.py:23
  58.1 15.4 %collective-permute-start.27 = (bf16[320,640]{1,0:T(8,128)(2,1)S(1)}, bf16[320,640]{1,0:T(8,128)(2,1)S(1)}, u32[]{:S(2)}, u32[]{:S(2)}) collective-permute-start(bf16[320,640]{1,0:T(8,128)(2,1)S(1)} %collective-permute-done.19.refs_2_), channel_id=1, source_target_pairs={{0,4},{4,0},{1,5},{5,1},{2,6},{6,2},{3,7},{7,3},{8,12},{12,8},{9,1... | collective-permute-start | bytes 1228808 | tf_op jit(solution)/shard_map/ppermute | solution.py:23
  63.6 15.5 %collective-permute-start.28 = (bf16[320,640]{1,0:T(8,128)(2,1)S(1)}, bf16[320,640]{1,0:T(8,128)(2,1)S(1)}, u32[]{:S(2)}, u32[]{:S(2)}) collective-permute-start(bf16[320,640]{1,0:T(8,128)(2,1)S(1)} %collective-permute-done.20.refs_3_), channel_id=1, source_target_pairs={{0,4},{4,0},{1,5},{5,1},{2,6},{6,2},{3,7},{7,3},{8,12},{12,8},{9,1... | collective-permute-start | bytes 1228808 | tf_op jit(solution)/shard_map/ppermute | solution.py:23
  64.7 14.4 %collective-permute-start.32 = (bf16[320,640]{1,0:T(8,128)(2,1)S(1)}, bf16[320,640]{1,0:T(8,128)(2,1)S(1)}, u32[]{:S(2)}, u32[]{:S(2)}) collective-permute-start(bf16[320,640]{1,0:T(8,128)(2,1)S(1)} %collective-permute-done.24.refs_7_), channel_id=1, source_target_pairs={{0,4},{4,0},{1,5},{5,1},{2,6},{6,2},{3,7},{7,3},{8,12},{12,8},{9,1... | collective-permute-start | bytes 1228808 | tf_op jit(solution)/shard_map/ppermute | solution.py:23
  67.8 11.3 %collective-permute-start.29 = (bf16[320,640]{1,0:T(8,128)(2,1)S(1)}, bf16[320,640]{1,0:T(8,128)(2,1)S(1)}, u32[]{:S(2)}, u32[]{:S(2)}) collective-permute-start(bf16[320,640]{1,0:T(8,128)(2,1)S(1)} %collective-permute-done.22.refs_4_), channel_id=1, source_target_pairs={{0,4},{4,0},{1,5},{5,1},{2,6},{6,2},{3,7},{7,3},{8,12},{12,8},{9,1... | collective-permute-start | bytes 1228808 | tf_op jit(solution)/shard_map/ppermute | solution.py:23
  69.1 10.0 %collective-permute-start.30 = (bf16[320,640]{1,0:T(8,128)(2,1)S(1)}, bf16[320,640]{1,0:T(8,128)(2,1)S(1)}, u32[]{:S(2)}, u32[]{:S(2)}) collective-permute-start(bf16[320,640]{1,0:T(8,128)(2,1)S(1)} %collective-permute-done.23.refs_5_), channel_id=1, source_target_pairs={{0,4},{4,0},{1,5},{5,1},{2,6},{6,2},{3,7},{7,3},{8,12},{12,8},{9,1... | collective-permute-start | bytes 1228808 | tf_op jit(solution)/shard_map/ppermute | solution.py:23
  73.6 5.5 %collective-permute-start.10 = (bf16[128,640]{1,0:T(8,128)(2,1)S(1)}, bf16[128,640]{1,0:T(8,128)(2,1)S(1)}, u32[]{:S(2)}, u32[]{:S(2)}) collective-permute-start(bf16[128,640]{1,0:T(8,128)(2,1)S(1)} %get-tuple-element.52), channel_id=1, source_target_pairs={{0,4},{4,0},{1,5},{5,1},{2,6},{6,2},{3,7},{7,3},{8,12},{12,8},{9,1... | collective-permute-start | bytes 491528 | tf_op jit(solution)/shard_map/ppermute | solution.py:23
  82.9 7.0 %collective-permute-start.33 = (bf16[32,2688]{1,0:T(8,128)(2,1)S(1)}, bf16[32,2688]{1,0:T(8,128)(2,1)S(1)}, u32[]{:S(2)}, u32[]{:S(2)}) collective-permute-start(bf16[32,2688]{1,0:T(8,128)(2,1)S(1)} %get-tuple-element.54), channel_id=1, source_target_pairs={{0,2},{1,3},{2,0},{3,1},{4,6},{5,7},{6,4},{7,5},{8,10},{9,11},{10,... | collective-permute-start | bytes 516104 | tf_op jit(solution)/shard_map/ppermute | solution.py:23
  85.9 8.1 %collective-permute-start.34 = (bf16[32,2688]{1,0:T(8,128)(2,1)S(1)}, bf16[32,2688]{1,0:T(8,128)(2,1)S(1)}, u32[]{:S(2)}, u32[]{:S(2)}) collective-permute-start(bf16[32,2688]{1,0:T(8,128)(2,1)S(1)} %get-tuple-element.55), channel_id=1, source_target_pairs={{0,1},{1,0},{2,3},{3,2},{4,5},{5,4},{6,7},{7,6},{8,9},{9,8},{10,11... | collective-permute-start | bytes 516104 | tf_op jit(solution)/shard_map/ppermute | solution.py:23
  86.3 7.7 %collective-permute-start.35 = (bf16[32,2688]{1,0:T(8,128)(2,1)S(1)}, bf16[32,2688]{1,0:T(8,128)(2,1)S(1)}, u32[]{:S(2)}, u32[]{:S(2)}) collective-permute-start(bf16[32,2688]{1,0:T(8,128)(2,1)S(1)} %get-tuple-element.56), channel_id=1, source_target_pairs={{0,3},{1,2},{2,1},{3,0},{4,7},{5,6},{6,5},{7,4},{8,11},{9,10},{10,... | collective-permute-start | bytes 516104 | tf_op jit(solution)/shard_map/ppermute | solution.py:23
  (16 other events, 37.3 us)

commit v6 on v5

--- a/solution.py
+++ b/solution.py
@@ -71,7 +71,7 @@
     return parts[:size] + parts[size : 2 * size] + parts[2 * size :]
 
 
-def state_kernel(place, values, keys, log_decay, msg, cum_ref):
+def state_kernel(place, values, keys, log_decay, msg, cum_ref, values_out):
     lane = lanes()
     cum = jnp.concatenate([log_decay[...], jnp.zeros((4, TOK), F32)], axis=0)
     step = 1
@@ -90,7 +90,9 @@
     for p in range(10):
         cols = slice(p * LANE, (p + 1) * LANE)
         wide = two_heads(factor[:, 2 * p : 2 * p + 1], factor[:, 2 * p + 1 : 2 * p + 2], lane)
-        decayed = (values[:, cols].astype(F32) * wide).astype(BF)
+        piece = values[:, cols]
+        values_out[:, cols] = piece
+        decayed = (piece.astype(F32) * wide).astype(BF)
         msg[cols, :] = lax.dot_general(decayed, key, TN, preferred_element_type=F32).astype(BF)
 
 
@@ -232,11 +234,17 @@
             pieces.append(
                 jnp.dot(weight, values[:, h * 64 : h * 64 + 64], preferred_element_type=F32)
             )
-        read = lax.dot_general(q, got[cols, :], NT, preferred_element_type=F32)
-        read = read * two_heads(zero_level[:, 2 * p : 2 * p + 1], zero_level[:, 2 * p + 1 : 2 * p + 2], lane)
         gain = two_heads(skip[:, 2 * p : 2 * p + 1], skip[:, 2 * p + 1 : 2 * p + 2], lane)
         out = slice((p % 5) * LANE, (p % 5) * LANE + LANE)
-        base[:, out] = jnp.concatenate(pieces, axis=1) + read + gain * values[:, cols].astype(F32)
+        base[:, out] = jnp.concatenate(pieces, axis=1) + gain * values[:, cols].astype(F32)
+
+    @pl.when(place[0] == 1)
+    def _():
+        for p in range(side * 5, side * 5 + 5):
+            out = slice((p % 5) * LANE, (p % 5) * LANE + LANE)
+            read = lax.dot_general(q, got[p * LANE : (p + 1) * LANE, :], NT, preferred_element_type=F32)
+            wide = two_heads(zero_level[:, 2 * p : 2 * p + 1], zero_level[:, 2 * p + 1 : 2 * p + 2], lane)
+            base[:, out] = base[:, out] + read * wide
 
 
 def level_weights(place, factors, mail, first_total, prefixes):
@@ -433,9 +441,9 @@
     places = [lax.axis_index(name) for name in ("core", "y", "x", "z")]
     place = jnp.stack(places).astype(I32)
     own_w, other_w = gather_weights(out_proj)
-    state, cum = call(
+    state, cum, values = call(
         state_kernel, place, (values, key_rows, log_decay.T),
-        [shaped(COLS + 96, NST), shaped(TOK, LANE, dtype=F32)],
+        [shaped(COLS + 96, NST), shaped(TOK, LANE, dtype=F32), shaped(TOK, COLS)],
         vmem=6,
     )
     got0 = flip(state, "core", 1, 2)

time: 95.8 us -> 101 us (1.054)
  the two profiles are of different devices: /device:TPU:1 before, /device:TPU:6 now
where the time goes in v6:
time: 101 us; the launch traced here: 99.3 us
  waiting for transfers between devices  43.9 us (43%)
  starting transfers between devices  32.3 us (32%)
  Pallas kernels  19.1 us (19%)
  local copies, waits for them, and re-layouts  3.7 us (4%)
    ppermute x29, waiting for transfers between devices, flip(): return lax.ppermute(value, axis, [(i, i ^ mask) for i in range(size)])  36.5 us
    pallas_call x15, Pallas kernels, call(): pl.pallas_call(body, out_shape=outs, in_specs=[pl.BlockSpec(memory_space=...  19.1 us
    ppermute x29, starting transfers between devices, flip(): return lax.ppermute(value, axis, [(i, i ^ mask) for i in range(size)])  18.5 us
    ppermute x7, starting transfers between devices, shift(): lax.ppermute(value, axis, [(i, (i + step) % size) for i in range(size)])  13.8 us
    ppermute x7, waiting for transfers between devices, shift(): lax.ppermute(value, axis, [(i, (i + step) % size) for i in range(size)])  7.37 us
    unnamed x22, local copies, waits for them, and re-layouts  3.7 us
  transfers between devices with their start and end apart: 36, of which 15 were waited for; matrix products, arithmetic and copies ran while one was open for 0% of the time, Pallas kernels for 14%

profile of v6, /device:TPU:6, one launch (start us, length us, event | category | flops | bytes accessed | tf_op | source)
XLA Modules:
  0.0 99.3 jit_solution(14120738692969148562)
XLA Ops:
  2.4 1.9 %shard_map.109 = (bf16[1376,128]{1,0:T(8,128)(2,1)S(1)}, f32[128,128]{1,0:T(8,128)S(1)}, bf16[128,1280]{1,0:T(8,128)(2,1)S(1)}) custom-call(s32[4]{0:T(128)S(1)} %pad_add_fusion.place.r_0_, bf16[128,1280]{1,0:T(8,128)(2,1)S(1)} %copy-done.2, bf16[128,128]{1,0:T(8,128)(2,1)S(1)} %copy-done.3, f32[20,128]{1,0:T(8,128)S(1)} %bitcast.13), custom_call_target="tpu_custom_call" | custom-call | flops 100000000 | bytes 1048576 | tf_op jit(solution)/shard_map/pallas_call | solution.py:31
  4.5 5.9 %collective-permute-start.14 = (bf16[80,640]{1,0:T(8,128)(2,1)S(1)}, bf16[80,640]{1,0:T(8,128)(2,1)S(1)}, u32[]{:S(2)}, u32[]{:S(2)}) collective-permute-start(bf16[80,640]{1,0:T(8,128)(2,1)S(1)} %fusion.c), channel_id=1, source_target_pairs={{0,56},{8,0},{16,8},{24,16},{32,24},{40,32},{48,40},{56,48},{1,57}... | collective-permute-start | bytes 307208 | tf_op jit(solution)/shard_map/ppermute | solution.py:27
  11.2 2.0 %collective-permute-done.14.d = bf16[80,640]{1,0:T(8,128)(2,1)S(1)} collective-permute-done((bf16[80,640]{1,0:T(8,128)(2,1)S(1)}, bf16[80,640]{1,0:T(8,128)(2,1)S(1)}, u32[]{:S(2)}, u32[]{:S(2)}) %collective-permute-start.14) | collective-permute-done | bytes 102432 | tf_op jit(solution)/shard_map/ppermute | solution.py:27
  13.2 3.7 %collective-permute-start.15 = (bf16[80,640]{1,0:T(8,128)(2,1)S(1)}, bf16[80,640]{1,0:T(8,128)(2,1)S(1)}, u32[]{:S(2)}, u32[]{:S(2)}) collective-permute-start(bf16[80,640]{1,0:T(8,128)(2,1)S(1)} %collective-permute-done.14.d), channel_id=1, source_target_pairs={{0,56},{8,0},{16,8},{24,16},{32,24},{40,32},{48,40},{56,48},{1,57}... | collective-permute-start | bytes 307208 | tf_op jit(solution)/shard_map/ppermute | solution.py:27
  16.9 3.0 %collective-permute-done.15.a = bf16[80,640]{1,0:T(8,128)(2,1)S(1)} collective-permute-done((bf16[80,640]{1,0:T(8,128)(2,1)S(1)}, bf16[80,640]{1,0:T(8,128)(2,1)S(1)}, u32[]{:S(2)}, u32[]{:S(2)}) %collective-permute-start.15) | collective-permute-done | bytes 102432 | tf_op jit(solution)/shard_map/ppermute | solution.py:27
  19.9 2.9 %collective-permute-start.16 = (bf16[80,640]{1,0:T(8,128)(2,1)S(1)}, bf16[80,640]{1,0:T(8,128)(2,1)S(1)}, u32[]{:S(2)}, u32[]{:S(2)}) collective-permute-start(bf16[80,640]{1,0:T(8,128)(2,1)S(1)} %collective-permute-done.15.a), channel_id=1, source_target_pairs={{0,56},{8,0},{16,8},{24,16},{32,24},{40,32},{48,40},{56,48},{1,57}... | collective-permute-start | bytes 307208 | tf_op jit(solution)/shard_map/ppermute | solution.py:27
  25.0 3.9 %collective-permute-done.3.r_2_.r_4_.got2 = bf16[368,128]{1,0:T(8,128)(2,1)S(1)} collective-permute-done((bf16[368,128]{1,0:T(8,128)(2,1)S(1)}, bf16[368,128]{1,0:T(8,128)(2,1)S(1)}, u32[]{:S(2)}, u32[]{:S(2)}) %collective-permute-start.3) | collective-permute-done | bytes 94240 | tf_op jit(solution)/shard_map/ppermute | solution.py:23
  28.9 1.3 %collective-permute-start.17 = (bf16[80,640]{1,0:T(8,128)(2,1)S(1)}, bf16[80,640]{1,0:T(8,128)(2,1)S(1)}, u32[]{:S(2)}, u32[]{:S(2)}) collective-permute-start(bf16[80,640]{1,0:T(8,128)(2,1)S(1)} %collective-permute-done.16.b), channel_id=1, source_target_pairs={{0,56},{8,0},{16,8},{24,16},{32,24},{40,32},{48,40},{56,48},{1,57}... | collective-permute-start | bytes 307208 | tf_op jit(solution)/shard_map/ppermute | solution.py:27
  32.4 1.6 %collective-permute-done.17.c = bf16[80,640]{1,0:T(8,128)(2,1)S(1)} collective-permute-done((bf16[80,640]{1,0:T(8,128)(2,1)S(1)}, bf16[80,640]{1,0:T(8,128)(2,1)S(1)}, u32[]{:S(2)}, u32[]{:S(2)}) %collective-permute-start.17) | collective-permute-done | bytes 102432 | tf_op jit(solution)/shard_map/ppermute | solution.py:27
  35.4 1.1 %shard_map.110 = (f32[128,128]{1,0:T(8,128)S(1)}, bf16[384,128]{1,0:T(8,128)(2,1)S(1)}, f32[3,128,128]{2,1,0:T(8,128)S(1)}) custom-call(s32[4]{0:T(128)S(1)} %pad_add_fusion.place.r_0_, bf16[128,128]{1,0:T(8,128)(2,1)S(1)} %copy-done, f32[128,128]{1,0:T(8,128)S(1)} %get-tuple-element.33.cum_ref.r_4_, s32[1,128]{1,0:T(1,128)S(1)} %bitcast.20, ...), custom_call_target="tpu_custom_call" | custom-call | flops 100000000 | bytes 1048576 | tf_op jit(solution)/shard_map/pallas_call | solution.py:31
  36.5 1.6 %collective-permute-done.4.r_2_.got3 = bf16[368,128]{1,0:T(8,128)(2,1)S(1)} collective-permute-done((bf16[368,128]{1,0:T(8,128)(2,1)S(1)}, bf16[368,128]{1,0:T(8,128)(2,1)S(1)}, u32[]{:S(2)}, u32[]{:S(2)}) %collective-permute-start.4) | collective-permute-done | bytes 94240 | tf_op jit(solution)/shard_map/ppermute | solution.py:23
  39.5 1.1 %collective-permute-start.5 = (bf16[368,128]{1,0:T(8,128)(2,1)S(1)}, bf16[368,128]{1,0:T(8,128)(2,1)S(1)}, u32[]{:S(2)}, u32[]{:S(2)}) collective-permute-start(bf16[368,128]{1,0:T(8,128)(2,1)S(1)} %get-tuple-element.45), channel_id=1, source_target_pairs={{0,64},{64,0},{128,192},{192,128},{1,65},{65,1},{129,193},{193,129... | collective-permute-start | bytes 282632 | tf_op jit(solution)/shard_map/ppermute | solution.py:23
  40.6 2.4 %collective-permute-start.6 = (bf16[368,128]{1,0:T(8,128)(2,1)S(1)}, bf16[368,128]{1,0:T(8,128)(2,1)S(1)}, u32[]{:S(2)}, u32[]{:S(2)}) collective-permute-start(bf16[368,128]{1,0:T(8,128)(2,1)S(1)} %get-tuple-element.45), channel_id=1, source_target_pairs={{0,128},{64,192},{128,0},{192,64},{1,129},{65,193},{129,1},{193,65... | collective-permute-start | bytes 282632 | tf_op jit(solution)/shard_map/ppermute | solution.py:23
  43.1 1.1 %collective-permute-start.24 = (bf16[320,640]{1,0:T(8,128)(2,1)S(1)}, bf16[320,640]{1,0:T(8,128)(2,1)S(1)}, u32[]{:S(2)}, u32[]{:S(2)}) collective-permute-start(bf16[320,640]{1,0:T(8,128)(2,1)S(1)} %shard_map.121.refs_1_), channel_id=1, source_target_pairs={{0,192},{64,128},{128,64},{192,0},{1,193},{65,129},{129,65},{193,1... | collective-permute-start | bytes 1228808 | tf_op jit(solution)/shard_map/ppermute | solution.py:23
  44.2 1.1 %collective-permute-done.5.r1 = bf16[368,128]{1,0:T(8,128)(2,1)S(1)} collective-permute-done((bf16[368,128]{1,0:T(8,128)(2,1)S(1)}, bf16[368,128]{1,0:T(8,128)(2,1)S(1)}, u32[]{:S(2)}, u32[]{:S(2)}) %collective-permute-start.5) | collective-permute-done | bytes 94240 | tf_op jit(solution)/shard_map/ppermute | solution.py:23
  45.3 1.1 %collective-permute-start.8 = (bf16[640,128]{1,0:T(8,128)(2,1)S(1)}, bf16[640,128]{1,0:T(8,128)(2,1)S(1)}, u32[]{:S(2)}, u32[]{:S(2)}) collective-permute-start(bf16[640,128]{1,0:T(8,128)(2,1)S(1)} %get-tuple-element.47), channel_id=1, source_target_pairs={{0,8},{8,0},{16,24},{24,16},{32,40},{40,32},{48,56},{56,48},{1,9},... | collective-permute-start | bytes 491528 | tf_op jit(solution)/shard_map/ppermute | solution.py:23
  46.4 2.7 %collective-permute-done.6.r2 = bf16[368,128]{1,0:T(8,128)(2,1)S(1)} collective-permute-done((bf16[368,128]{1,0:T(8,128)(2,1)S(1)}, bf16[368,128]{1,0:T(8,128)(2,1)S(1)}, u32[]{:S(2)}, u32[]{:S(2)}) %collective-permute-start.6) | collective-permute-done | bytes 94240 | tf_op jit(solution)/shard_map/ppermute | solution.py:23
  49.8 9.2 %collective-permute-done.7.r3 = bf16[368,128]{1,0:T(8,128)(2,1)S(1)} collective-permute-done((bf16[368,128]{1,0:T(8,128)(2,1)S(1)}, bf16[368,128]{1,0:T(8,128)(2,1)S(1)}, u32[]{:S(2)}, u32[]{:S(2)}) %collective-permute-start.7) | collective-permute-done | bytes 94240 | tf_op jit(solution)/shard_map/ppermute | solution.py:23
  59.3 1.1 %collective-permute-start.23 = (bf16[320,640]{1,0:T(8,128)(2,1)S(1)}, bf16[320,640]{1,0:T(8,128)(2,1)S(1)}, u32[]{:S(2)}, u32[]{:S(2)}) collective-permute-start(bf16[320,640]{1,0:T(8,128)(2,1)S(1)} %collective-permute-done.20.refs_3_), channel_id=1, source_target_pairs={{0,192},{64,128},{128,64},{192,0},{1,193},{65,129},{129,65},{193,1... | collective-permute-start | bytes 1228808 | tf_op jit(solution)/shard_map/ppermute | solution.py:23
  61.0 1.8 %collective-permute-start.9 = (bf16[640,128]{1,0:T(8,128)(2,1)S(1)}, bf16[640,128]{1,0:T(8,128)(2,1)S(1)}, u32[]{:S(2)}, u32[]{:S(2)}) collective-permute-start(bf16[640,128]{1,0:T(8,128)(2,1)S(1)} %get-tuple-element.50.late), channel_id=1, source_target_pairs={{0,8},{8,0},{16,24},{24,16},{32,40},{40,32},{48,56},{56,48},{1,9},... | collective-permute-start | bytes 491528 | tf_op jit(solution)/shard_map/ppermute | solution.py:23
  62.8 4.6 %collective-permute-done.9.late_side = bf16[640,128]{1,0:T(8,128)(2,1)S(1)} collective-permute-done((bf16[640,128]{1,0:T(8,128)(2,1)S(1)}, bf16[640,128]{1,0:T(8,128)(2,1)S(1)}, u32[]{:S(2)}, u32[]{:S(2)}) %collective-permute-start.9) | collective-permute-done | bytes 163872 | tf_op jit(solution)/shard_map/ppermute | solution.py:23
  67.3 2.5 %collective-permute-done.22.refs_4_ = bf16[320,640]{1,0:T(8,128)(2,1)S(1)} collective-permute-done((bf16[320,640]{1,0:T(8,128)(2,1)S(1)}, bf16[320,640]{1,0:T(8,128)(2,1)S(1)}, u32[]{:S(2)}, u32[]{:S(2)}) %collective-permute-start.22) | collective-permute-done | bytes 409632 | tf_op jit(solution)/shard_map/ppermute | solution.py:23
  70.3 2.0 %collective-permute-done.23.refs_5_ = bf16[320,640]{1,0:T(8,128)(2,1)S(1)} collective-permute-done((bf16[320,640]{1,0:T(8,128)(2,1)S(1)}, bf16[320,640]{1,0:T(8,128)(2,1)S(1)}, u32[]{:S(2)}, u32[]{:S(2)}) %collective-permute-start.23) | collective-permute-done | bytes 409632 | tf_op jit(solution)/shard_map/ppermute | solution.py:23
  72.4 2.0 %shard_map.118 = (f32[128,640]{1,0:T(8,128)S(1)}, f32[128,640]{1,0:T(8,128)S(1)}, f32[128,128]{1,0:T(8,128)S(1)}, f32[128,128]{1,0:T(8,128)S(1)}) custom-call(s32[4]{0:T(128)S(1)} %pad_add_fusion.place.r_0_, bf16[128,128]{1,0:T(8,128)(2,1)S(1)} %copy-done, f32[128,128]{1,0:T(8,128)S(1)} %get-tuple-element.37.factors, ...), custom_call_target="tpu_custom_call" | custom-call | flops 100000000 | bytes 1048576 | tf_op jit(solution)/shard_map/pallas_call | solution.py:31
  74.4 1.5 %shard_map.119 = (f32[128,640]{1,0:T(8,128)S(1)}, bf16[128,640]{1,0:T(8,128)(2,1)S(1)}) custom-call(s32[4]{0:T(128)S(1)} %pad_add_fusion.place.r_0_, bf16[128,128]{1,0:T(8,128)(2,1)S(1)} %copy-done, bf16[384,128]{1,0:T(8,128)(2,1)S(1)} %collective-permute-done.1.mail, f32[128,128]{1,0:T(8,128)S(1)} %get-tuple-element.48.own_w, ...), custom_call_target="tpu_custom_call" | custom-call | flops 100000000 | bytes 1048576 | tf_op jit(solution)/shard_map/pallas_call | solution.py:31
  77.2 2.2 %shard_map.112.high = f32[128,640]{1,0:T(8,128)S(1)} custom-call(s32[4]{0:T(128)S(1)} %pad_add_fusion.place.r_0_, bf16[128,128]{1,0:T(8,128)(2,1)S(1)} %copy-done, bf16[128,128]{1,0:T(8,128)(2,1)S(1)} %copy-done.3, bf16[128,1280]{1,0:T(8,128)(2,1)S(1)} %get-tuple-element.32.r_3_, f32[128,128]{1,0:T(8,128)S(1)} %get-tuple-element.33.cum_ref.r_4_, ...), custom_call_target="tpu_custom_call" | custom-call | flops 100000000 | bytes 1048576 | tf_op jit(solution)/shard_map/pallas_call | solution.py:31
  79.4 2.0 %shard_map.111.low = f32[128,640]{1,0:T(8,128)S(1)} custom-call(s32[4]{0:T(128)S(1)} %pad_add_fusion.place.r_0_, bf16[128,128]{1,0:T(8,128)(2,1)S(1)} %copy-done, bf16[128,128]{1,0:T(8,128)(2,1)S(1)} %copy-done.3, bf16[128,1280]{1,0:T(8,128)(2,1)S(1)} %get-tuple-element.32.r_3_, f32[128,128]{1,0:T(8,128)S(1)} %get-tuple-element.33.cum_ref.r_4_, ...), custom_call_target="tpu_custom_call" | custom-call | flops 100000000 | bytes 1048576 | tf_op jit(solution)/shard_map/pallas_call | solution.py:31
  81.6 3.8 %shard_map.122 = (bf16[32,2688]{1,0:T(8,128)(2,1)S(1)}, bf16[32,2688]{1,0:T(8,128)(2,1)S(1)}, bf16[32,2688]{1,0:T(8,128)(2,1)S(1)}, bf16[32,2688]{1,0:T(8,128)(2,1)S(1)}) custom-call(s32[4]{0:T(128)S(1)} %pad_add_fusion.place.r_0_, f32[128,640]{1,0:T(8,128)S(1)} %shard_map.111.low, f32[128,640]{1,0:T(8,128)S(1)} %shard_map.112.high, ...), custom_call_target="tpu_custom_call" | custom-call | flops 1000000000 | bytes 1048576 | tf_op jit(solution)/shard_map/pallas_call | solution.py:31
  85.3 3.3 %collective-permute-start.33 = (bf16[32,2688]{1,0:T(8,128)(2,1)S(1)}, bf16[32,2688]{1,0:T(8,128)(2,1)S(1)}, u32[]{:S(2)}, u32[]{:S(2)}) collective-permute-start(bf16[32,2688]{1,0:T(8,128)(2,1)S(1)} %get-tuple-element.56), channel_id=1, source_target_pairs={{0,2},{1,3},{2,0},{3,1},{4,6},{5,7},{6,4},{7,5},{8,10},{9,11},{10,... | collective-permute-start | bytes 516104 | tf_op jit(solution)/shard_map/ppermute | solution.py:23
  89.6 4.5 %collective-permute-done.33.b_ref = bf16[32,2688]{1,0:T(8,128)(2,1)S(1)} collective-permute-done((bf16[32,2688]{1,0:T(8,128)(2,1)S(1)}, bf16[32,2688]{1,0:T(8,128)(2,1)S(1)}, u32[]{:S(2)}, u32[]{:S(2)}) %collective-permute-start.33) | collective-permute-done | bytes 172064 | tf_op jit(solution)/shard_map/ppermute | solution.py:23
  94.2 3.7 %collective-permute-done.34.c_ref = bf16[32,2688]{1,0:T(8,128)(2,1)S(1)} collective-permute-done((bf16[32,2688]{1,0:T(8,128)(2,1)S(1)}, bf16[32,2688]{1,0:T(8,128)(2,1)S(1)}, u32[]{:S(2)}, u32[]{:S(2)}) %collective-permute-start.34) | collective-permute-done | bytes 172064 | tf_op jit(solution)/shard_map/ppermute | solution.py:23
  97.8 1.5 %shard_map.123 = bf16[32,2560]{1,0:T(8,128)(2,1)} custom-call(s32[4]{0:T(128)S(1)} %pad_add_fusion.place.r_0_, bf16[32,2688]{1,0:T(8,128)(2,1)S(1)} %get-tuple-element.55.a_ref, bf16[32,2688]{1,0:T(8,128)(2,1)S(1)} %collective-permute-done.33.b_ref, bf16[32,2688]{1,0:T(8,128)(2,1)S(1)} %collective-permute-done.34.c_ref, ...), custom_call_target="tpu_custom_call" | custom-call | flops 100000000 | bytes 1048576 | tf_op jit(solution)/shard_map/pallas_call | solution.py:31
  (80 shorter events, 14.9 us)
Async XLA Ops:
  4.3 6.1 %collective-permute-start = (bf16[1376,128]{1,0:T(8,128)(2,1)S(1)}, bf16[1376,128]{1,0:T(8,128)(2,1)S(1)}, u32[]{:S(2)}, u32[]{:S(2)}) collective-permute-start(bf16[1376,128]{1,0:T(8,128)(2,1)S(1)} %get-tuple-element.35.own), channel_id=1, source_target_pairs={{0,4},{4,0},{1,5},{5,1},{2,6},{6,2},{3,7},{7,3},{8,12},{12,8},{9,1... | collective-permute-start | bytes 1056776 | tf_op jit(solution)/shard_map/ppermute | solution.py:23
  4.5 8.7 %collective-permute-start.14 = (bf16[80,640]{1,0:T(8,128)(2,1)S(1)}, bf16[80,640]{1,0:T(8,128)(2,1)S(1)}, u32[]{:S(2)}, u32[]{:S(2)}) collective-permute-start(bf16[80,640]{1,0:T(8,128)(2,1)S(1)} %fusion.c), channel_id=1, source_target_pairs={{0,56},{8,0},{16,8},{24,16},{32,24},{40,32},{48,40},{56,48},{1,57}... | collective-permute-start | bytes 307208 | tf_op jit(solution)/shard_map/ppermute | solution.py:27
  10.4 6.5 %collective-permute-start.12 = (bf16[80,640]{1,0:T(8,128)(2,1)S(1)}, bf16[80,640]{1,0:T(8,128)(2,1)S(1)}, u32[]{:S(2)}, u32[]{:S(2)}) collective-permute-start(bf16[80,640]{1,0:T(8,128)(2,1)S(1)} %fusion.c), channel_id=1, source_target_pairs={{0,8},{8,16},{16,24},{24,32},{32,40},{40,48},{48,56},{56,0},{1,9},... | collective-permute-start | bytes 307208 | tf_op jit(solution)/shard_map/ppermute | solution.py:27
  11.1 11.7 %collective-permute-start.2 = (bf16[688,128]{1,0:T(8,128)(2,1)S(1)}, bf16[688,128]{1,0:T(8,128)(2,1)S(1)}, u32[]{:S(2)}, u32[]{:S(2)}) collective-permute-start(bf16[688,128]{1,0:T(8,128)(2,1)S(1)} %get-tuple-element.39.own), channel_id=1, source_target_pairs={{0,8},{8,0},{16,24},{24,16},{32,40},{40,32},{48,56},{56,48},{1,9},... | collective-permute-start | bytes 528392 | tf_op jit(solution)/shard_map/ppermute | solution.py:23
  13.2 6.7 %collective-permute-start.15 = (bf16[80,640]{1,0:T(8,128)(2,1)S(1)}, bf16[80,640]{1,0:T(8,128)(2,1)S(1)}, u32[]{:S(2)}, u32[]{:S(2)}) collective-permute-start(bf16[80,640]{1,0:T(8,128)(2,1)S(1)} %collective-permute-done.14.d), channel_id=1, source_target_pairs={{0,56},{8,0},{16,8},{24,16},{32,24},{40,32},{48,40},{56,48},{1,57}... | collective-permute-start | bytes 307208 | tf_op jit(solution)/shard_map/ppermute | solution.py:27
  16.9 6.6 %collective-permute-start.13 = (bf16[80,640]{1,0:T(8,128)(2,1)S(1)}, bf16[80,640]{1,0:T(8,128)(2,1)S(1)}, u32[]{:S(2)}, u32[]{:S(2)}) collective-permute-start(bf16[80,640]{1,0:T(8,128)(2,1)S(1)} %collective-permute-done.12.b), channel_id=1, source_target_pairs={{0,8},{8,16},{16,24},{24,32},{32,40},{40,48},{48,56},{56,0},{1,9},... | collective-permute-start | bytes 307208 | tf_op jit(solution)/shard_map/ppermute | solution.py:27
  23.4 5.6 %collective-permute-start.3 = (bf16[368,128]{1,0:T(8,128)(2,1)S(1)}, bf16[368,128]{1,0:T(8,128)(2,1)S(1)}, u32[]{:S(2)}, u32[]{:S(2)}) collective-permute-start(bf16[368,128]{1,0:T(8,128)(2,1)S(1)} %get-tuple-element.41.r_1_), channel_id=1, source_target_pairs={{0,16},{8,24},{16,0},{24,8},{32,48},{40,56},{48,32},{56,40},{1,17}... | collective-permute-start | bytes 282632 | tf_op jit(solution)/shard_map/ppermute | solution.py:23
  23.5 17.1 %collective-permute-start.21 = (bf16[320,640]{1,0:T(8,128)(2,1)S(1)}, bf16[320,640]{1,0:T(8,128)(2,1)S(1)}, u32[]{:S(2)}, u32[]{:S(2)}) collective-permute-start(bf16[320,640]{1,0:T(8,128)(2,1)S(1)} %shard_map.120.refs_0_), channel_id=1, source_target_pairs={{0,192},{64,128},{128,64},{192,0},{1,193},{65,129},{129,65},{193,1... | collective-permute-start | bytes 1228808 | tf_op jit(solution)/shard_map/ppermute | solution.py:23
  24.1 19.0 %collective-permute-start.19 = (bf16[320,640]{1,0:T(8,128)(2,1)S(1)}, bf16[320,640]{1,0:T(8,128)(2,1)S(1)}, u32[]{:S(2)}, u32[]{:S(2)}) collective-permute-start(bf16[320,640]{1,0:T(8,128)(2,1)S(1)} %shard_map.120.refs_0_), channel_id=1, source_target_pairs={{0,64},{64,0},{128,192},{192,128},{1,65},{65,1},{129,193},{193,129... | collective-permute-start | bytes 1228808 | tf_op jit(solution)/shard_map/ppermute | solution.py:23
  25.0 19.2 %collective-permute-start.25 = (bf16[320,640]{1,0:T(8,128)(2,1)S(1)}, bf16[320,640]{1,0:T(8,128)(2,1)S(1)}, u32[]{:S(2)}, u32[]{:S(2)}) collective-permute-start(bf16[320,640]{1,0:T(8,128)(2,1)S(1)} %shard_map.120.refs_0_), channel_id=1, source_target_pairs={{0,4},{4,0},{1,5},{5,1},{2,6},{6,2},{3,7},{7,3},{8,12},{12,8},{9,1... | collective-permute-start | bytes 1228808 | tf_op jit(solution)/shard_map/ppermute | solution.py:23
  25.0 6.5 %collective-permute-start.18 = (bf16[80,640]{1,0:T(8,128)(2,1)S(1)}, bf16[80,640]{1,0:T(8,128)(2,1)S(1)}, u32[]{:S(2)}, u32[]{:S(2)}) collective-permute-start(bf16[80,640]{1,0:T(8,128)(2,1)S(1)} %collective-permute-done.13.a), channel_id=1, source_target_pairs={{0,8},{8,16},{16,24},{24,32},{32,40},{40,48},{48,56},{56,0},{1,9},... | collective-permute-start | bytes 307208 | tf_op jit(solution)/shard_map/ppermute | solution.py:27
  31.5 6.7 %collective-permute-start.4 = (bf16[368,128]{1,0:T(8,128)(2,1)S(1)}, bf16[368,128]{1,0:T(8,128)(2,1)S(1)}, u32[]{:S(2)}, u32[]{:S(2)}) collective-permute-start(bf16[368,128]{1,0:T(8,128)(2,1)S(1)} %get-tuple-element.43.r_1_), channel_id=1, source_target_pairs={{0,48},{8,56},{16,32},{24,40},{32,16},{40,24},{48,0},{56,8},{1,49}... | collective-permute-start | bytes 282632 | tf_op jit(solution)/shard_map/ppermute | solution.py:23
  34.1 25.2 %collective-permute-start.20 = (bf16[320,640]{1,0:T(8,128)(2,1)S(1)}, bf16[320,640]{1,0:T(8,128)(2,1)S(1)}, u32[]{:S(2)}, u32[]{:S(2)}) collective-permute-start(bf16[320,640]{1,0:T(8,128)(2,1)S(1)} %shard_map.121.refs_1_), channel_id=1, source_target_pairs={{0,64},{64,0},{128,192},{192,128},{1,65},{65,1},{129,193},{193,129... | collective-permute-start | bytes 1228808 | tf_op jit(solution)/shard_map/ppermute | solution.py:23
  39.5 5.8 %collective-permute-start.5 = (bf16[368,128]{1,0:T(8,128)(2,1)S(1)}, bf16[368,128]{1,0:T(8,128)(2,1)S(1)}, u32[]{:S(2)}, u32[]{:S(2)}) collective-permute-start(bf16[368,128]{1,0:T(8,128)(2,1)S(1)} %get-tuple-element.45), channel_id=1, source_target_pairs={{0,64},{64,0},{128,192},{192,128},{1,65},{65,1},{129,193},{193,129... | collective-permute-start | bytes 282632 | tf_op jit(solution)/shard_map/ppermute | solution.py:23
  40.6 8.4 %collective-permute-start.6 = (bf16[368,128]{1,0:T(8,128)(2,1)S(1)}, bf16[368,128]{1,0:T(8,128)(2,1)S(1)}, u32[]{:S(2)}, u32[]{:S(2)}) collective-permute-start(bf16[368,128]{1,0:T(8,128)(2,1)S(1)} %get-tuple-element.45), channel_id=1, source_target_pairs={{0,128},{64,192},{128,0},{192,64},{1,129},{65,193},{129,1},{193,65... | collective-permute-start | bytes 282632 | tf_op jit(solution)/shard_map/ppermute | solution.py:23
  43.1 17.9 %collective-permute-start.24 = (bf16[320,640]{1,0:T(8,128)(2,1)S(1)}, bf16[320,640]{1,0:T(8,128)(2,1)S(1)}, u32[]{:S(2)}, u32[]{:S(2)}) collective-permute-start(bf16[320,640]{1,0:T(8,128)(2,1)S(1)} %shard_map.121.refs_1_), channel_id=1, source_target_pairs={{0,192},{64,128},{128,64},{192,0},{1,193},{65,129},{129,65},{193,1... | collective-permute-start | bytes 1228808 | tf_op jit(solution)/shard_map/ppermute | solution.py:23
  44.2 18.6 %collective-permute-start.26 = (bf16[320,640]{1,0:T(8,128)(2,1)S(1)}, bf16[320,640]{1,0:T(8,128)(2,1)S(1)}, u32[]{:S(2)}, u32[]{:S(2)}) collective-permute-start(bf16[320,640]{1,0:T(8,128)(2,1)S(1)} %shard_map.121.refs_1_), channel_id=1, source_target_pairs={{0,4},{4,0},{1,5},{5,1},{2,6},{6,2},{3,7},{7,3},{8,12},{12,8},{9,1... | collective-permute-start | bytes 1228808 | tf_op jit(solution)/shard_map/ppermute | solution.py:23
  45.3 14.0 %collective-permute-start.8 = (bf16[640,128]{1,0:T(8,128)(2,1)S(1)}, bf16[640,128]{1,0:T(8,128)(2,1)S(1)}, u32[]{:S(2)}, u32[]{:S(2)}) collective-permute-start(bf16[640,128]{1,0:T(8,128)(2,1)S(1)} %get-tuple-element.47), channel_id=1, source_target_pairs={{0,8},{8,0},{16,24},{24,16},{32,40},{40,32},{48,56},{56,48},{1,9},... | collective-permute-start | bytes 491528 | tf_op jit(solution)/shard_map/ppermute | solution.py:23
  49.0 9.9 %collective-permute-start.7 = (bf16[368,128]{1,0:T(8,128)(2,1)S(1)}, bf16[368,128]{1,0:T(8,128)(2,1)S(1)}, u32[]{:S(2)}, u32[]{:S(2)}) collective-permute-start(bf16[368,128]{1,0:T(8,128)(2,1)S(1)} %get-tuple-element.45), channel_id=1, source_target_pairs={{0,192},{64,128},{128,64},{192,0},{1,193},{65,129},{129,65},{193,1... | collective-permute-start | bytes 282632 | tf_op jit(solution)/shard_map/ppermute | solution.py:23
  59.0 10.8 %collective-permute-start.22 = (bf16[320,640]{1,0:T(8,128)(2,1)S(1)}, bf16[320,640]{1,0:T(8,128)(2,1)S(1)}, u32[]{:S(2)}, u32[]{:S(2)}) collective-permute-start(bf16[320,640]{1,0:T(8,128)(2,1)S(1)} %collective-permute-done.21.refs_6_), channel_id=1, source_target_pairs={{0,64},{64,0},{128,192},{192,128},{1,65},{65,1},{129,193},{193,129... | collective-permute-start | bytes 1228808 | tf_op jit(solution)/shard_map/ppermute | solution.py:23
  59.3 10.6 %collective-permute-start.31 = (bf16[320,640]{1,0:T(8,128)(2,1)S(1)}, bf16[320,640]{1,0:T(8,128)(2,1)S(1)}, u32[]{:S(2)}, u32[]{:S(2)}) collective-permute-start(bf16[320,640]{1,0:T(8,128)(2,1)S(1)} %collective-permute-done.21.refs_6_), channel_id=1, source_target_pairs={{0,4},{4,0},{1,5},{5,1},{2,6},{6,2},{3,7},{7,3},{8,12},{12,8},{9,1... | collective-permute-start | bytes 1228808 | tf_op jit(solution)/shard_map/ppermute | solution.py:23
  59.3 13.1 %collective-permute-start.23 = (bf16[320,640]{1,0:T(8,128)(2,1)S(1)}, bf16[320,640]{1,0:T(8,128)(2,1)S(1)}, u32[]{:S(2)}, u32[]{:S(2)}) collective-permute-start(bf16[320,640]{1,0:T(8,128)(2,1)S(1)} %collective-permute-done.20.refs_3_), channel_id=1, source_target_pairs={{0,192},{64,128},{128,64},{192,0},{1,193},{65,129},{129,65},{193,1... | collective-permute-start | bytes 1228808 | tf_op jit(solution)/shard_map/ppermute | solution.py:23
  61.0 6.3 %collective-permute-start.9 = (bf16[640,128]{1,0:T(8,128)(2,1)S(1)}, bf16[640,128]{1,0:T(8,128)(2,1)S(1)}, u32[]{:S(2)}, u32[]{:S(2)}) collective-permute-start(bf16[640,128]{1,0:T(8,128)(2,1)S(1)} %get-tuple-element.50.late), channel_id=1, source_target_pairs={{0,8},{8,0},{16,24},{24,16},{32,40},{40,32},{48,56},{56,48},{1,9},... | collective-permute-start | bytes 491528 | tf_op jit(solution)/shard_map/ppermute | solution.py:23
  62.8 13.1 %collective-permute-start.27 = (bf16[320,640]{1,0:T(8,128)(2,1)S(1)}, bf16[320,640]{1,0:T(8,128)(2,1)S(1)}, u32[]{:S(2)}, u32[]{:S(2)}) collective-permute-start(bf16[320,640]{1,0:T(8,128)(2,1)S(1)} %collective-permute-done.19.refs_2_), channel_id=1, source_target_pairs={{0,4},{4,0},{1,5},{5,1},{2,6},{6,2},{3,7},{7,3},{8,12},{12,8},{9,1... | collective-permute-start | bytes 1228808 | tf_op jit(solution)/shard_map/ppermute | solution.py:23
  67.3 14.2 %collective-permute-start.28 = (bf16[320,640]{1,0:T(8,128)(2,1)S(1)}, bf16[320,640]{1,0:T(8,128)(2,1)S(1)}, u32[]{:S(2)}, u32[]{:S(2)}) collective-permute-start(bf16[320,640]{1,0:T(8,128)(2,1)S(1)} %collective-permute-done.20.refs_3_), channel_id=1, source_target_pairs={{0,4},{4,0},{1,5},{5,1},{2,6},{6,2},{3,7},{7,3},{8,12},{12,8},{9,1... | collective-permute-start | bytes 1228808 | tf_op jit(solution)/shard_map/ppermute | solution.py:23
  69.8 11.7 %collective-permute-start.32 = (bf16[320,640]{1,0:T(8,128)(2,1)S(1)}, bf16[320,640]{1,0:T(8,128)(2,1)S(1)}, u32[]{:S(2)}, u32[]{:S(2)}) collective-permute-start(bf16[320,640]{1,0:T(8,128)(2,1)S(1)} %collective-permute-done.24.refs_7_), channel_id=1, source_target_pairs={{0,4},{4,0},{1,5},{5,1},{2,6},{6,2},{3,7},{7,3},{8,12},{12,8},{9,1... | collective-permute-start | bytes 1228808 | tf_op jit(solution)/shard_map/ppermute | solution.py:23
  69.8 11.7 %collective-permute-start.29 = (bf16[320,640]{1,0:T(8,128)(2,1)S(1)}, bf16[320,640]{1,0:T(8,128)(2,1)S(1)}, u32[]{:S(2)}, u32[]{:S(2)}) collective-permute-start(bf16[320,640]{1,0:T(8,128)(2,1)S(1)} %collective-permute-done.22.refs_4_), channel_id=1, source_target_pairs={{0,4},{4,0},{1,5},{5,1},{2,6},{6,2},{3,7},{7,3},{8,12},{12,8},{9,1... | collective-permute-start | bytes 1228808 | tf_op jit(solution)/shard_map/ppermute | solution.py:23
  72.4 9.2 %collective-permute-start.30 = (bf16[320,640]{1,0:T(8,128)(2,1)S(1)}, bf16[320,640]{1,0:T(8,128)(2,1)S(1)}, u32[]{:S(2)}, u32[]{:S(2)}) collective-permute-start(bf16[320,640]{1,0:T(8,128)(2,1)S(1)} %collective-permute-done.23.refs_5_), channel_id=1, source_target_pairs={{0,4},{4,0},{1,5},{5,1},{2,6},{6,2},{3,7},{7,3},{8,12},{12,8},{9,1... | collective-permute-start | bytes 1228808 | tf_op jit(solution)/shard_map/ppermute | solution.py:23
  75.9 5.6 %collective-permute-start.10 = (bf16[128,640]{1,0:T(8,128)(2,1)S(1)}, bf16[128,640]{1,0:T(8,128)(2,1)S(1)}, u32[]{:S(2)}, u32[]{:S(2)}) collective-permute-start(bf16[128,640]{1,0:T(8,128)(2,1)S(1)} %get-tuple-element.54), channel_id=1, source_target_pairs={{0,4},{4,0},{1,5},{5,1},{2,6},{6,2},{3,7},{7,3},{8,12},{12,8},{9,1... | collective-permute-start | bytes 491528 | tf_op jit(solution)/shard_map/ppermute | solution.py:23
  85.3 8.8 %collective-permute-start.33 = (bf16[32,2688]{1,0:T(8,128)(2,1)S(1)}, bf16[32,2688]{1,0:T(8,128)(2,1)S(1)}, u32[]{:S(2)}, u32[]{:S(2)}) collective-permute-start(bf16[32,2688]{1,0:T(8,128)(2,1)S(1)} %get-tuple-element.56), channel_id=1, source_target_pairs={{0,2},{1,3},{2,0},{3,1},{4,6},{5,7},{6,4},{7,5},{8,10},{9,11},{10,... | collective-permute-start | bytes 516104 | tf_op jit(solution)/shard_map/ppermute | solution.py:23
  88.6 9.2 %collective-permute-start.34 = (bf16[32,2688]{1,0:T(8,128)(2,1)S(1)}, bf16[32,2688]{1,0:T(8,128)(2,1)S(1)}, u32[]{:S(2)}, u32[]{:S(2)}) collective-permute-start(bf16[32,2688]{1,0:T(8,128)(2,1)S(1)} %get-tuple-element.57), channel_id=1, source_target_pairs={{0,1},{1,0},{2,3},{3,2},{4,5},{5,4},{6,7},{7,6},{8,9},{9,8},{10,11... | collective-permute-start | bytes 516104 | tf_op jit(solution)/shard_map/ppermute | solution.py:23
  89.3 8.6 %collective-permute-start.35 = (bf16[32,2688]{1,0:T(8,128)(2,1)S(1)}, bf16[32,2688]{1,0:T(8,128)(2,1)S(1)}, u32[]{:S(2)}, u32[]{:S(2)}) collective-permute-start(bf16[32,2688]{1,0:T(8,128)(2,1)S(1)} %get-tuple-element.58), channel_id=1, source_target_pairs={{0,3},{1,2},{2,1},{3,0},{4,7},{5,6},{6,5},{7,4},{8,11},{9,10},{10,... | collective-permute-start | bytes 516104 | tf_op jit(solution)/shard_map/ppermute | solution.py:23
  (15 other events, 33.1 us)
